TPU v7x, 32 devices: a whole 2x2x4 slice. The times are simulated.
32 devices in a mesh: dp: 4 (over y, core), tensor: 8 (over z, x).
Axes of the slice: x: 2, y: 2, z: 4, core: 2. Of those that a mesh axis runs over, the one named last changes fastest.
Arguments:
- tokens: bfloat16 [8192, 1024], P('dp'), may hold values from -6 to 6
- cotangent: bfloat16 [8192, 1024], P('dp'), may hold values from -6 to 6
- gain_attn: float32 [1024], replicated, may hold values from 0.1 to 1.9
- gain_moe: float32 [1024], replicated, may hold values from 0.1 to 1.9
- w_qkv: bfloat16 [1024, 3, 1024], P(None, None, 'tensor'), may hold values from -0.1875 to 0.1875
- w_out: bfloat16 [1024, 1024], P('tensor'), may hold values from -0.75 to 0.75
- rel_bias: bfloat16 [32, 16], P(None, 'tensor'), may hold values from -6 to 6
- w_router: bfloat16 [1024, 8], replicated, may hold values from -0.375 to 0.375
- w_in: bfloat16 [8, 2, 1024, 2816], P(None, None, None, 'tensor'), may hold values from -0.1875 to 0.1875
- w_down: bfloat16 [8, 2816, 1024], P(None, 'tensor'), may hold values from -0.109375 to 0.109375
- segment_ids: int32 [8, 1024], P('dp'), may hold values from 0 to 15, never falling along the last dimension, each value on 1 to 512 neighbouring positions
- routes: int32 [8192, 2], P('dp'), may hold values from 0 to 7, all different within a row
- order: int32 [4, 2048], P('dp'), may hold values from 0 to 2047, each once within a row
Outputs:
- result: float32 [8192, 1024], P('dp')
- input_grad: float32 [8192, 1024], P('dp')
- gain_attn_grad: float32 [1024], P('dp')
- gain_moe_grad: float32 [1024], P('dp')
- w_qkv_grad: float32 [1024, 3, 1024], P('dp', None, 'tensor')
- w_out_grad: float32 [1024, 1024], P('tensor', 'dp')
- rel_bias_grad: float32 [32, 16], P('dp', 'tensor')
- w_router_grad: float32 [1024, 8], P('dp')
- w_in_grad: float32 [8, 2, 1024, 2816], P(None, None, 'dp', 'tensor')
- w_down_grad: float32 [8, 2816, 1024], P(None, 'tensor', 'dp')
Inputs may be any that keep to these rules, and one draw needn't show every extreme that they name: `segment_ids`: within a sequence the ids never fall; each document has at most 512 tokens. `routes`: the two experts of a token differ. `order`: each row holds every token index of its group once.
All inputs are finite; a program needn't handle non-finite values.
Results may differ from a plain program's by a relative error of at most 0.015.
The roundings to bfloat16 on the way count: a program that leaves them out, or rounds other values in their place, can miss the bound.
Values sent between devices are 32-bit elements; how exact they have to be, the bound alone decides.
A program may use at most 320 MiB of HBM per device.

v0:
```python
import math

import jax
import jax.numpy as jnp
import numpy as np
from jax import lax
from jax.sharding import PartitionSpec as P

D = 1024
HD = 64
NB = 32
MAXDIST = 128
EXPERTS = 8
LEN = 1024
CAP = 576


EPSILON = 1e-06
PRECISE = lax.Precision.HIGHEST


def thresholds(bucket_count, reach):
    half_count = bucket_count // 2
    exact_count = half_count // 2
    listing = []
    for bucket_level in range(1, half_count):
        if bucket_level <= exact_count:
            listing.append(bucket_level)
        else:
            distance = exact_count
            while (
                exact_count
                + int(
                    np.floor(
                        np.log(distance / exact_count)
                        / np.log(reach / exact_count)
                        * (half_count - exact_count)
                    )
                )
                < bucket_level
            ):
                distance += 1
            listing.append(distance)
    return listing


def bucket_of(query_pos, key_pos):
    relative = key_pos[None, :] - query_pos[:, None]
    magnitude = jnp.abs(relative)
    bucket_ids = jnp.where(relative > 0, NB // 2, 0).astype(jnp.int32)
    for boundary in thresholds(NB, MAXDIST):
        bucket_ids = bucket_ids + (magnitude >= boundary).astype(jnp.int32)
    return bucket_ids.astype(jnp.int32)


def slot_tables(routes, order):
    tok_dev = routes.shape[0]
    ordered = jnp.take(routes, order, axis=0)
    pair_expert = jnp.concatenate([ordered[:, 0], ordered[:, 1]])
    pair_token = jnp.concatenate([order, order])
    pair_choice = jnp.concatenate(
        [jnp.zeros((tok_dev,), jnp.int32), jnp.ones((tok_dev,), jnp.int32)]
    )
    onehot = (pair_expert[:, None] == jnp.arange(EXPERTS, dtype=jnp.int32)[None, :]).astype(
        jnp.int32
    )
    before = jnp.cumsum(onehot, axis=0) - onehot
    position = jnp.sum(before * onehot, axis=1)
    target = jnp.where(position < CAP, pair_expert * CAP + position, EXPERTS * CAP)
    slot_token = (
        jnp.full((EXPERTS * CAP + 1,), -1, jnp.int32).at[target].set(pair_token)[: EXPERTS * CAP]
    )
    slot_choice = (
        jnp.zeros((EXPERTS * CAP + 1,), jnp.int32).at[target].set(pair_choice)[: EXPERTS * CAP]
    )
    token_target = jnp.zeros((tok_dev, 2), jnp.int32).at[pair_token, pair_choice].set(target)
    return (slot_token, slot_choice, token_target)


def rms_norm(values, gain):
    return values * lax.rsqrt(jnp.mean(values * values, axis=-1, keepdims=True) + EPSILON) * gain


def geglu(gate, upper):
    return jax.nn.gelu(gate, approximate=True) * upper


def shards(
    tokens,
    cotangent,
    gain_attn,
    gain_moe,
    w_qkv,
    w_out,
    rel_bias,
    w_router,
    w_in,
    w_down,
    segment_ids,
    routes,
    order,
):
    tok_dev = tokens.shape[0]
    seq_count = segment_ids.shape[0]
    heads_local = w_qkv.shape[2] // HD
    block_rows = min(512, LEN)
    score_scale = 1.0 / math.sqrt(HD)
    positions = jnp.arange(LEN, dtype=jnp.int32)
    bucket_range = jnp.arange(NB, dtype=jnp.int32)
    inputs = tokens.astype(jnp.float32)
    attn_input = rms_norm(inputs, gain_attn).astype(jnp.bfloat16)
    projected = jnp.einsum(
        "td,dgn->tgn", attn_input, w_qkv, preferred_element_type=jnp.float32
    ).astype(jnp.bfloat16)
    qkv_seq = projected.reshape(seq_count, LEN, 3, heads_local, HD)

    def block_scores(query_rows, key_vecs, query_seg, key_seg, offset):
        query_pos = offset + jnp.arange(block_rows, dtype=jnp.int32)
        onehot = (
            bucket_of(query_pos, positions)[:, :, None] == bucket_range[None, None, :]
        ).astype(jnp.bfloat16)
        scores = (
            jnp.einsum("qhd,khd->hqk", query_rows, key_vecs, preferred_element_type=jnp.float32)
            * score_scale
        )
        scores = scores + jnp.einsum(
            "qkb,bh->hqk", onehot, rel_bias, preferred_element_type=jnp.float32
        )
        scores = jnp.where((query_seg[:, None] == key_seg[None, :])[None], scores, -1000000000.0)
        return (scores, onehot)

    def attend(packed):
        qkv_one, seg_one = packed
        queries, key_vecs, value_vecs = (qkv_one[:, 0], qkv_one[:, 1], qkv_one[:, 2])
        pieces = []
        log_parts = []
        for offset in range(0, LEN, block_rows):
            scores, onehot = block_scores(
                queries[offset : offset + block_rows],
                key_vecs,
                seg_one[offset : offset + block_rows],
                seg_one,
                offset,
            )
            row_max = jnp.max(scores, axis=-1, keepdims=True)
            exponent = jnp.exp(scores - row_max)
            row_sum = jnp.sum(exponent, axis=-1, keepdims=True)
            attn_probs = (exponent / row_sum).astype(jnp.bfloat16)
            pieces.append(
                jnp.einsum(
                    "hqk,khd->qhd", attn_probs, value_vecs, preferred_element_type=jnp.float32
                ).astype(jnp.bfloat16)
            )
            log_parts.append((row_max + jnp.log(row_sum))[:, :, 0])
        return (jnp.concatenate(pieces, axis=0), jnp.concatenate(log_parts, axis=1))

    attended_seq, log_totals = lax.map(attend, (qkv_seq, segment_ids))
    attended = attended_seq.reshape(tok_dev, heads_local * HD)
    attn_part = jnp.dot(attended, w_out, preferred_element_type=jnp.float32)
    attn_out = lax.psum(attn_part, "tensor")
    hidden_one = inputs + attn_out
    moe_input = rms_norm(hidden_one, gain_moe).astype(jnp.bfloat16)
    logits = jnp.dot(moe_input, w_router, preferred_element_type=jnp.float32)
    picked = (routes[:, :, None] == jnp.arange(EXPERTS, dtype=jnp.int32)[None, None, :]).astype(
        jnp.float32
    )

    def route_share(logit_rows):
        soft = jax.nn.softmax(logit_rows, axis=-1)
        chosen = jnp.sum(soft[:, None, :] * picked, axis=-1)
        return chosen / jnp.sum(chosen, axis=-1, keepdims=True)

    pair_share, share_back = jax.vjp(route_share, logits)
    slot_token, slot_choice, token_target = slot_tables(routes, order[0])
    filled = slot_token >= 0
    source_row = jnp.maximum(slot_token, 0)
    dispatched = jnp.where(
        filled[:, None], moe_input[source_row], jnp.zeros((), jnp.bfloat16)
    ).reshape(EXPERTS, CAP, D)
    gate_up = jnp.einsum("ecd,egdf->ecgf", dispatched, w_in, preferred_element_type=jnp.float32)
    gate_part = gate_up[:, :, 0]
    upper_part = gate_up[:, :, 1]
    activated = geglu(gate_part, upper_part).astype(jnp.bfloat16)
    expert_out = jnp.einsum(
        "ecf,efd->ecd", activated, w_down, preferred_element_type=jnp.float32
    ).reshape(EXPERTS * CAP, D)
    out_rows = jnp.concatenate([expert_out, jnp.zeros((1, D), jnp.float32)], axis=0)
    pair_rows = out_rows[token_target]
    moe_part = jnp.sum(pair_share[:, :, None] * pair_rows, axis=1)
    moe_out = lax.psum(moe_part, "tensor")
    result = hidden_one + moe_out
    upstream = cotangent.astype(jnp.float32)
    share_part = jnp.sum(pair_rows * upstream[:, None, :], axis=-1)
    share_grad = lax.psum(share_part, "tensor")
    logits_grad = share_back(share_grad)[0]
    router_grad = jnp.dot(moe_input.astype(jnp.float32).T, logits_grad, precision=PRECISE)
    router_input_grad = jnp.dot(logits_grad, w_router.astype(jnp.float32).T, precision=PRECISE)
    slot_share = jnp.where(slot_choice == 0, pair_share[source_row, 0], pair_share[source_row, 1])
    out_grad = (
        jnp.where(filled[:, None], slot_share[:, None] * upstream[source_row], 0.0)
        .astype(jnp.bfloat16)
        .reshape(EXPERTS, CAP, D)
    )
    act_grad = jnp.einsum("ecd,efd->ecf", out_grad, w_down, preferred_element_type=jnp.float32)
    unused_value, geglu_back = jax.vjp(geglu, gate_part, upper_part)
    gate_grad, upper_grad = geglu_back(act_grad)
    gate_up_grad = jnp.stack([gate_grad, upper_grad], axis=2).astype(jnp.bfloat16)
    w_in_local = jnp.einsum(
        "ecd,ecgf->egdf", dispatched, gate_up_grad, preferred_element_type=jnp.float32
    )
    w_down_local = jnp.einsum(
        "ecf,ecd->efd", activated, out_grad, preferred_element_type=jnp.float32
    )
    w_in_grad, w_down_grad = (
        lax.psum_scatter(w_in_local, "dp", scatter_dimension=2, tiled=True),
        lax.psum_scatter(w_down_local, "dp", scatter_dimension=2, tiled=True),
    )
    dispatched_grad = jnp.einsum(
        "ecgf,egdf->ecd", gate_up_grad, w_in, preferred_element_type=jnp.float32
    ).reshape(EXPERTS * CAP, D)
    grad_rows = jnp.concatenate([dispatched_grad, jnp.zeros((1, D), jnp.float32)], axis=0)
    moe_in_part = jnp.sum(grad_rows[token_target], axis=1)
    moe_in_sum = lax.psum(moe_in_part, "tensor")
    moe_input_grad = moe_in_sum + router_input_grad
    unused_norm, norm_two_back = jax.vjp(rms_norm, hidden_one, gain_moe)
    hidden_norm_grad, gain_moe_local = norm_two_back(moe_input_grad)
    hidden_grad = upstream + hidden_norm_grad
    proj_grad = hidden_grad.astype(jnp.bfloat16)
    w_out_local = jnp.einsum("tn,td->nd", attended, proj_grad, preferred_element_type=jnp.float32)
    attended_grad = jnp.einsum(
        "td,nd->tn", proj_grad, w_out, preferred_element_type=jnp.float32
    ).astype(jnp.bfloat16)
    attended_grad = attended_grad.reshape(seq_count, LEN, heads_local, HD)

    def attend_back(packed):
        qkv_one, seg_one, grad_one, total_one = packed
        queries, key_vecs, value_vecs = (qkv_one[:, 0], qkv_one[:, 1], qkv_one[:, 2])
        key_grad = jnp.zeros((LEN, heads_local, HD), jnp.float32)
        value_grad = jnp.zeros((LEN, heads_local, HD), jnp.float32)
        bias_grad = jnp.zeros((NB, heads_local), jnp.float32)
        query_grads = []
        for offset in range(0, LEN, block_rows):
            query_rows = queries[offset : offset + block_rows]
            scores, onehot = block_scores(
                query_rows, key_vecs, seg_one[offset : offset + block_rows], seg_one, offset
            )
            attn_probs = jnp.exp(scores - total_one[:, offset : offset + block_rows, None])
            grad_block = grad_one[offset : offset + block_rows]
            prob_grad = jnp.einsum(
                "qhd,khd->hqk", grad_block, value_vecs, preferred_element_type=jnp.float32
            )
            score_grad = (
                attn_probs * (prob_grad - jnp.sum(attn_probs * prob_grad, axis=-1, keepdims=True))
            ).astype(jnp.bfloat16)
            query_grads.append(
                jnp.einsum("hqk,khd->qhd", score_grad, key_vecs, preferred_element_type=jnp.float32)
                * score_scale
            )
            key_grad = (
                key_grad
                + jnp.einsum(
                    "hqk,qhd->khd", score_grad, query_rows, preferred_element_type=jnp.float32
                )
                * score_scale
            )
            value_grad = value_grad + jnp.einsum(
                "hqk,qhd->khd",
                attn_probs.astype(jnp.bfloat16),
                grad_block,
                preferred_element_type=jnp.float32,
            )
            bias_grad = bias_grad + jnp.einsum(
                "hqk,qkb->bh", score_grad, onehot, preferred_element_type=jnp.float32
            )
        query_grad = jnp.concatenate(query_grads, axis=0)
        return (
            jnp.stack([query_grad, key_grad, value_grad], axis=1).astype(jnp.bfloat16),
            bias_grad,
        )

    qkv_grad_seq, bias_grads = lax.map(
        attend_back, (qkv_seq, segment_ids, attended_grad, log_totals)
    )
    bias_local = jnp.sum(bias_grads, axis=0)
    qkv_grad = qkv_grad_seq.reshape(tok_dev, 3, heads_local * HD)
    w_qkv_local = jnp.einsum(
        "td,tgn->dgn", attn_input, qkv_grad, preferred_element_type=jnp.float32
    )
    attn_in_part = jnp.einsum("tgn,dgn->td", qkv_grad, w_qkv, preferred_element_type=jnp.float32)
    attn_in_sum = lax.psum(attn_in_part, "tensor")
    unused_first, norm_one_back = jax.vjp(rms_norm, inputs, gain_attn)
    input_norm_grad, gain_attn_local = norm_one_back(attn_in_sum)
    input_grad = hidden_grad + input_norm_grad
    w_qkv_grad, w_out_grad, rel_bias_grad, w_router_grad, gain_attn_grad, gain_moe_grad = (
        lax.psum_scatter(w_qkv_local, "dp", scatter_dimension=0, tiled=True),
        lax.psum_scatter(w_out_local, "dp", scatter_dimension=1, tiled=True),
        lax.psum_scatter(bias_local, "dp", scatter_dimension=0, tiled=True),
        lax.psum_scatter(router_grad, "dp", scatter_dimension=0, tiled=True),
        lax.psum_scatter(gain_attn_local, "dp", scatter_dimension=0, tiled=True),
        lax.psum_scatter(gain_moe_local, "dp", scatter_dimension=0, tiled=True),
    )
    return (
        result,
        input_grad,
        gain_attn_grad,
        gain_moe_grad,
        w_qkv_grad,
        w_out_grad,
        rel_bias_grad,
        w_router_grad,
        w_in_grad,
        w_down_grad,
    )


def solution(mesh):
    return jax.shard_map(
        shards,
        mesh=mesh,
        in_specs=(
            P("dp", None),
            P("dp", None),
            P(),
            P(),
            P(None, None, "tensor"),
            P("tensor", None),
            P(None, "tensor"),
            P(),
            P(None, None, None, "tensor"),
            P(None, "tensor", None),
            P("dp", None),
            P("dp", None),
            P("dp", None),
        ),
        out_specs=(
            P("dp", None),
            P("dp", None),
            P("dp"),
            P("dp"),
            P("dp", None, "tensor"),
            P("tensor", "dp"),
            P("dp", "tensor"),
            P("dp", None),
            P(None, None, "dp", "tensor"),
            P(None, "tensor", "dp"),
        ),
        check_vma=False,
    )
```

profile of v0, /device:TPU:0, one launch (start us, length us, event | category | flops | bytes accessed | tf_op | source)
XLA Modules:
  0.0 2007.7 jit_solution(15822492877952848147)
XLA Ops:
  23.3 73.0 %while.28 = (s32[]{:T(128)}, bf16[2,1024,2,64]{1,3,2,0:T(8,128)(2,1)S(1)}, f32[2,2,1024]{2,1,0:T(2,128)}, bf16[2,1024,3,2,64]{1,4,3,2,0:T(8,128)(2,1)S(1)}, s32[...) while((s32[]{:T(128)}, ...), condition=%wide.region_6.7_spmd.clone.clone, body=%wide.region_1.6_spmd.clone.clone.sunk | while | flops 776602112 | bytes 56209800 | solution.py:157
  114.4 15.5 scatter_custom_fusion.2
  130.0 15.7 scatter_custom_fusion.1
  145.8 15.5 scatter_custom_fusion
  168.9 24.1 %gather_fusion.5 = f32[4608,1024]{1,0:T(8,128)} fusion(f32[2048,1024]{1,0:T(8,128)} %convert_element_type.568, s32[5120]{0:T(1024)S(1)} %pad_clamp_fusion), kind=kCustom, calls=%fused_computation.5 | custom fusion | bytes 37767168 | tf_op jit(solution)/shard_map/gather | solution.py:200
  193.0 182.4 %all-reduce.13.cloned.1.call-done = f32[2048,1024]{1,0:T(8,128)} async-done(((f32[2048,1024]{1,0:T(8,128)}), f32[2048,1024]{1,0:T(8,128)}) %all-reduce.13.cloned.1.call-update) | async-done | bytes 8388624 | tf_op jit(solution)/shard_map/psum | solution.py:160
  386.9 23.4 %gather_fusion.1 = bf16[4608,1024]{1,0:T(8,128)(2,1)} fusion(bf16[2048,1024]{1,0:T(8,128)(2,1)} %multiply_convert_fusion.2, s32[5120]{0:T(1024)S(1)} %pad_clamp_fusion), kind=kCustom, calls=%fused_computation.1 | custom fusion | bytes 18892800 | tf_op jit(solution)/shard_map/gather | solution.py:178
  414.5 39.0 %gather_fusion.4 = f32[4608]{0:T(1024)S(1)} fusion(f32[2048,2]{0,1:T(2,128)S(1)} %broadcast_divide_fusion, s32[4608]{0:T(1024)S(1)} %get-tuple-element.404), kind=kCustom, calls=%fused_computation.4 | custom fusion | bytes 73728 | tf_op jit(solution)/shard_map/gather | solution.py:198
  453.5 39.0 %gather_fusion.3 = f32[4608]{0:T(1024)S(1)} fusion(f32[2048,2]{0,1:T(2,128)S(1)} %broadcast_divide_fusion, s32[4608]{0:T(1024)S(1)} %get-tuple-element.405), kind=kCustom, calls=%fused_computation.3 | custom fusion | bytes 73728 | tf_op jit(solution)/shard_map/gather | solution.py:198
  492.6 16.4 fusion.148
  509.1 21.5 %fusion.171 = (bf16[8,576,1,352]{3,1,0,2:T(8,128)(2,1)}, bf16[8,576,1,352]{3,1,0,2:T(8,128)(2,1)}, bf16[8,576,352]{2,1,0:T(8,128)(2,1)}) fusion(f32[8,576,2,352]{3,1,2,0:T(8,128)} %fusion.148, bf16[8,352,1024]{2,1,0:T(8,128)(2,1)} %param.26, f32[8,576,1024]{2,1,0:T(8,128)} %bitcast.367, f32[8,576]{1,0:T(8,128)S(1)} %select_n.136, pred[8,576]{1,0:T(8,128)(4,1)S(1)} %ge.498), kind=kOutput, calls=%fused_computation.250 | convolution fusion | flops 3378216960 | bytes 47372800 | tf_op jit(solution)/shard_map/ecd,efd->ecf/dot_general | solution.py:204
  530.6 16.6 fusion.142
  547.2 15.1 concatenate.87
  562.3 28.6 %gather_fusion.6 = f32[4096,1024]{1,0:T(8,128)} fusion(f32[4609,1024]{1,0:T(8,128)} %concatenate.87, s32[4096]{0:T(1024)S(1)} %broadcast_clamp_fusion), kind=kCustom, calls=%fused_computation.6 | custom fusion | bytes 33570816 | tf_op jit(solution)/shard_map/gather | solution.py:222
  590.9 20.0 reshape.883
  611.0 23.7 %reduce_sum.206 = f32[2048,1024]{1,0:T(8,128)} reduce(f32[2048,2,1024]{2,1,0:T(2,128)} %reshape.883, f32[]{:T(128)} %constant.111.clone.1), dimensions={1}, to_apply=%region_21.22 | reduce | flops 2097152 | bytes 25165828 | tf_op jit(solution)/shard_map/reduce_sum | solution.py:222
  651.6 28.7 %gather_fusion.2 = f32[4096,1024]{1,0:T(8,128)} fusion(f32[4609,1024]{1,0:T(8,128)} %concatenate.82, s32[4096]{0:T(1024)S(1)} %broadcast_clamp_fusion), kind=kCustom, calls=%fused_computation.2 | custom fusion | bytes 33570816 | tf_op jit(solution)/shard_map/gather | solution.py:188
  680.3 20.1 reshape.851
  700.4 35.9 %multiply_reduce_fusion.2 = (f32[2048,2]{1,0:T(8,128)S(1)}, f32[2048,1024]{1,0:T(8,128)}) fusion(f32[2048,2,1024]{2,1,0:T(2,128)} %reshape.851, f32[2048,1024]{1,0:T(8,128)} %convert_element_type.568, f32[2048,2]{1,0:T(8,128)S(1)} %copy.207), kind=kLoop, calls=%fused_computation.199 | loop fusion | flops 14675968 | bytes 33587200 | tf_op jit(solution)/shard_map/reduce_sum | solution.py:193
  736.6 36.8 %psum.38 = f32[2048,2]{0,1:T(2,128)S(1)} all-reduce(f32[2048,2]{0,1:T(2,128)S(1)} %copy.214), channel_id=1, replica_groups=mesh['dp'=4,'tensor'=8] {'tensor'}, use_global_device_ids=true, to_apply=%region_24.25 | all-reduce | flops 4096 | bytes 32768 | tf_op jit(solution)/shard_map/psum | solution.py:194
  773.6 131.3 %all-reduce.15.cloned.1.call-done = f32[2048,1024]{1,0:T(8,128)} async-done(((f32[2048,1024]{1,0:T(8,128)}), f32[2048,1024]{1,0:T(8,128)}) %all-reduce.15.cloned.1.call-update) | async-done | bytes 8388624 | tf_op jit(solution)/shard_map/psum | solution.py:223
  925.3 216.5 %while.29 = (s32[]{:T(128)}, bf16[2,1024,3,2,64]{1,4,3,2,0:T(8,128)(2,1)}, f32[2,32,2]{1,2,0:T(2,128)S(1)}, bf16[2,1024,3,2,64]{1,4,3,2,0:T(8,128)(2,1)}, s32[2,...) while((s32[]{:T(128)}, ...), condition=%wide.region_32.33_spmd.clone.clone, body=%wide.region_29.32_spmd.clone.clone.sunk | while | flops 1754921472 | bytes 257252560 | solution.py:281
  971.1 12.3 fusion.289
  1075.0 12.3 fusion.289
  1109.4 12.1 fusion.298
  1171.5 12.6 fusion.172
  1184.2 17.5 fusion.156
  1204.2 459.3 %all-reduce.17.cloned.1.call-done = (f32[2048,1024]{1,0:T(8,128)}, f32[2048,1024]{1,0:T(8,128)}) async-done(((f32[2048,1024]{1,0:T(8,128)}, f32[2048,1024]{1,0:T(8,128)}), (f32[2048,1024]{1,0:T(8,128)}, f32[2048,1024]{1,0:T(8,128)})) %all-reduce.17.cloned.1.call-update) | async-done | bytes 16777232 | tf_op jit(solution)/shard_map/psum | solution.py:190
  1663.5 12.3 add.702
  1709.5 31.0 %reduce-scatter.7.cloned.1.call-done = f32[256,3,128]{2,0,1:T(8,128)} async-done(((f32[1024,3,128]{2,0,1:T(8,128)}), f32[256,3,128]{2,0,1:T(8,128)}) %reduce-scatter.7.cloned.1.call-update) | async-done | bytes 393232 | tf_op jit(solution)/shard_map/reduce_scatter | solution.py:295
  1740.5 93.9 %reduce-scatter.15.cloned.1.call-done = f32[8,352,256]{2,1,0:T(8,128)} async-done(((f32[8,352,1024]{2,1,0:T(8,128)}), f32[8,352,256]{2,1,0:T(8,128)}) %reduce-scatter.15.cloned.1.call-update) | async-done | bytes 2883600 | tf_op jit(solution)/shard_map/reduce_scatter | solution.py:216
  1834.4 166.2 %reduce-scatter.13.cloned.1.call-done = f32[8,2,256,352]{2,3,1,0:T(8,128)} async-done(((f32[8,2,1024,352]{2,3,1,0:T(8,128)}), f32[8,2,256,352]{2,3,1,0:T(8,128)}) %reduce-scatter.13.cloned.1.call-update) | async-done | bytes 5767184 | tf_op jit(solution)/shard_map/reduce_scatter | solution.py:215
  (381 shorter events, 402.4 us)
Async XLA Ops:
  7.2 368.2 %all-reduce.13.cloned.1.call-start = ((), (), s32[]{:S(2)}) async-start(), calls=%async_computation.5 | async-start | bytes 16777216 | tf_op jit(solution)/shard_map/psum | solution.py:160
  23.3 74.5 %copy-start.31 = (bf16[128,1024]{1,0:T(8,128)(2,1)S(1)}, bf16[128,1024]{1,0:T(8,128)(2,1)}, u32[]{:S(2)}) copy-start(bf16[128,1024]{1,0:T(8,128)(2,1)} %param.22) | copy-start | bytes 786436
  102.5 802.4 %all-reduce.15.cloned.1.call-start = ((), (), s32[]{:S(2)}) async-start(), calls=%async_computation.6 | async-start | bytes 16777216 | tf_op jit(solution)/shard_map/psum | solution.py:223
  161.4 347.7 %copy-start.52 = (pred[8,576]{1,0:T(8,128)(4,1)}, pred[8,576]{1,0:T(8,128)(4,1)S(1)}, u32[]{:S(2)}) copy-start(pred[8,576]{1,0:T(8,128)(4,1)S(1)} %ge.498) | copy-start | bytes 13828
  193.0 191.5 %copy-start.65 = (f32[1024]{0:T(1024)S(1)}, f32[1024]{0:T(1024)}, u32[]{:S(2)}) copy-start(f32[1024]{0:T(1024)} %param.20) | copy-start | bytes 12292
  386.9 23.5 %copy-start.62 = (bf16[1024,8]{0,1:T(8,128)(2,1)S(1)}, bf16[1024,8]{0,1:T(8,128)(2,1)}, u32[]{:S(2)}) copy-start(bf16[1024,8]{0,1:T(8,128)(2,1)} %param.24) | copy-start | bytes 49156
  414.0 39.5 %copy-start.45 = (f32[2048,2]{0,1:T(2,128)}, f32[2048,2]{0,1:T(2,128)S(1)}, u32[]{:S(2)}) copy-start(f32[2048,2]{0,1:T(2,128)S(1)} %get-tuple-element.343) | copy-start | bytes 49156
  414.0 39.5 %copy-start.50 = (f32[2048]{0:T(1024)}, f32[2048]{0:T(1024)S(1)}, u32[]{:S(2)}) copy-start(f32[2048]{0:T(1024)S(1)} %get-tuple-element.342) | copy-start | bytes 24580
  492.6 16.4 copy-start.35
  634.7 1028.8 %all-reduce.17.cloned.1.call-start = ((), (), s32[]{:S(2)}) async-start(), calls=%async_computation.12 | async-start | bytes 33554432 | tf_op jit(solution)/shard_map/psum | solution.py:190
  700.3 73.0 %copy-start.51 = (f32[2048]{0:T(1024)S(1)}, f32[2048]{0:T(1024)}, u32[]{:S(2)}) copy-start(f32[2048]{0:T(1024)} %copy-done.50) | copy-start | bytes 24580
  700.4 73.0 %copy-start.46 = (f32[2048,2]{0,1:T(2,128)S(1)}, f32[2048,2]{0,1:T(2,128)}, u32[]{:S(2)}) copy-start(f32[2048,2]{0,1:T(2,128)} %copy-done.45) | copy-start | bytes 49156
  700.4 73.1 %copy-start.44 = (s32[2048,2]{0,1:T(2,128)S(1)}, s32[2048,2]{0,1:T(2,128)}, u32[]{:S(2)}) copy-start(s32[2048,2]{0,1:T(2,128)} %param.28) | copy-start | bytes 49156
  700.4 73.1 %copy-start.41 = (f32[2048]{0:T(1024)S(1)}, f32[2048]{0:T(1024)}, u32[]{:S(2)}) copy-start(f32[2048]{0:T(1024)} %copy-done.40) | copy-start | bytes 24580
  700.4 73.2 %copy-start.25 = (f32[2048,8]{0,1:T(8,128)S(1)}, f32[2048,8]{0,1:T(8,128)}, u32[]{:S(2)}) copy-start(f32[2048,8]{0,1:T(8,128)} %copy-done.24) | copy-start | bytes 196612
  700.4 73.2 %copy-start.38 = (f32[2048]{0:T(1024)S(1)}, f32[2048]{0:T(1024)}, u32[]{:S(2)}) copy-start(f32[2048]{0:T(1024)} %copy-done.37) | copy-start | bytes 24580
  700.4 204.5 %copy-start.48 = (f32[2048]{0:T(1024)S(1)}, f32[2048]{0:T(1024)}, u32[]{:S(2)}) copy-start(f32[2048]{0:T(1024)} %copy-done.47) | copy-start | bytes 24580
  700.4 204.5 %copy-start.63 = (bf16[1024,8]{0,1:T(8,128)(2,1)S(1)}, bf16[1024,8]{0,1:T(8,128)(2,1)}, u32[]{:S(2)}) copy-start(bf16[1024,8]{0,1:T(8,128)(2,1)} %param.24) | copy-start | bytes 49156
  700.4 204.5 %copy-start.66 = (f32[1024]{0:T(1024)S(1)}, f32[1024]{0:T(1024)}, u32[]{:S(2)}) copy-start(f32[1024]{0:T(1024)} %param.20) | copy-start | bytes 12292
  773.5 141.3 %copy-start.29 = (f32[2048,8]{0,1:T(8,128)}, f32[2048,8]{0,1:T(8,128)S(1)}, u32[]{:S(2)}) copy-start(f32[2048,8]{0,1:T(8,128)S(1)} %select_reduce_fusion.2) | copy-start | bytes 196612
  773.6 141.2 %copy-start.54 = (f32[2048]{0:T(1024)}, f32[2048]{0:T(1024)S(1)}, u32[]{:S(2)}) copy-start(f32[2048]{0:T(1024)S(1)} %neg.13) | copy-start | bytes 24580
  773.6 141.2 %copy-start.59 = (f32[2048]{0:T(1024)S(1)}, f32[2048]{0:T(1024)}, u32[]{:S(2)}) copy-start(f32[2048]{0:T(1024)} %copy-done.58) | copy-start | bytes 24580
  927.5 30.8 %copy-start.5 = (bf16[1024,3,2,64]{0,3,2,1:T(8,128)(2,1)}, bf16[1024,3,2,64]{0,3,2,1:T(8,128)(2,1)S(1)}, u32[]{:S(2)}) copy-start(bf16[1024,3,2,64]{0,3,2,1:T(8,128)(2,1)S(1)} %dynamic-slice_bitcast_fusion.21) | copy-start | bytes 2359300 | tf_op jit(solution)/shard_map/while
  1005.5 12.1 copy-start.16
  1031.5 30.8 %copy-start.5 = (bf16[1024,3,2,64]{0,3,2,1:T(8,128)(2,1)}, bf16[1024,3,2,64]{0,3,2,1:T(8,128)(2,1)S(1)}, u32[]{:S(2)}) copy-start(bf16[1024,3,2,64]{0,3,2,1:T(8,128)(2,1)S(1)} %dynamic-slice_bitcast_fusion.21) | copy-start | bytes 2359300 | tf_op jit(solution)/shard_map/while
  1154.7 546.7 %reduce-scatter.11.cloned.1.call-start = ((), (), s32[]{:S(2)}) async-start(), calls=%async_computation.9 | async-start | bytes 40960 | tf_op jit(solution)/shard_map/reduce_scatter | solution.py:298
  1160.1 549.5 %reduce-scatter.9.cloned.1.call-start = ((), (), s32[]{:S(2)}) async-start(), calls=%async_computation.8 | async-start | bytes 655360 | tf_op jit(solution)/shard_map/reduce_scatter | solution.py:296
  1165.2 575.4 %reduce-scatter.7.cloned.1.call-start = ((), (), s32[]{:S(2)}) async-start(), calls=%async_computation.7 | async-start | bytes 1966080 | tf_op jit(solution)/shard_map/reduce_scatter | solution.py:295
  1171.4 663.0 %reduce-scatter.15.cloned.1.call-start = ((), (), s32[]{:S(2)}) async-start(), calls=%async_computation.11 | async-start | bytes 14417920 | tf_op jit(solution)/shard_map/reduce_scatter | solution.py:216
  1184.1 816.5 %reduce-scatter.13.cloned.1.call-start = ((), (), s32[]{:S(2)}) async-start(), calls=%async_computation.10 | async-start | bytes 28835840 | tf_op jit(solution)/shard_map/reduce_scatter | solution.py:215
  1663.5 12.3 copy-start.12
  1675.8 13.7 copy-start.57
  (66 other events, 322.4 us)
Sparse Core Ops, SparseCore 0:
  102.6 272.7 all-reduce.12
  634.9 269.9 all-reduce.14
  1154.8 508.7 all-reduce.16
  1666.3 18.5 reduce-scatter.10
  1687.9 21.6 reduce-scatter.8
  1712.5 27.9 reduce-scatter.6
  1743.7 90.6 reduce-scatter.14
  1837.6 162.9 reduce-scatter.12
where the time goes:
time: 2010 us
  waiting for transfers between devices  1070 us (53%)
  local copies, waits for them, and re-layouts  390 us (19%)
  matrix products  330 us (16%)
  other arithmetic  145 us (7%)
  blocking collectives  43.4 us (2%)
    psum x1, waiting for transfers between devices, shards(): moe_out = lax.psum(moe_part, 'tensor')  459 us
    psum x1, waiting for transfers between devices, shards(): attn_out = lax.psum(attn_part, 'tensor')  182 us
    reduce_scatter x1, waiting for transfers between devices, shards(): lax.psum_scatter(w_in_local, 'dp', scatter_dimension=2, tiled=True)  166 us
    psum x1, waiting for transfers between devices, shards(): moe_in_sum = lax.psum(moe_in_part, 'tensor')  131 us
    reduce_scatter x1, waiting for transfers between devices, shards(): lax.psum_scatter(w_down_local, 'dp', scatter_dimension=2, tiled=True)  93.9 us
    dot_general x8, matrix products, block_scores(): jnp.einsum('qkb,bh->hqk', onehot, rel_bias, preferred_element_type=jnp.fl...  91.5 us
    gather x2, local copies, waits for them, and re-layouts, shards(): pair_rows = out_rows[token_target]  48.8 us
    gather x2, local copies, waits for them, and re-layouts, shards(): moe_in_part = jnp.sum(grad_rows[token_target], axis=1)  48.7 us
  transfers between devices with their start and end apart: 8, of which 7 were waited for; matrix products, arithmetic and copies ran while one was open for 13% of the time, Pallas kernels for 0%

commit v1 on v0

v1 whole, which is shorter than its diff:
```python
import functools
import math

import jax
import jax.numpy as jnp
import numpy as np
from jax import lax
from jax.experimental import pallas as pl
from jax.experimental.pallas import tpu as pltpu
from jax.sharding import PartitionSpec as P

F32 = jnp.float32
BF16 = jnp.bfloat16


def dot(a, b, ca, cb):
    return lax.dot_general(a, b, (((ca,), (cb,)), ((), ())), preferred_element_type=F32)


NB=32; MAXDIST=128; HD=64; NEG=-1000000000.0

def thresholds(bucket_count, reach):
    half_count = bucket_count // 2
    exact_count = half_count // 2
    listing = []
    for bucket_level in range(1, half_count):
        if bucket_level <= exact_count:
            listing.append(bucket_level)
        else:
            distance = exact_count
            while (exact_count + int(np.floor(np.log(distance / exact_count) / np.log(reach / exact_count) * (half_count - exact_count))) < bucket_level):
                distance += 1
            listing.append(distance)
    return listing

THRESH = thresholds(NB, MAXDIST)
HALF = NB // 2
CH = 128

def distance(row0, rows, cols, origin):
    r = lax.broadcasted_iota(jnp.int32, (rows, cols), 0)
    c = lax.broadcasted_iota(jnp.int32, (rows, cols), 1)
    return r + (row0 - origin) - c

def build_bias(rb_ref, bias, heads, length, block):
    total = 2 * length - block
    origin = length - block
    low_end = (origin - THRESH[-1] + 1) // CH * CH
    high_start = -(-(origin + block - 1 + THRESH[-1]) // CH) * CH
    for h in range(heads):
        bias[h, 0:low_end, :] = jnp.full((low_end, block), rb_ref[(HALF - 1) * heads + h], F32)
        bias[h, high_start:total, :] = jnp.full((total - high_start, block), rb_ref[(NB - 1) * heads + h], F32)

        def chunk(i, carry):
            row0 = pl.multiple_of(low_end + i * CH, CH)
            d = distance(row0, CH, block, origin)
            mag = jnp.abs(d)
            back = jnp.full((CH, block), rb_ref[h], F32)
            ahead = jnp.full((CH, block), rb_ref[HALF * heads + h], F32)
            for level, t in enumerate(THRESH):
                far = mag >= t
                back = jnp.where(far, rb_ref[(level + 1) * heads + h], back)
                ahead = jnp.where(far, rb_ref[(HALF + level + 1) * heads + h], ahead)
            bias[h, pl.ds(row0, CH), :] = jnp.where(d > 0, ahead, back)
            return carry
        lax.fori_loop(0, (high_start - low_end) // CH, chunk, 0)

def fwd_kernel(heads, length, block, rb_ref, q_ref, k_ref, vt_ref, segr_ref, segc_ref, o_ref, bias):
    @pl.when(pl.program_id(0) == 0)
    def _():
        build_bias(rb_ref, bias, heads, length, block)
    lanes = heads * HD
    lane = lax.broadcasted_iota(jnp.int32, (block, lanes), 1) // HD
    def step(i, carry):
        q0 = pl.multiple_of(i * block, block)
        start = pl.multiple_of(length - block - q0, block)
        qb = q_ref[pl.ds(q0, block), :] * 0.125
        same = segc_ref[...] == segr_ref[0, :, pl.ds(q0, block)]
        pieces = []
        for h in range(heads):
            qm = jnp.where(lane == h, qb, jnp.zeros_like(qb)) if heads > 1 else qb
            s = dot(k_ref[...], qm, 1, 1) + bias[h, pl.ds(start, length), :]
            s = jnp.where(same, s, NEG)
            p = jnp.exp(s - jnp.max(s, axis=0, keepdims=True))
            total = jnp.sum(p, axis=0, keepdims=True)
            p = (p * (1.0 / total)).astype(BF16)
            pieces.append(dot(vt_ref[h * HD:(h + 1) * HD, :], p, 1, 0))
        o = jnp.concatenate(pieces, axis=0) if heads > 1 else pieces[0]
        o_ref[pl.ds(q0, block), :] = o.T.astype(BF16).astype(F32)
        return carry
    lax.fori_loop(0, length // block, step, 0)

def bwd_kernel(heads, length, block, rb_ref, q_ref, k_ref, v_ref, kt_ref, do_ref, segr_ref, segc_ref,
               dq_ref, dk_ref, dv_ref, db_ref, bias, dbias, dk, dv):
    step_id = pl.program_id(0)
    total_rows = 2 * length - block
    @pl.when(step_id == 0)
    def _():
        build_bias(rb_ref, bias, heads, length, block)
        dbias[...] = jnp.zeros_like(dbias)
    dk[...] = jnp.zeros_like(dk)
    dv[...] = jnp.zeros_like(dv)
    lanes = heads * HD
    lane = lax.broadcasted_iota(jnp.int32, (block, lanes), 1) // HD
    def step(i, carry):
        q0 = pl.multiple_of(i * block, block)
        start = pl.multiple_of(length - block - q0, block)
        qb = q_ref[pl.ds(q0, block), :] * 0.125
        dob = do_ref[pl.ds(q0, block), :].astype(BF16)
        same = segc_ref[...] == segr_ref[0, :, pl.ds(q0, block)]
        pieces = []
        for h in range(heads):
            qm = jnp.where(lane == h, qb, jnp.zeros_like(qb)) if heads > 1 else qb
            dom = jnp.where(lane == h, dob, jnp.zeros_like(dob)) if heads > 1 else dob
            s = dot(k_ref[...], qm, 1, 1) + bias[h, pl.ds(start, length), :]
            s = jnp.where(same, s, NEG)
            p = jnp.exp(s - jnp.max(s, axis=0, keepdims=True))
            p = p * (1.0 / jnp.sum(p, axis=0, keepdims=True))
            dp = dot(v_ref[...], dom, 1, 1)
            ds = (p * (dp - jnp.sum(p * dp, axis=0, keepdims=True))).astype(BF16)
            dbias[h, pl.ds(start, length), :] += ds.astype(F32)
            dk[...] += dot(ds, qm, 1, 0)
            dv[...] += dot(p.astype(BF16), dom, 1, 0)
            pieces.append(dot(kt_ref[h * HD:(h + 1) * HD, :], ds, 1, 0))
        dq = jnp.concatenate(pieces, axis=0) if heads > 1 else pieces[0]
        dq_ref[pl.ds(q0, block), :] = (dq * 0.125).T.astype(BF16)
        return carry
    lax.fori_loop(0, length // block, step, 0)
    dk_ref[...] = dk[...].astype(BF16)
    dv_ref[...] = dv[...].astype(BF16)

    @pl.when(step_id == pl.num_programs(0) - 1)
    def _():
        origin = length - block
        low_end = (origin - THRESH[-1] + 1) // CH * CH
        high_start = -(-(origin + block - 1 + THRESH[-1]) // CH) * CH
        def fold(x):
            return jnp.sum(x, axis=0, keepdims=True)
        for h in range(heads):
            def rows(lo, hi):
                def body(i, acc):
                    r0 = pl.multiple_of(lo + i * CH, CH)
                    return acc + fold(dbias[h, pl.ds(r0, CH), :])
                return lax.fori_loop(0, (hi - lo) // CH, body, jnp.zeros((1, block), F32))
            def chunk(i, sums):
                r0 = pl.multiple_of(low_end + i * CH, CH)
                g = dbias[h, pl.ds(r0, CH), :]
                d = distance(r0, CH, block, origin)
                mag = jnp.abs(d)
                gb = jnp.where(d > 0, 0.0, g)
                ga = jnp.where(d > 0, g, 0.0)
                out = [sums[0] + fold(gb), sums[HALF] + fold(ga)]
                tb, ta = [], []
                for t in THRESH:
                    far = mag >= t
                    tb.append(fold(jnp.where(far, gb, 0.0)))
                    ta.append(fold(jnp.where(far, ga, 0.0)))
                new = [out[0]] + [sums[1 + n] + tb[n] for n in range(HALF - 1)]
                new += [out[1]] + [sums[HALF + 1 + n] + ta[n] for n in range(HALF - 1)]
                return tuple(new)
            sums = lax.fori_loop(0, (high_start - low_end) // CH, chunk,
                                 tuple(jnp.zeros((1, block), F32) for _ in range(NB)))
            left, right = rows(0, low_end), rows(high_start, total_rows)
            for b in range(NB):
                val = sums[b]
                if b not in (HALF - 1, NB - 1):
                    val = val - sums[b + 1]
                else:
                    val = val + (left if b == HALF - 1 else right)
                db_ref[h, b:b + 1, :] = jnp.broadcast_to(jnp.sum(val, axis=1, keepdims=True), (1, 128))

def attention_fwd(q, k, vt, seg, rb, block=256):
    tok, lanes = q.shape
    seqs, length = seg.shape
    heads = lanes // HD
    full = pl.BlockSpec((length, lanes), lambda s: (s, 0))
    return pl.pallas_call(
        functools.partial(fwd_kernel, heads, length, block),
        grid=(seqs,),
        out_shape=jax.ShapeDtypeStruct((tok, lanes), F32),
        in_specs=[pl.BlockSpec(memory_space=pltpu.SMEM), full, full,
                  pl.BlockSpec((lanes, length), lambda s: (0, s)),
                  pl.BlockSpec((1, 1, length), lambda s: (s, 0, 0)),
                  pl.BlockSpec((length, 1), lambda s: (s, 0))],
        out_specs=full,
        scratch_shapes=[pltpu.VMEM((heads, 2 * length - block, block), F32)],
        compiler_params=pltpu.CompilerParams(vmem_limit_bytes=56 << 20),
        cost_estimate=pl.CostEstimate(flops=4 * tok * length * lanes, bytes_accessed=tok * lanes * 10, transcendentals=tok * length * heads),
        name="attn_fwd",
    )(rb, q, k, vt, seg.reshape(seqs, 1, length), seg.reshape(tok, 1))

def attention_bwd(q, k, v, kt, do, seg, rb, block=256):
    tok, lanes = q.shape
    seqs, length = seg.shape
    heads = lanes // HD
    full = pl.BlockSpec((length, lanes), lambda s: (s, 0))
    sh = jax.ShapeDtypeStruct((tok, lanes), BF16)
    return pl.pallas_call(
        functools.partial(bwd_kernel, heads, length, block),
        grid=(seqs,),
        out_shape=(sh, sh, sh, jax.ShapeDtypeStruct((heads, NB, 128), F32)),
        in_specs=[pl.BlockSpec(memory_space=pltpu.SMEM), full, full, full,
                  pl.BlockSpec((lanes, length), lambda s: (0, s)), full,
                  pl.BlockSpec((1, 1, length), lambda s: (s, 0, 0)),
                  pl.BlockSpec((length, 1), lambda s: (s, 0))],
        out_specs=(full, full, full, pl.BlockSpec((heads, NB, 128), lambda s: (0, 0, 0))),
        scratch_shapes=[pltpu.VMEM((heads, 2 * length - block, block), F32)] * 2
        + [pltpu.VMEM((length, lanes), F32)] * 2,
        compiler_params=pltpu.CompilerParams(vmem_limit_bytes=56 << 20),
        cost_estimate=pl.CostEstimate(flops=10 * tok * length * lanes, bytes_accessed=tok * lanes * 20, transcendentals=tok * length * heads),
        name="attn_bwd",
    )(rb, q, k, v, kt, do, seg.reshape(seqs, 1, length), seg.reshape(tok, 1))


EXPERTS=8; CAP=576; SLOTS=EXPERTS*CAP; LN=128
GC = math.sqrt(2.0/math.pi)

def spread(dst, row0, sub, src, rows, width, dtype=None):
    for j in range(sub):
        dst[pl.ds(row0 * sub + j, rows, stride=sub), :] = src[:, j * LN:(j + 1) * LN].astype(F32)

def dispatch_kernel(tok, sub, step_slots, with_share, tgt, src, *rest):
    if with_share:
        share, out, share_out, rows_in, rows_out, share_rows = rest
    else:
        out, rows_in, rows_out = rest
    step = pl.program_id(0)
    @pl.when(step == 0)
    def _():
        def load(i, c):
            t0 = pl.multiple_of(i * 64, 64)
            spread(rows_in, t0, sub, src.at[pl.ds(t0, 64), :], 64, sub * LN)
            return c
        lax.fori_loop(0, tok // 64, load, 0)
        def zero(i, c):
            r0 = pl.multiple_of(i * 8 * sub, 8 * sub)
            rows_out[pl.ds(r0, 8 * sub), :] = jnp.zeros((8 * sub, LN), F32)
            if with_share:
                share_rows[pl.ds(pl.multiple_of(i * 8, 8), 8), :] = jnp.zeros((8, LN), F32)
            return c
        lax.fori_loop(0, SLOTS // 8, zero, 0)
        def move(i, c):
            for u in range(8):
                t = i * 8 + u
                row = rows_in[pl.ds(pl.multiple_of(t * sub, sub), sub), :]
                for choice in range(2):
                    slot = tgt[choice * tok + t]
                    rows_out[pl.ds(pl.multiple_of(slot * sub, sub), sub), :] = row
                    if with_share:
                        share_rows[pl.ds(slot, 1), :] = share[pl.ds(choice * tok + t, 1), :]
            return c
        lax.fori_loop(0, tok // 8, move, 0)
    base = step * step_slots
    def emit(i, c):
        s0 = pl.multiple_of(i * 64, 64)
        for j in range(sub):
            out[pl.ds(s0, 64), j * LN:(j + 1) * LN] = rows_out[pl.ds((base + s0) * sub + j, 64, stride=sub), :].astype(BF16)
        return c
    lax.fori_loop(0, step_slots // 64, emit, 0)
    if with_share:
        share_out[...] = share_rows[pl.ds(pl.multiple_of(base, step_slots), step_slots), :]

def dispatch(tgt, src, share=None, step_slots=512):
    tok, width = src.shape
    sub = width // LN
    ws = share is not None
    steps = SLOTS // step_slots
    whole = lambda shape: pl.BlockSpec(shape, lambda i, t: (0, 0), pipeline_mode=pl.Buffered(1))
    out_shape = [jax.ShapeDtypeStruct((SLOTS, width), BF16)]
    out_specs = [pl.BlockSpec((step_slots, width), lambda i, t: (i, 0))]
    scratch = [pltpu.VMEM((tok * sub, LN), F32), pltpu.VMEM(((SLOTS + 1) * sub, LN), F32)]
    in_specs = [whole((tok, width))]
    args = [src]
    if ws:
        in_specs.append(whole((2 * tok, LN)))
        args.append(share)
        out_shape.append(jax.ShapeDtypeStruct((SLOTS, LN), F32))
        out_specs.append(pl.BlockSpec((step_slots, LN), lambda i, t: (i, 0)))
        scratch.append(pltpu.VMEM((SLOTS + 8, LN), F32))
    r = pl.pallas_call(
        functools.partial(dispatch_kernel, tok, sub, step_slots, ws),
        grid_spec=pltpu.PrefetchScalarGridSpec(num_scalar_prefetch=1, grid=(steps,), in_specs=in_specs,
                                               out_specs=out_specs, scratch_shapes=scratch),
        out_shape=out_shape,
        compiler_params=pltpu.CompilerParams(vmem_limit_bytes=56 << 20),
        cost_estimate=pl.CostEstimate(flops=0, bytes_accessed=tok * width * 4 + SLOTS * width * 2, transcendentals=0),
        name="dispatch",
    )(tgt, *args)
    return r if ws else r[0]

def combine_rows(tgt, rows, mix, out, tok, sub, t0, count):
    def body(i, c):
        for u in range(8):
            r = i * 8 + u
            a = rows[pl.ds(pl.multiple_of(tgt[t0 + r] * sub, sub), sub), :]
            b = rows[pl.ds(pl.multiple_of(tgt[tok + t0 + r] * sub, sub), sub), :]
            mix[pl.ds(pl.multiple_of(r * sub, sub), sub), :] = a + b
        return c
    lax.fori_loop(0, count // 8, body, 0)
    for j in range(sub):
        out[:, j * LN:(j + 1) * LN] = mix[pl.ds(j, count, stride=sub), :]

def k1_kernel(tok, sub, count, tgt, x, y, sh, win, wdn, act, dgu, mi, sg, rows, sgr, mix):
    step = pl.program_id(0)
    width = sub * LN
    @pl.when(step == 0)
    def _():
        rows[SLOTS * sub:, :] = jnp.zeros((sub, LN), F32)
        sgr[SLOTS:, :] = jnp.zeros((8, LN), F32)
    @pl.when(step < EXPERTS)
    def _():
        g = dot(x[...], win[0, 0], 1, 0)
        u = dot(x[...], win[0, 1], 1, 0)
        h = dot(y[...], wdn[0], 1, 1)
        g2 = g * g
        t = jnp.tanh(GC * (g + 0.044715 * g2 * g))
        half = 0.5 * (1.0 + t)
        gel = g * half
        a = (gel * u).astype(BF16)
        act[0] = a
        sgrow = jnp.sum(a.astype(F32) * h, axis=1, keepdims=True)
        da = sh[:, 0:1] * h
        slope = half + (0.5 * GC) * g * (1.0 - t * t) * (1.0 + (3 * 0.044715) * g2)
        dg = (da * u * slope).astype(BF16)
        du = (da * gel).astype(BF16)
        dgu[0, 0] = dg
        dgu[0, 1] = du
        dx = dot(dg, win[0, 0], 1, 1) + dot(du, win[0, 1], 1, 1)
        row0 = step * CAP
        spread(rows, row0, sub, dx, CAP, width)
        sgr[pl.ds(pl.multiple_of(row0, 8), CAP), :] = jnp.broadcast_to(sgrow, (CAP, LN))
    @pl.when(step >= EXPERTS)
    def _():
        t0 = (step - EXPERTS) * count
        combine_rows(tgt, rows, mix, mi, tok, sub, t0, count)
        def body(i, c):
            for n in range(8):
                r = i * 8 + n
                for choice in range(2):
                    sg[choice, pl.ds(r, 1), :] = sgr[pl.ds(tgt[choice * tok + t0 + r], 1), :]
            return c
        lax.fori_loop(0, count // 8, body, 0)

def k1(tgt, x, y, sh, win, wdn, tok, count=256):
    width = x.shape[1]; sub = width // LN; ff = wdn.shape[1]
    e = lambda i: jnp.minimum(i, EXPERTS - 1)
    c = lambda i: jnp.maximum(i - EXPERTS, 0)
    return pl.pallas_call(
        functools.partial(k1_kernel, tok, sub, count),
        grid_spec=pltpu.PrefetchScalarGridSpec(
            num_scalar_prefetch=1, grid=(EXPERTS + tok // count,),
            in_specs=[pl.BlockSpec((CAP, width), lambda i, t: (e(i), 0)),
                      pl.BlockSpec((CAP, width), lambda i, t: (e(i), 0)),
                      pl.BlockSpec((CAP, LN), lambda i, t: (e(i), 0)),
                      pl.BlockSpec((1, 2, width, ff), lambda i, t: (e(i), 0, 0, 0)),
                      pl.BlockSpec((1, ff, width), lambda i, t: (e(i), 0, 0))],
            out_specs=[pl.BlockSpec((1, CAP, ff), lambda i, t: (e(i), 0, 0)),
                       pl.BlockSpec((1, 2, CAP, ff), lambda i, t: (e(i), 0, 0, 0)),
                       pl.BlockSpec((count, width), lambda i, t: (c(i), 0)),
                       pl.BlockSpec((2, count, LN), lambda i, t: (0, c(i), 0))],
            scratch_shapes=[pltpu.VMEM(((SLOTS + 1) * sub, LN), F32), pltpu.VMEM((SLOTS + 8, LN), F32),
                            pltpu.VMEM((count * sub, LN), F32)]),
        out_shape=[jax.ShapeDtypeStruct((EXPERTS, CAP, ff), BF16), jax.ShapeDtypeStruct((EXPERTS, 2, CAP, ff), BF16),
                   jax.ShapeDtypeStruct((tok, width), F32), jax.ShapeDtypeStruct((2, tok, LN), F32)],
        compiler_params=pltpu.CompilerParams(vmem_limit_bytes=60 << 20),
        cost_estimate=pl.CostEstimate(flops=10 * SLOTS * width * ff, bytes_accessed=60 << 20, transcendentals=SLOTS * ff),
        name="experts_back",
    )(tgt, x, y, sh, win, wdn)

def k2_kernel(tok, sub, count, parts, tgt, x, y, sh, act, dgu, wdn, dwin, dwdn, mo, rows, mix):
    step = pl.program_id(0)
    width = sub * LN
    @pl.when(step == 0)
    def _():
        rows[SLOTS * sub:, :] = jnp.zeros((sub, LN), F32)
    @pl.when(step < EXPERTS)
    def _():
        a = act[0]
        share = sh[:, 0:1]
        eo = dot(a, wdn[0], 1, 0) * share
        spread(rows, step * CAP, sub, eo, CAP, width)
        og = (y[...].astype(F32) * share).astype(BF16)
        wide = width // parts
        dd = dot(a, og, 0, 0)
        for p in range(parts):
            dwdn[p, 0] = dd[:, p * wide:(p + 1) * wide]
        for g in range(2):
            dw = dot(x[...], dgu[0, g], 0, 0)
            for p in range(parts):
                dwin[p, 0, g] = dw[p * wide:(p + 1) * wide, :]
    @pl.when(step >= EXPERTS)
    def _():
        combine_rows(tgt, rows, mix, mo, tok, sub, (step - EXPERTS) * count, count)

def k2(tgt, x, y, sh, act, dgu, wdn, tok, parts, count=256):
    width = x.shape[1]; sub = width // LN; ff = wdn.shape[1]; wide = width // parts
    e = lambda i: jnp.minimum(i, EXPERTS - 1)
    c = lambda i: jnp.maximum(i - EXPERTS, 0)
    return pl.pallas_call(
        functools.partial(k2_kernel, tok, sub, count, parts),
        grid_spec=pltpu.PrefetchScalarGridSpec(
            num_scalar_prefetch=1, grid=(EXPERTS + tok // count,),
            in_specs=[pl.BlockSpec((CAP, width), lambda i, t: (e(i), 0)),
                      pl.BlockSpec((CAP, width), lambda i, t: (e(i), 0)),
                      pl.BlockSpec((CAP, LN), lambda i, t: (e(i), 0)),
                      pl.BlockSpec((1, CAP, ff), lambda i, t: (e(i), 0, 0)),
                      pl.BlockSpec((1, 2, CAP, ff), lambda i, t: (e(i), 0, 0, 0)),
                      pl.BlockSpec((1, ff, width), lambda i, t: (e(i), 0, 0))],
            out_specs=[pl.BlockSpec((parts, 1, 2, wide, ff), lambda i, t: (0, e(i), 0, 0, 0)),
                       pl.BlockSpec((parts, 1, ff, wide), lambda i, t: (0, e(i), 0, 0)),
                       pl.BlockSpec((count, width), lambda i, t: (c(i), 0))],
            scratch_shapes=[pltpu.VMEM(((SLOTS + 1) * sub, LN), F32), pltpu.VMEM((count * sub, LN), F32)]),
        out_shape=[jax.ShapeDtypeStruct((parts, EXPERTS, 2, wide, ff), F32), jax.ShapeDtypeStruct((parts, EXPERTS, ff, wide), F32),
                   jax.ShapeDtypeStruct((tok, width), F32)],
        compiler_params=pltpu.CompilerParams(vmem_limit_bytes=60 << 20),
        cost_estimate=pl.CostEstimate(flops=8 * SLOTS * width * ff, bytes_accessed=80 << 20, transcendentals=0),
        name="experts_weights",
    )(tgt, x, y, sh, act, dgu, wdn)

def slot_targets(routes, order):
    tok = routes.shape[0]
    pos = jnp.arange(tok, dtype=jnp.int32)
    rank = jnp.sum(jnp.where(order[:, None] == pos[None, :], pos[:, None], 0), axis=0)
    earlier = (rank[:, None] > rank[None, :]).astype(BF16)
    ex = jnp.arange(EXPERTS, dtype=jnp.int32)
    onehot = (routes[:, :, None] == ex[None, None, :]).astype(BF16)
    before = dot(earlier, onehot.reshape(tok, 2 * EXPERTS), 1, 0).reshape(tok, 2, EXPERTS)
    first = jnp.sum(onehot[:, 0].astype(F32), axis=0)
    before = before + jnp.stack([jnp.zeros((EXPERTS,), F32), first])[None]
    slot = jnp.sum(before * onehot.astype(F32), axis=2).astype(jnp.int32)
    return jnp.where(slot < CAP, routes * CAP + slot, SLOTS).T.reshape(-1)


MESH = pl.DeviceIdType.MESH


class Ring:
    def __init__(self, n, rows):
        self.n = n
        self.inner = 1
        while (self.inner * 2) ** 2 <= n:
            self.inner *= 2
        self.outer = n // self.inner
        self.rows = rows
        self.rows_b = max(rows // 8 // 8 * 8, 8)
        self.rows_a = rows - self.rows_b
        self.count = next(c for c in (4, 2, 1) if self.rows_a % (8 * c) == 0)
        self.piece = self.rows_a // self.count
        self.pieces = [(p * self.piece, self.piece) for p in range(self.count)]

    def place(self):
        me = lax.axis_index("tensor")
        self.o, self.i = lax.div(me, self.inner), lax.rem(me, self.inner)

    def shard(self, back, side=0):
        return (lax.rem(self.o - back + 2 * self.outer, self.outer) * self.inner
                + lax.rem(self.i - side + self.inner, self.inner))

    def barrier(self):
        peers = [self.shard(-1)] + ([self.shard(1)] if self.outer > 2 else [])
        peers += [self.shard(0, j) for j in range(1, self.inner)]
        sem = pltpu.get_barrier_semaphore()
        for peer in peers:
            pl.semaphore_signal(sem, inc=1, device_id={"tensor": peer}, device_id_type=MESH)
        pl.semaphore_wait(sem, len(peers))

    def gather_semaphores(self):
        dma = pltpu.SemaphoreType.DMA
        one = [dma((self.outer - 1, self.count)), dma((self.inner - 1, self.outer, self.count)),
               dma((self.inner, self.outer - 1)), dma((self.inner - 1,))]
        return one + one

    def reduce_scratch(self, width):
        dma = pltpu.SemaphoreType.DMA
        one = [dma((self.inner - 1, self.outer, self.count)), dma((self.outer - 1, self.count)),
               dma((self.inner, self.outer - 1)), dma((self.inner - 1,))]
        return [pltpu.VMEM((self.inner - 1, self.outer, self.rows_a, width), F32),
                pltpu.VMEM((self.outer - 1, self.rows_a, width), F32),
                pltpu.VMEM((self.inner, self.outer - 1, self.rows_b, width), F32),
                pltpu.VMEM((self.inner - 1, self.rows_b, width), F32)] + one + one


def remote(src, dst, send, recv, peer):
    return pltpu.make_async_remote_copy(src_ref=src, dst_ref=dst, send_sem=send, recv_sem=recv,
                                        device_id={"tensor": peer}, device_id_type=MESH)


class Gather:
    def __init__(self, ring, view, own, sems):
        self.r, self.view, self.own = ring, view, own
        (self.s_oa, self.s_ia, self.s_ob, self.s_ib, self.r_oa, self.r_ia, self.r_ob, self.r_ib) = sems
        self.sent = []

    def outer_a(self, step, p):
        r = self.r
        row, rows = r.pieces[p]
        shard = r.shard(step)
        src = self.own(row, rows) if step == 0 else self.view(shard, row, rows)
        return remote(src, self.view(shard, row, rows), self.s_oa.at[step, p], self.r_oa.at[step, p], r.shard(-1))

    def inner_a(self, j, step, p):
        r = self.r
        row, rows = r.pieces[p]
        shard = r.shard(step)
        src = self.own(row, rows) if step == 0 else self.view(shard, row, rows)
        return remote(src, self.view(shard, row, rows), self.s_ia.at[j - 1, step, p], self.r_ia.at[j - 1, step, p],
                      r.shard(0, -j))

    def outer_b(self, j, step):
        r = self.r
        shard = r.shard(step, j)
        src = self.own(r.rows_a, r.rows_b) if step == 0 and j == 0 else self.view(shard, r.rows_a, r.rows_b)
        return remote(src, self.view(shard, r.rows_a, r.rows_b), self.s_ob.at[j, step], self.r_ob.at[j, step], r.shard(-1))

    def inner_b(self, j):
        r = self.r
        return remote(self.own(r.rows_a, r.rows_b), self.view(r.shard(0), r.rows_a, r.rows_b),
                      self.s_ib.at[j - 1], self.r_ib.at[j - 1], r.shard(0, -j))

    def go(self, copy):
        copy.start()
        self.sent.append(copy)

    def start_a(self, p):
        self.go(self.outer_a(0, p))
        for j in range(1, self.r.inner):
            self.go(self.inner_a(j, 0, p))

    def start_b(self):
        for j in range(1, self.r.inner):
            self.go(self.inner_b(j))
        self.go(self.outer_b(0, 0))

    def middle(self):
        r = self.r
        for j in range(1, r.inner):
            self.inner_b(j).wait_recv()
            self.go(self.outer_b(j, 0))
        for step in range(1, r.outer):
            for p in range(r.count):
                self.outer_a(step - 1, p).wait_recv()
                if step < r.outer - 1:
                    self.go(self.outer_a(step, p))
                for j in range(1, r.inner):
                    self.go(self.inner_a(j, step, p))
            for j in range(r.inner):
                self.outer_b(j, step - 1).wait_recv()
                if step < r.outer - 1:
                    self.go(self.outer_b(j, step))

    def finish(self):
        r = self.r
        for step in range(r.outer):
            for p in range(r.count):
                for j in range(1, r.inner):
                    self.inner_a(j, step, p).wait_recv()
        for copy in self.sent:
            copy.wait_send()


class Reduce:
    def __init__(self, ring, src, scratch):
        self.r, self.src = ring, src
        (self.ia, self.oa, self.ob, self.ib, self.s_ia, self.s_oa, self.s_ob, self.s_ib,
         self.r_ia, self.r_oa, self.r_ob, self.r_ib) = scratch
        self.sent = []

    def part(self, shard, row, rows):
        return self.src.at[pl.ds(pl.multiple_of(shard * self.r.rows + row, 8), rows), :]

    def inner_a(self, j, step, p):
        r = self.r
        row, rows = r.pieces[p]
        return remote(self.part(r.shard(step + 1, -j), row, rows), self.ia.at[j - 1, step, pl.ds(row, rows), :],
                      self.s_ia.at[j - 1, step, p], self.r_ia.at[j - 1, step, p], r.shard(0, -j))

    def outer_a(self, step, p):
        r = self.r
        row, rows = r.pieces[p]
        src = self.ia.at[0, 0, pl.ds(row, rows), :] if step == 0 else self.oa.at[step - 1, pl.ds(row, rows), :]
        return remote(src, self.oa.at[step, pl.ds(row, rows), :], self.s_oa.at[step, p], self.r_oa.at[step, p], r.shard(-1))

    def outer_b(self, j, step):
        r = self.r
        src = self.part(r.shard(1, j), r.rows_a, r.rows_b) if step == 0 else self.ob.at[j, step - 1]
        return remote(src, self.ob.at[j, step], self.s_ob.at[j, step], self.r_ob.at[j, step], r.shard(-1))

    def inner_b(self, j):
        r = self.r
        return remote(self.ob.at[j, r.outer - 2], self.ib.at[j - 1], self.s_ib.at[j - 1], self.r_ib.at[j - 1], r.shard(0, j))

    def go(self, copy):
        copy.start()
        self.sent.append(copy)

    def start(self):
        r = self.r
        for j in range(r.inner):
            self.go(self.outer_b(j, 0))
        for step in range(r.outer):
            for p in range(r.count):
                for j in range(1, r.inner):
                    self.go(self.inner_a(j, step, p))

    def run(self, done_a, done_b):
        r = self.r
        for step in range(r.outer):
            last = step == r.outer - 1
            for p in range(r.count):
                row, rows = r.pieces[p]
                for j in range(1, r.inner):
                    self.inner_a(j, step, p).wait_recv()
                total = self.part(r.shard(step + 1), row, rows)[...]
                for j in range(1, r.inner):
                    total = total + self.ia[j - 1, step, pl.ds(row, rows), :]
                if step == 0:
                    self.ia[0, 0, pl.ds(row, rows), :] = total
                else:
                    self.outer_a(step - 1, p).wait_recv()
                    total = total + self.oa[step - 1, pl.ds(row, rows), :]
                    if not last:
                        self.oa[step - 1, pl.ds(row, rows), :] = total
                if last:
                    done_a(p, total)
                else:
                    self.go(self.outer_a(step, p))
            if step >= 1:
                for j in range(r.inner):
                    self.outer_b(j, step - 1).wait_recv()
                    total = self.ob[j, step - 1] + self.part(r.shard(step + 1, j), r.rows_a, r.rows_b)[...]
                    self.ob[j, step - 1] = total
                    if not last:
                        self.go(self.outer_b(j, step))
                    elif j > 0:
                        self.go(self.inner_b(j))
        total = self.ob[0, r.outer - 2]
        for j in range(1, r.inner):
            self.inner_b(j).wait_recv()
            total = total + self.ib[j - 1]
        done_b(total)

    def finish(self):
        for copy in self.sent:
            copy.wait_send()


def params(cid, vmem):
    return pltpu.CompilerParams(collective_id=cid, has_side_effects=True, vmem_limit_bytes=vmem)


def gather_columns(x, n, cid):
    rows, lanes = x.shape
    ring = Ring(n, rows)
    flat = lanes % 128 == 0

    def kernel(x_ref, out, *sems):
        ring.place()
        ring.barrier()

        def view(shard, row, count):
            if flat:
                return out.at[pl.ds(row, count), pl.ds(pl.multiple_of(shard * lanes, 128), lanes)]
            return out.at[shard, pl.ds(row, count), :]

        gather = Gather(ring, view, lambda row, count: x_ref.at[pl.ds(row, count), :], sems[:8])
        keep = pltpu.make_async_copy(x_ref, view(ring.shard(0), 0, rows), sems[8])
        gather.start_b()
        for p in range(ring.count):
            gather.start_a(p)
        keep.start()
        gather.middle()
        gather.finish()
        keep.wait()

    shape = (rows, n * lanes) if flat else (n, rows, lanes)
    out = pl.pallas_call(
        kernel,
        out_shape=jax.ShapeDtypeStruct(shape, F32),
        in_specs=[pl.BlockSpec(memory_space=pltpu.VMEM)],
        out_specs=pl.BlockSpec(memory_space=pl.ANY),
        scratch_shapes=ring.gather_semaphores() + [pltpu.SemaphoreType.DMA],
        compiler_params=params(cid, 16 << 20),
        name="gather_columns",
    )(x)
    return out if flat else out.transpose(1, 0, 2).reshape(rows, n * lanes)


def reduce_rows(x, n, cid):
    total, width = x.shape
    rows = total // n
    ring = Ring(n, rows)

    def kernel(x_ref, out, *scratch):
        ring.place()
        ring.barrier()
        reduce = Reduce(ring, x_ref, scratch)
        reduce.start()

        def done_a(p, value):
            row, count = ring.pieces[p]
            out[pl.ds(row, count), :] = value

        def done_b(value):
            out[pl.ds(ring.rows_a, ring.rows_b), :] = value

        reduce.run(done_a, done_b)
        reduce.finish()

    return pl.pallas_call(
        kernel,
        out_shape=jax.ShapeDtypeStruct((rows, width), F32),
        in_specs=[pl.BlockSpec(memory_space=pltpu.VMEM)],
        out_specs=pl.BlockSpec(memory_space=pltpu.VMEM),
        scratch_shapes=ring.reduce_scratch(width),
        compiler_params=params(cid, 40 << 20),
        name="reduce_rows",
    )(x)


def reduce_norm_gather(part, values, upper, gain, n, cid):
    total, width = part.shape
    rows = total // n
    ring = Ring(n, rows)
    n_red = len(ring.reduce_scratch(width))

    def kernel(part_ref, val_ref, up_ref, gain_ref, out, gain_out, piece, keep_sem, *scratch):
        ring.place()
        ring.barrier()
        reduce = Reduce(ring, part_ref, scratch[:n_red])
        gather = Gather(ring, lambda shard, row, count: out.at[pl.ds(pl.multiple_of(shard * rows + row, 8), count), :],
                        lambda row, count: piece.at[pl.ds(row, count), :], scratch[n_red:])
        gain_out[...] = jnp.zeros_like(gain_out)
        reduce.start()

        def back(row, count, grad):
            x = val_ref[pl.ds(row, count), :]
            rr = lax.rsqrt(jnp.mean(x * x, axis=1, keepdims=True) + EPSILON)
            scaled = gain_ref[...] * grad
            inner = jnp.mean(scaled * x, axis=1, keepdims=True)
            piece[pl.ds(row, count), :] = up_ref[pl.ds(row, count), :] + rr * scaled - x * (rr * rr * rr * inner)
            gain_out[...] += jnp.sum(grad * x * rr, axis=0, keepdims=True)

        def done_a(p, value):
            row, count = ring.pieces[p]
            back(row, count, value)
            gather.start_a(p)

        def done_b(value):
            back(ring.rows_a, ring.rows_b, value)
            gather.start_b()

        reduce.run(done_a, done_b)
        keep = pltpu.make_async_copy(piece, out.at[pl.ds(pl.multiple_of(ring.shard(0) * rows, 8), rows), :], keep_sem)
        keep.start()
        gather.middle()
        gather.finish()
        reduce.finish()
        keep.wait()

    vm = pl.BlockSpec(memory_space=pltpu.VMEM)
    out, gain_part = pl.pallas_call(
        kernel,
        out_shape=(jax.ShapeDtypeStruct((total, width), F32), jax.ShapeDtypeStruct((1, width), F32)),
        in_specs=[vm] * 4,
        out_specs=(pl.BlockSpec(memory_space=pl.ANY), vm),
        scratch_shapes=[pltpu.VMEM((rows, width), F32), pltpu.SemaphoreType.DMA]
        + ring.reduce_scratch(width) + ring.gather_semaphores(),
        compiler_params=params(cid, 48 << 20),
        name="reduce_norm_gather",
    )(part, values, upper, gain.reshape(1, width))
    return out, gain_part[0]


EPSILON = 1e-06
PRECISE = lax.Precision.HIGHEST


def rms_norm(values, gain):
    return values * lax.rsqrt(jnp.mean(values * values, axis=-1, keepdims=True) + EPSILON) * gain


def rms_back(values, gain, grad):
    rr = lax.rsqrt(jnp.mean(values * values, axis=-1, keepdims=True) + EPSILON)
    scaled = gain * grad
    back = rr * scaled - values * (rr * rr * rr) * jnp.mean(scaled * values, axis=-1, keepdims=True)
    return back, jnp.sum(grad * values * rr, axis=0)


def make_shards(mesh):
    n_tensor = mesh.shape["tensor"]
    n_dp = mesh.shape["dp"]

    def shards(tokens, cotangent, gain_attn, gain_moe, w_qkv, w_out, rel_bias, w_router, w_in, w_down,
               segment_ids, routes, order):
        tok, width = tokens.shape
        lanes = w_qkv.shape[2]
        share_rows = tok // n_tensor
        row0 = lax.axis_index("tensor") * share_rows

        def halve(a):
            bit = 1
            while bit < n_dp:
                pairs = a.reshape((a.shape[0] // 2, 2) + a.shape[1:])
                side = lax.axis_index("dp") // bit % 2
                keep = lax.dynamic_index_in_dim(pairs, side, 1, keepdims=False)
                give = lax.dynamic_index_in_dim(pairs, 1 - side, 1, keepdims=False)
                a = keep + lax.ppermute(give, "dp", [(d, d ^ bit) for d in range(n_dp)])
                bit *= 2
            return a[0]

        def own(a):
            return lax.dynamic_slice_in_dim(a, row0, share_rows, 0)

        one = (order[0, 0] >= 0).astype(F32)
        w_out_all = lax.all_gather(w_out.astype(F32), "tensor", axis=0, tiled=True) * one
        x = tokens.astype(F32)
        attn_input = rms_norm(x, gain_attn).astype(BF16)
        qkv = jnp.dot(attn_input, w_qkv.reshape(width, 3 * lanes), preferred_element_type=F32).astype(BF16)
        q, k, v = (qkv[:, i * lanes:(i + 1) * lanes] for i in range(3))
        rb = rel_bias.astype(F32).reshape(-1)
        attended = attention_fwd(q, k, v.T, segment_ids, rb)
        tgt = slot_targets(routes, order[0])
        y = dispatch(tgt, cotangent)

        attended_all = gather_columns(attended, n_tensor, 0)
        hidden_one = x + jnp.dot(attended_all, w_out_all, preferred_element_type=F32)
        moe_input = rms_norm(hidden_one, gain_moe).astype(BF16)
        logits = jnp.dot(moe_input, w_router, preferred_element_type=F32)
        picked = (routes[:, :, None] == jnp.arange(EXPERTS, dtype=jnp.int32)[None, None, :]).astype(F32)

        def route(logit_rows, picked_rows):
            soft = jax.nn.softmax(logit_rows, axis=-1)
            chosen = jnp.sum(soft[:, None, :] * picked_rows, axis=-1)
            return soft, chosen, jnp.sum(chosen, axis=-1, keepdims=True)

        soft, chosen, both = route(logits, picked)
        pair_share = chosen / both
        xs, slot_share = dispatch(tgt, moe_input, jnp.broadcast_to(pair_share.T.reshape(-1, 1), (2 * tok, LN)))
        act, gate_up_grad, moe_in_part, share_part = k1(tgt, xs, y, slot_share, w_in, w_down, tok)
        w_in_local, w_down_local, moe_part = k2(tgt, xs, y, slot_share, act, gate_up_grad, w_down, tok, n_dp)

        share_grad = lax.psum_scatter(share_part[:, :, 0].T, "tensor", scatter_dimension=0, tiled=True)
        moe_in_sum = reduce_rows(moe_in_part, n_tensor, 1)
        result = hidden_one + lax.psum(moe_part, "tensor")

        soft_s, chosen_s, both_s, picked_s = own(soft), own(chosen), own(both), own(picked)
        chosen_grad = share_grad / both_s - jnp.sum(share_grad * chosen_s, axis=-1, keepdims=True) / (both_s * both_s)
        prob_grad = jnp.sum(chosen_grad[:, :, None] * picked_s, axis=1)
        logits_grad = soft_s * (prob_grad - jnp.sum(soft_s * prob_grad, axis=-1, keepdims=True))
        moe_input_s = own(moe_input)
        router_part = jnp.dot(moe_input_s.astype(F32).T, logits_grad, precision=PRECISE)
        moe_input_grad = moe_in_sum + jnp.dot(logits_grad, w_router.astype(F32).T, precision=PRECISE)
        norm_grad, gain_moe_part = rms_back(own(hidden_one), gain_moe, moe_input_grad)
        hidden_grad = own(cotangent).astype(F32) + norm_grad
        proj_grad = hidden_grad.astype(BF16)
        att_grad_s = lax.dot_general(proj_grad, w_out_all.astype(BF16), (((1,), (1,)), ((), ())), preferred_element_type=F32)
        att_grad_s = att_grad_s.astype(BF16).astype(F32)
        pieces = att_grad_s.reshape(share_rows, n_tensor, lanes).transpose(1, 0, 2)
        attended_grad = lax.all_to_all(pieces, "tensor", 0, 0, tiled=False).reshape(tok, lanes)
        w_out_part = lax.dot_general(own(attended_all).astype(BF16), proj_grad, (((0,), (0,)), ((), ())), preferred_element_type=F32)

        dq, dk, dv, bias_part = attention_bwd(q, k, v, k.T, attended_grad, segment_ids, rb)
        qkv_grad = jnp.concatenate([dq, dk, dv], axis=1)
        attn_in_part = lax.dot_general(qkv_grad, w_qkv.reshape(width, 3 * lanes), (((1,), (1,)), ((), ())), preferred_element_type=F32)
        w_qkv_part = lax.dot_general(attn_input, qkv_grad, (((0,), (0,)), ((), ())), preferred_element_type=F32)

        input_grad, gain_attn_part = reduce_norm_gather(attn_in_part, own(x), hidden_grad, gain_attn, n_tensor, 2)

        def over_dp(a, dim):
            return lax.psum_scatter(a, "dp", scatter_dimension=dim, tiled=True)

        w_in_grad = halve(w_in_local)
        w_down_grad = halve(w_down_local)
        w_qkv_grad = over_dp(w_qkv_part, 0).reshape(width // n_dp, 3, lanes)
        w_out_grad = lax.psum_scatter(over_dp(w_out_part, 1), "tensor", scatter_dimension=0, tiled=True)
        small = jnp.concatenate([gain_attn_part[:, None], gain_moe_part[:, None], router_part], axis=1)
        small = over_dp(lax.psum(small, "tensor"), 0)
        rel_bias_grad = over_dp(bias_part[:, :, 0].T, 0)
        return (result, input_grad, small[:, 0], small[:, 1], w_qkv_grad, w_out_grad, rel_bias_grad,
                small[:, 2:], w_in_grad, w_down_grad)

    return shards


def solution(mesh):
    return jax.shard_map(
        make_shards(mesh),
        mesh=mesh,
        in_specs=(
            P("dp", None),
            P("dp", None),
            P(),
            P(),
            P(None, None, "tensor"),
            P("tensor", None),
            P(None, "tensor"),
            P(),
            P(None, None, None, "tensor"),
            P(None, "tensor", None),
            P("dp", None),
            P("dp", None),
            P("dp", None),
        ),
        out_specs=(
            P("dp", None),
            P("dp", None),
            P("dp"),
            P("dp"),
            P("dp", None, "tensor"),
            P("tensor", "dp"),
            P("dp", "tensor"),
            P("dp", None),
            P(None, None, "dp", "tensor"),
            P(None, "tensor", "dp"),
        ),
        check_vma=False,
    )
```

time: 2010 us -> 1170 us (0.58)
  waiting for transfers between devices: 1070 us -> 141 us
  Pallas kernels: 0 us -> 558 us
  matrix products: 330 us -> 42.1 us
  local copies, waits for them, and re-layouts: 390 us -> 122 us
  blocking collectives: 43.4 us -> 221 us
  other arithmetic: 145 us -> 56.7 us
    psum x3 -> x1, waiting for transfers between devices: 773 us -> 51.7 us  [shards(): result = hidden_one + lax.psum(moe_part, 'tensor')]
    pallas_call x0 -> x9, Pallas kernels: none -> 558 us  [the longest x1 173 us: reduce_norm_gather(): pl.pallas_call(kernel, out_shape=(jax.ShapeDtypeStruct((total, width), F3...]
    dot_general x55 -> x10, matrix products: 330 us -> 42.1 us  [the longest x1 10.8 us: shards(): jnp.dot(attended_all, w_out_all, preferred_element_type=F32)]
    reduce_scatter x5 -> x4, waiting for transfers between devices: 299 us -> 43.7 us  [the longest x1 43.7 us: shards(): lax.psum_scatter(over_dp(w_out_part, 1), 'tensor', scatter_dimension=0, t...]
    gather x9 -> x0, local copies, waits for them, and re-layouts: 228 us -> none  [the longest x2 48.8 us: shards(): pair_rows = out_rows[token_target]]
    unnamed x1, blocking collectives: 6.65 us -> 181 us
    reduce_sum x14 -> x8, other arithmetic: 69.5 us -> 2.89 us  [the longest x1 2.43 us: slot_targets(): jnp.sum(jnp.where(order[:, None] == pos[None, :], pos[:, None], 0), axis=0)]
    dynamic_slice x4, local copies, waits for them, and re-layouts: 0.04 us -> 44.4 us  [the longest x2 30.8 us: halve(): keep = lax.dynamic_index_in_dim(pairs, side, 1, keepdims=False)]
  transfers between devices with their start and end apart: 8 -> 12, of which waited for: 7 -> 4; matrix products, arithmetic and copies ran while one was open for 13% -> 14% of each run, Pallas kernels for 0% -> 42%
where the time goes in v1:
time: 1170 us; the launch traced here: 1160 us
  Pallas kernels  558 us (48%)
  blocking collectives  221 us (19%)
  waiting for transfers between devices  141 us (12%)
  local copies, waits for them, and re-layouts  122 us (10%)
  other arithmetic  56.7 us (5%)
  matrix products  42.1 us (4%)
  between operations  16.3 us (1%)
    unnamed x1, blocking collectives  181 us
    pallas_call x1, Pallas kernels, reduce_norm_gather(): pl.pallas_call(kernel, out_shape=(jax.ShapeDtypeStruct((total, width), F3...  173 us
    pallas_call x1, Pallas kernels, gather_columns(): pl.pallas_call(kernel, out_shape=jax.ShapeDtypeStruct(shape, F32), in_spe...  108 us
    pallas_call x1, Pallas kernels, reduce_rows(): pl.pallas_call(kernel, out_shape=jax.ShapeDtypeStruct((rows, width), F32)...  92.6 us
    psum x1, waiting for transfers between devices, shards(): result = hidden_one + lax.psum(moe_part, 'tensor')  51.7 us
    unnamed x46, local copies, waits for them, and re-layouts  49.9 us
    pallas_call x1, Pallas kernels, k1(): pl.pallas_call(functools.partial(k1_kernel, tok, sub, count), grid_spec=p...  46.8 us
    pallas_call x2, Pallas kernels, dispatch(): pl.pallas_call(functools.partial(dispatch_kernel, tok, sub, step_slots, w...  44.7 us
  transfers between devices with their start and end apart: 12, of which 4 were waited for; matrix products, arithmetic and copies ran while one was open for 14% of the time, Pallas kernels for 42%

profile of v1, /device:TPU:0, one launch (start us, length us, event | category | flops | bytes accessed | tf_op | source)
XLA Modules:
  0.0 1163.8 jit_solution(10562685239595549597)
XLA Ops:
  26.7 4.2 convolution_convert_fusion
  34.1 19.6 %attn_fwd.1.x_ref = f32[2048,128]{1,0:T(8,128)} custom-call(f32[64]{0:T(128)} %reshape.143.rb_ref, bf16[2048,128]{1,0:T(8,128)(2,1)} %copy.73.q_ref, bf16[2048,128]{1,0:T(8,128)(2,1)} %copy.74.k_ref, bf16[128,2048]{1,0:T(8,128)(2,1)} %get-tuple-element.89.vt_ref, s32[2,1,1024]{2,1,0:T(1,128)} %reshape.134.segr_ref, s32[2048,1]{1,0:T(8,128)} %bitcast.90), custom_call_target="tpu_custom_call" | custom-call | flops 1073741824 | bytes 2621440 | tf_op jit(solution)/shard_map/attn_fwd/pallas_call | solution.py:177
  55.0 107.7 %gather_columns.1 = f32[2048,1024]{1,0:T(8,128)S(1)} custom-call(f32[2048,128]{1,0:T(8,128)S(1)} %copy-done.4), custom_call_target="tpu_custom_call" | custom-call | tf_op jit(solution)/shard_map/gather_columns/pallas_call | solution.py:676
  166.1 16.2 %copy.77.win = bf16[8,2,1024,352]{3,2,1,0:T(8,128)(2,1)} copy(bf16[8,2,1024,352]{2,3,1,0:T(8,128)(2,1)} %param.21) | data formatting | bytes 23068672 | tf_op args[8]
  182.3 20.9 %dispatch.3.y = bf16[4608,1024]{1,0:T(8,128)(2,1)} custom-call(s32[4096]{0:T(1024)} %bitcast.92, bf16[2048,1024]{1,0:T(8,128)(2,1)} %src.1), custom_call_target="tpu_custom_call" | custom-call | bytes 17825792 | tf_op jit(solution)/shard_map/dispatch/pallas_call | solution.py:280
  203.2 10.8 multiply_reduce_fusion
  220.7 23.8 %dispatch.2 = (bf16[4608,1024]{1,0:T(8,128)(2,1)}, f32[4608,128]{1,0:T(8,128)}) custom-call(s32[4096]{0:T(1024)} %bitcast.93, bf16[2048,1024]{1,0:T(8,128)(2,1)} %copy-done.6, f32[4096,128]{1,0:T(8,128)} %broadcast_in_dim.28.rest_0_), custom_call_target="tpu_custom_call" | custom-call | bytes 17825792 | tf_op jit(solution)/shard_map/dispatch/pallas_call | solution.py:280
  244.5 46.8 %experts_back.1 = (bf16[8,576,352]{2,1,0:T(8,128)(2,1)}, bf16[8,2,576,352]{3,2,1,0:T(8,128)(2,1)}, f32[2048,1024]{1,0:T(8,128)}, f32[2,2048,128]{2,1,0:T(8,128)}) custom-call(s32[4096]{0:T(1024)} %bitcast.94, bf16[4608,1024]{1,0:T(8,128)(2,1)} %get-tuple-element.25.x, bf16[4608,1024]{1,0:T(8,128)(2,1)} %dispatch.3.y, f32[4608,128]{1,0:T(8,128)} %get-tuple-element.26.sh, ...), custom_call_target="tpu_custom_call" | custom-call | flops 16609443840 | bytes 62914560 | tf_op jit(solution)/shard_map/experts_back/pallas_call | solution.py:348
  298.3 92.6 %reduce_rows.1 = f32[256,1024]{1,0:T(8,128)S(1)} custom-call(f32[2048,1024]{1,0:T(8,128)S(1)} %copy-done.3), custom_call_target="tpu_custom_call" | custom-call | tf_op jit(solution)/shard_map/reduce_rows/pallas_call | solution.py:709
  390.9 28.3 %reduce-scatter.17.cloned.1.call-done = f32[256,2]{1,0:T(8,128)} async-done(((f32[2048,2]{1,0:T(8,128)}), f32[256,2]{1,0:T(8,128)}) %reduce-scatter.17.cloned.1.call-update) | async-done | bytes 2064
  424.2 4.0 fusion.25
  428.3 44.1 %experts_weights.1 = (f32[4,8,2,256,352]{4,3,2,1,0:T(8,128)}, f32[4,8,352,256]{3,2,1,0:T(8,128)}, f32[2048,1024]{1,0:T(8,128)}) custom-call(s32[4096]{0:T(1024)} %bitcast.95, bf16[4608,1024]{1,0:T(8,128)(2,1)} %get-tuple-element.25.x, bf16[4608,1024]{1,0:T(8,128)(2,1)} %dispatch.3.y, f32[4608,128]{1,0:T(8,128)} %get-tuple-element.26.sh, ...), custom_call_target="tpu_custom_call" | custom-call | flops 13287555072 | bytes 83886080 | tf_op jit(solution)/shard_map/experts_weights/pallas_call | solution.py:399
  472.3 18.6 %constant_dynamic-slice_fusion.2 = (f32[2,1,8,2,256,352]{5,4,3,2,1,0:T(8,128)}, f32[2,1,8,2,256,352]{5,4,3,2,1,0:T(8,128)}) fusion(f32[2,2,8,2,256,352]{5,4,3,2,1,0:T(8,128)} %bitcast.83, s32[]{:T(128)S(6)} %select_n.65, s32[]{:T(128)S(6)} %select_n.66), kind=kLoop, calls=%fused_computation.71 | loop fusion | bytes 46137352 | tf_op jit(solution)/shard_map/jit(dynamic_index_in_dim)/dynamic_slice | solution.py:805
  490.9 12.3 %copy.85 = f32[2,1,8,2,256,352]{4,5,3,2,0,1:T(8,128)} copy(f32[2,1,8,2,256,352]{5,4,3,2,1,0:T(8,128)} %get-tuple-element.87) | data formatting | bytes 23068672 | tf_op jit(solution)/shard_map/jit(dynamic_index_in_dim)/dynamic_slice | solution.py:806
  507.2 4.2 all-to-all-start
  511.7 6.5 convert_element_type.57
  521.9 16.3 %all-to-all-done = f32[8,256,128]{2,1,0:T(8,128)} async-done(((f32[8,256,128]{2,1,0:T(8,128)}), f32[8,256,128]{2,1,0:T(8,128)}, u32[]{:S(2)}, u32[]{:S(2)}) %all-to-all-start) | async-done | bytes 1048608 | tf_op jit(solution)/shard_map/all_to_all | solution.py:859
  538.1 29.9 %attn_bwd.1 = (bf16[2048,128]{1,0:T(8,128)(2,1)}, bf16[2048,128]{1,0:T(8,128)(2,1)}, bf16[2048,128]{1,0:T(8,128)(2,1)}, f32[2,32,128]{2,1,0:T(8,128)}) custom-call(f32[64]{0:T(128)} %reshape.143.rb_ref, bf16[2048,128]{1,0:T(8,128)(2,1)} %copy.73.q_ref, bf16[2048,128]{1,0:T(8,128)(2,1)} %copy.74.k_ref, bf16[2048,128]{1,0:T(8,128)(2,1)} %copy.81.v_ref, ...), custom_call_target="tpu_custom_call" | custom-call | flops 2684354560 | bytes 5242880 | tf_op jit(solution)/shard_map/attn_bwd/pallas_call | solution.py:198
  571.5 5.7 fusion.44.part_ref
  577.2 173.2 %reduce_norm_gather.1 = (f32[2048,1024]{1,0:T(8,128)}, f32[1,1024]{1,0:T(1,128)S(1)}) custom-call(f32[2048,1024]{1,0:T(8,128)} %fusion.44.part_ref, f32[256,1024]{1,0:T(8,128)S(1)} %constant_dynamic-slice_fusion.3.val_ref, f32[256,1024]{1,0:T(8,128)S(1)} %subtract_add_fusion.up_ref, f32[1,1024]{1,0:T(1,128)S(1)} %bitcast.81), custom_call_target="tpu_custom_call" | custom-call | tf_op jit(solution)/shard_map/reduce_norm_gather/pallas_call | solution.py:761
  751.4 6.3 fusion.21
  758.3 5.7 dynamic-slice_bitcast_fusion
  764.0 12.3 %copy.84 = f32[2,1,8,2,256,352]{4,5,3,2,0,1:T(8,128)} copy(f32[2,1,8,2,256,352]{5,4,3,2,1,0:T(8,128)} %get-tuple-element.86) | data formatting | bytes 23068672 | tf_op jit(solution)/shard_map/jit(dynamic_index_in_dim)/dynamic_slice | solution.py:805
  776.3 9.3 bitcast_add_fusion
  793.3 5.1 bitcast_add_fusion.1
  804.5 180.9 %all-reduce.1 = f32[32,2]{0,1:T(2,128)S(1)} all-reduce(f32[32,2]{0,1:T(2,128)S(1)} %bitcast.101), channel_id=7, replica_groups=mesh['dp'=4,'tensor'=8] {'dp'}, use_global_device_ids=true, to_apply=%region_22.23.clone | all-reduce | flops 64 | bytes 512
  986.1 39.6 %psum.16 = f32[256,10]{0,1:T(8,128)S(1)} all-reduce(f32[256,10]{0,1:T(8,128)} %reduce-scatter.15.cloned.1.call-done), channel_id=1, replica_groups=mesh['dp'=4,'tensor'=8] {'tensor'}, use_global_device_ids=true, to_apply=%region_17.18 | all-reduce | flops 2560 | bytes 20480 | tf_op jit(solution)/shard_map/psum | solution.py:877
  1029.0 51.7 %all-reduce.4.cloned.1.call-done = f32[2048,1024]{1,0:T(8,128)} async-done(((f32[2048,1024]{1,0:T(8,128)}), f32[2048,1024]{1,0:T(8,128)}) %all-reduce.4.cloned.1.call-update) | async-done | bytes 8388624 | tf_op jit(solution)/shard_map/psum | solution.py:844
  1080.7 12.2 %add.133 = f32[2048,1024]{1,0:T(8,128)} add(f32[2048,1024]{1,0:T(8,128)} %copy-done.7, f32[2048,1024]{1,0:T(8,128)} %all-reduce.4.cloned.1.call-done) | non-fusion elementwise | flops 2097152 | bytes 25165824 | tf_op jit(solution)/shard_map/add | solution.py:844
  1096.6 7.8 add_bitcast_fusion
  1104.4 43.7 %reduce-scatter.13.cloned.1.call-done = f32[128,256]{1,0:T(8,128)} async-done(((f32[1024,256]{1,0:T(8,128)}), f32[128,256]{1,0:T(8,128)}) %reduce-scatter.13.cloned.1.call-update) | async-done | bytes 131088 | tf_op jit(solution)/shard_map/reduce_scatter | solution.py:875
  1148.1 8.5 copy.104
  (121 shorter events, 79.0 us)
Async XLA Ops:
  7.2 210.2 %copy-start = (bf16[1024,8]{0,1:T(8,128)(2,1)S(1)}, bf16[1024,8]{0,1:T(8,128)(2,1)}, u32[]{:S(2)}) copy-start(bf16[1024,8]{0,1:T(8,128)(2,1)} %param.20) | copy-start | bytes 49156
  7.2 14.1 %copy-start.12 = (s32[2048,2]{0,1:T(2,128)S(1)}, s32[2048,2]{0,1:T(2,128)}, u32[]{:S(2)}) copy-start(s32[2048,2]{0,1:T(2,128)} %param.24) | copy-start | bytes 49156
  7.2 14.8 %copy-start.11 = (bf16[1024,3,128]{2,0,1:T(8,128)(2,1)S(1)}, bf16[1024,3,128]{2,0,1:T(8,128)(2,1)}, u32[]{:S(2)}) copy-start(bf16[1024,3,128]{2,0,1:T(8,128)(2,1)} %param.17) | copy-start | bytes 2359300
  7.2 195.9 %all-gather.2.cloned.1.call-start = ((), (), s32[]{:S(2)}) async-start(), calls=%async_computation.6 | async-start | bytes 4718592 | tf_op jit(solution)/shard_map/all_gather | solution.py:815
  9.1 410.0 %reduce-scatter.17.cloned.1.call-start = ((), (), s32[]{:S(2)}) async-start(), calls=%async_computation.12 | async-start | bytes 1179648
  17.8 8.9 copy-start.5
  53.8 1.2 copy-start.4
  162.7 3.4 copy-start.2
  203.2 11.0 copy-start.13
  213.9 3.4 copy-start.7
  217.3 3.4 copy-start.6
  294.9 508.3 %reduce-scatter.11.cloned.1.call-start = ((), (), s32[]{:S(2)}) async-start(), calls=%async_computation.9 | async-start | bytes 5242880 | tf_op jit(solution)/shard_map/reduce_scatter | solution.py:870
  294.9 3.4 copy-start.3
  503.2 273.1 %collective-permute-start = (f32[2,8,2,256,352]{3,4,2,1,0:T(8,128)}, f32[2,8,2,256,352]{3,4,2,1,0:T(8,128)}, u32[]{:S(2)}, u32[]{:S(2)}) collective-permute-start(f32[2,8,2,256,352]{3,4,2,1,0:T(8,128)} %bitcast.86), channel_id=1, source_target_pairs={{0,8},{8,0},{16,24},{24,16},{1,9},{9,1},{17,25},{25,17},{2,10},{10... | collective-permute-start | bytes 34603016 | tf_op jit(solution)/shard_map/ppermute | solution.py:807
  507.2 31.0 %all-to-all-start = ((f32[8,256,128]{2,1,0:T(8,128)}), f32[8,256,128]{2,1,0:T(8,128)}, u32[]{:S(2)}, u32[]{:S(2)}) async-start(f32[8,256,128]{2,1,0:T(8,128)} %bitcast.80), calls=%async_computation | async-start | bytes 2097152 | tf_op jit(solution)/shard_map/all_to_all | solution.py:859
  511.4 474.7 %reduce-scatter.15.cloned.1.call-start = ((), (), s32[]{:S(2)}) async-start(), calls=%async_computation.11 | async-start | bytes 81920 | tf_op jit(solution)/shard_map/reduce_scatter | solution.py:870
  571.5 5.7 copy-start.10
  751.0 275.8 %reduce-scatter.9.cloned.1.call-start = ((), (), s32[]{:S(2)}) async-start(), calls=%async_computation.8 | async-start | bytes 1966080 | tf_op jit(solution)/shard_map/reduce_scatter | solution.py:870
  757.7 323.0 %all-reduce.4.cloned.1.call-start = ((), (), s32[]{:S(2)}) async-start(), calls=%async_computation.7 | async-start | bytes 16777216 | tf_op jit(solution)/shard_map/psum | solution.py:844
  758.2 389.8 %reduce-scatter.13.cloned.1.call-start = ((), (), s32[]{:S(2)}) async-start(), calls=%async_computation.10 | async-start | bytes 1179648 | tf_op jit(solution)/shard_map/reduce_scatter | solution.py:875
  764.0 29.3 %collective-permute-start.2 = (f32[2,8,352,256]{3,2,1,0:T(8,128)}, f32[2,8,352,256]{3,2,1,0:T(8,128)}, u32[]{:S(2)}, u32[]{:S(2)}) collective-permute-start(f32[2,8,352,256]{3,2,1,0:T(8,128)} %dynamic-slice_bitcast_fusion), channel_id=1, source_target_pairs={{0,8},{8,0},{16,24},{24,16},{1,9},{9,1},{17,25},{25,17},{2,10},{10... | collective-permute-start | bytes 17301512 | tf_op jit(solution)/shard_map/ppermute | solution.py:807
  785.6 6.1 copy-start.8
  791.7 304.9 %collective-permute-start.1 = (f32[1,8,2,256,352]{3,4,2,1,0:T(8,128)}, f32[1,8,2,256,352]{3,4,2,1,0:T(8,128)}, u32[]{:S(2)}, u32[]{:S(2)}) collective-permute-start(f32[1,8,2,256,352]{3,4,2,1,0:T(8,128)} %constant_dynamic-slice_fusion), channel_id=1, source_target_pairs={{0,16},{8,24},{16,0},{24,8},{1,17},{9,25},{17,1},{25,9},{2,18},{10... | collective-permute-start | bytes 17301512 | tf_op jit(solution)/shard_map/ppermute | solution.py:807
  798.5 2.5 copy-start.9
  801.0 2.2 copy-start.15
  801.0 3.4 copy-start.14
  802.7 290.1 %collective-permute-start.3 = (f32[1,8,352,256]{3,2,1,0:T(8,128)}, f32[1,8,352,256]{3,2,1,0:T(8,128)S(1)}, u32[]{:S(2)}, u32[]{:S(2)}) collective-permute-start(f32[1,8,352,256]{3,2,1,0:T(8,128)} %constant_dynamic-slice_fusion.5), channel_id=1, source_target_pairs={{0,16},{8,24},{16,0},{24,8},{1,17},{9,25},{17,1},{25,9},{2,18},{10... | collective-permute-start | bytes 8650760 | tf_op jit(solution)/shard_map/ppermute | solution.py:807
  1148.1 8.5 copy-start.1
Sparse Core Ops, SparseCore 0:
  10.7 100.8 all-gather.1
  295.0 124.1 reduce-scatter.16
  428.4 43.3 reduce-scatter.10
  751.2 18.1 reduce-scatter.14
  771.8 31.7 reduce-scatter.8
  807.9 272.6 all-reduce.3
  1084.6 63.3 reduce-scatter.12

commit v2 on v1

v2 whole, which is shorter than its diff:
```python
import functools
import math

import jax
import jax.numpy as jnp
import numpy as np
from jax import lax
from jax.experimental import pallas as pl
from jax.experimental.pallas import tpu as pltpu
from jax.sharding import PartitionSpec as P


F32 = jnp.float32
BF16 = jnp.bfloat16


def dot(a, b, ca, cb):
    return lax.dot_general(a, b, (((ca,), (cb,)), ((), ())), preferred_element_type=F32)


NB=32; MAXDIST=128; HD=64; NEG=-1000000000.0


def thresholds(bucket_count, reach):
    half_count = bucket_count // 2
    exact_count = half_count // 2
    listing = []
    for bucket_level in range(1, half_count):
        if bucket_level <= exact_count:
            listing.append(bucket_level)
        else:
            distance = exact_count
            while (exact_count + int(np.floor(np.log(distance / exact_count) / np.log(reach / exact_count) * (half_count - exact_count))) < bucket_level):
                distance += 1
            listing.append(distance)
    return listing


THRESH = thresholds(NB, MAXDIST)
HALF = NB // 2
CH = 128


def distance(row0, rows, cols, origin):
    r = lax.broadcasted_iota(jnp.int32, (rows, cols), 0)
    c = lax.broadcasted_iota(jnp.int32, (rows, cols), 1)
    return r + (row0 - origin) - c


def build_bias(rb_ref, bias, heads, length, block):
    total = 2 * length - block
    origin = length - block
    low_end = (origin - THRESH[-1] + 1) // CH * CH
    high_start = -(-(origin + block - 1 + THRESH[-1]) // CH) * CH
    for h in range(heads):
        bias[h, 0:low_end, :] = jnp.full((low_end, block), rb_ref[(HALF - 1) * heads + h], F32)
        bias[h, high_start:total, :] = jnp.full((total - high_start, block), rb_ref[(NB - 1) * heads + h], F32)

        def chunk(i, carry):
            row0 = pl.multiple_of(low_end + i * CH, CH)
            d = distance(row0, CH, block, origin)
            mag = jnp.abs(d)
            back = jnp.full((CH, block), rb_ref[h], F32)
            ahead = jnp.full((CH, block), rb_ref[HALF * heads + h], F32)
            for level, t in enumerate(THRESH):
                far = mag >= t
                back = jnp.where(far, rb_ref[(level + 1) * heads + h], back)
                ahead = jnp.where(far, rb_ref[(HALF + level + 1) * heads + h], ahead)
            bias[h, pl.ds(row0, CH), :] = jnp.where(d > 0, ahead, back)
            return carry

        lax.fori_loop(0, (high_start - low_end) // CH, chunk, 0)


def fwd_kernel(heads, length, block, rb_ref, q_ref, k_ref, vt_ref, segr_ref, segc_ref, o_ref, bias):
    @pl.when(pl.program_id(0) == 0)
    def _():
        build_bias(rb_ref, bias, heads, length, block)

    lanes = heads * HD
    lane = lax.broadcasted_iota(jnp.int32, (block, lanes), 1) // HD

    def step(i, carry):
        q0 = pl.multiple_of(i * block, block)
        start = pl.multiple_of(length - block - q0, block)
        qb = q_ref[pl.ds(q0, block), :] * 0.125
        same = segc_ref[...] == segr_ref[0, :, pl.ds(q0, block)]
        pieces = []
        for h in range(heads):
            qm = jnp.where(lane == h, qb, jnp.zeros_like(qb)) if heads > 1 else qb
            s = dot(k_ref[...], qm, 1, 1) + bias[h, pl.ds(start, length), :]
            s = jnp.where(same, s, NEG)
            p = jnp.exp(s - jnp.max(s, axis=0, keepdims=True))
            total = jnp.sum(p, axis=0, keepdims=True)
            p = (p * (1.0 / total)).astype(BF16)
            pieces.append(dot(vt_ref[h * HD:(h + 1) * HD, :], p, 1, 0))
        o = jnp.concatenate(pieces, axis=0) if heads > 1 else pieces[0]
        o_ref[pl.ds(q0, block), :] = o.T.astype(BF16).astype(F32)
        return carry

    lax.fori_loop(0, length // block, step, 0)


def bwd_kernel(heads, length, block, rb_ref, q_ref, k_ref, v_ref, kt_ref, do_ref, segr_ref, segc_ref,
               dq_ref, dk_ref, dv_ref, db_ref, bias, dbias, dk, dv):
    step_id = pl.program_id(0)
    total_rows = 2 * length - block

    @pl.when(step_id == 0)
    def _():
        build_bias(rb_ref, bias, heads, length, block)
        dbias[...] = jnp.zeros_like(dbias)

    dk[...] = jnp.zeros_like(dk)
    dv[...] = jnp.zeros_like(dv)
    lanes = heads * HD
    lane = lax.broadcasted_iota(jnp.int32, (block, lanes), 1) // HD

    def step(i, carry):
        q0 = pl.multiple_of(i * block, block)
        start = pl.multiple_of(length - block - q0, block)
        qb = q_ref[pl.ds(q0, block), :] * 0.125
        dob = do_ref[pl.ds(q0, block), :].astype(BF16)
        same = segc_ref[...] == segr_ref[0, :, pl.ds(q0, block)]
        pieces = []
        for h in range(heads):
            qm = jnp.where(lane == h, qb, jnp.zeros_like(qb)) if heads > 1 else qb
            dom = jnp.where(lane == h, dob, jnp.zeros_like(dob)) if heads > 1 else dob
            s = dot(k_ref[...], qm, 1, 1) + bias[h, pl.ds(start, length), :]
            s = jnp.where(same, s, NEG)
            p = jnp.exp(s - jnp.max(s, axis=0, keepdims=True))
            p = p * (1.0 / jnp.sum(p, axis=0, keepdims=True))
            dp = dot(v_ref[...], dom, 1, 1)
            ds = (p * (dp - jnp.sum(p * dp, axis=0, keepdims=True))).astype(BF16)
            dbias[h, pl.ds(start, length), :] += ds.astype(F32)
            dk[...] += dot(ds, qm, 1, 0)
            dv[...] += dot(p.astype(BF16), dom, 1, 0)
            pieces.append(dot(kt_ref[h * HD:(h + 1) * HD, :], ds, 1, 0))
        dq = jnp.concatenate(pieces, axis=0) if heads > 1 else pieces[0]
        dq_ref[pl.ds(q0, block), :] = (dq * 0.125).T.astype(BF16)
        return carry

    lax.fori_loop(0, length // block, step, 0)
    dk_ref[...] = dk[...].astype(BF16)
    dv_ref[...] = dv[...].astype(BF16)

    @pl.when(step_id == pl.num_programs(0) - 1)
    def _():
        origin = length - block
        low_end = (origin - THRESH[-1] + 1) // CH * CH
        high_start = -(-(origin + block - 1 + THRESH[-1]) // CH) * CH

        def fold(x):
            return jnp.sum(x, axis=0, keepdims=True)

        for h in range(heads):
            def rows(lo, hi):
                def body(i, acc):
                    r0 = pl.multiple_of(lo + i * CH, CH)
                    return acc + fold(dbias[h, pl.ds(r0, CH), :])

                return lax.fori_loop(0, (hi - lo) // CH, body, jnp.zeros((1, block), F32))

            def chunk(i, sums):
                r0 = pl.multiple_of(low_end + i * CH, CH)
                g = dbias[h, pl.ds(r0, CH), :]
                d = distance(r0, CH, block, origin)
                mag = jnp.abs(d)
                gb = jnp.where(d > 0, 0.0, g)
                ga = jnp.where(d > 0, g, 0.0)
                out = [sums[0] + fold(gb), sums[HALF] + fold(ga)]
                tb, ta = [], []
                for t in THRESH:
                    far = mag >= t
                    tb.append(fold(jnp.where(far, gb, 0.0)))
                    ta.append(fold(jnp.where(far, ga, 0.0)))
                new = [out[0]] + [sums[1 + n] + tb[n] for n in range(HALF - 1)]
                new += [out[1]] + [sums[HALF + 1 + n] + ta[n] for n in range(HALF - 1)]
                return tuple(new)

            sums = lax.fori_loop(0, (high_start - low_end) // CH, chunk,
                                 tuple(jnp.zeros((1, block), F32) for _ in range(NB)))
            left, right = rows(0, low_end), rows(high_start, total_rows)
            for b in range(NB):
                val = sums[b]
                if b not in (HALF - 1, NB - 1):
                    val = val - sums[b + 1]
                else:
                    val = val + (left if b == HALF - 1 else right)
                db_ref[h, b:b + 1, :] = jnp.broadcast_to(jnp.sum(val, axis=1, keepdims=True), (1, 128))


def attention_fwd(q, k, vt, seg, rb, block=256):
    tok, lanes = q.shape
    seqs, length = seg.shape
    heads = lanes // HD
    full = pl.BlockSpec((length, lanes), lambda s: (s, 0))
    return pl.pallas_call(
        functools.partial(fwd_kernel, heads, length, block),
        grid=(seqs,),
        out_shape=jax.ShapeDtypeStruct((tok, lanes), F32),
        in_specs=[pl.BlockSpec(memory_space=pltpu.SMEM), full, full,
                  pl.BlockSpec((lanes, length), lambda s: (0, s)),
                  pl.BlockSpec((1, 1, length), lambda s: (s, 0, 0)),
                  pl.BlockSpec((length, 1), lambda s: (s, 0))],
        out_specs=full,
        scratch_shapes=[pltpu.VMEM((heads, 2 * length - block, block), F32)],
        compiler_params=pltpu.CompilerParams(vmem_limit_bytes=56 << 20),
        cost_estimate=pl.CostEstimate(flops=4 * tok * length * lanes, bytes_accessed=tok * lanes * 10, transcendentals=tok * length * heads),
        name="attn_fwd",
    )(rb, q, k, vt, seg.reshape(seqs, 1, length), seg.reshape(tok, 1))


def attention_bwd(q, k, v, kt, do, seg, rb, block=256):
    tok, lanes = q.shape
    seqs, length = seg.shape
    heads = lanes // HD
    full = pl.BlockSpec((length, lanes), lambda s: (s, 0))
    sh = jax.ShapeDtypeStruct((tok, lanes), BF16)
    return pl.pallas_call(
        functools.partial(bwd_kernel, heads, length, block),
        grid=(seqs,),
        out_shape=(sh, sh, sh, jax.ShapeDtypeStruct((heads, NB, 128), F32)),
        in_specs=[pl.BlockSpec(memory_space=pltpu.SMEM), full, full, full,
                  pl.BlockSpec((lanes, length), lambda s: (0, s)), full,
                  pl.BlockSpec((1, 1, length), lambda s: (s, 0, 0)),
                  pl.BlockSpec((length, 1), lambda s: (s, 0))],
        out_specs=(full, full, full, pl.BlockSpec((heads, NB, 128), lambda s: (0, 0, 0))),
        scratch_shapes=[pltpu.VMEM((heads, 2 * length - block, block), F32)] * 2
        + [pltpu.VMEM((length, lanes), F32)] * 2,
        compiler_params=pltpu.CompilerParams(vmem_limit_bytes=56 << 20),
        cost_estimate=pl.CostEstimate(flops=10 * tok * length * lanes, bytes_accessed=tok * lanes * 20, transcendentals=tok * length * heads),
        name="attn_bwd",
    )(rb, q, k, v, kt, do, seg.reshape(seqs, 1, length), seg.reshape(tok, 1))


MESH = pl.DeviceIdType.MESH


class Ring:
    def __init__(self, n, rows):
        self.n = n
        self.inner = 1
        while (self.inner * 2) ** 2 <= n:
            self.inner *= 2
        self.outer = n // self.inner
        self.rows = rows
        self.rows_b = max(rows // 8 // 8 * 8, 8)
        self.rows_a = rows - self.rows_b
        self.count = next(c for c in (4, 2, 1) if self.rows_a % (8 * c) == 0)
        self.piece = self.rows_a // self.count
        self.pieces = [(p * self.piece, self.piece) for p in range(self.count)]

    def place(self):
        self.me = me = lax.axis_index("tensor")
        self.o, self.i = lax.div(me, self.inner), lax.rem(me, self.inner)

    def shard(self, back, side=0):
        return (lax.rem(self.o - back + 2 * self.outer, self.outer) * self.inner
                + lax.rem(self.i - side + self.inner, self.inner))

    def barrier(self, everyone=False, others=()):
        if everyone:
            peers = [{"tensor": self.peer(j)} for j in range(1, self.n)]
        else:
            peers = [self.shard(-1)] + ([self.shard(1)] if self.outer > 2 else [])
            peers += [self.shard(0, j) for j in range(1, self.inner)]
            peers = [{"tensor": p} for p in peers]
        peers += list(others)
        sem = pltpu.get_barrier_semaphore()
        for peer in peers:
            pl.semaphore_signal(sem, inc=1, device_id=peer, device_id_type=MESH)
        pl.semaphore_wait(sem, len(peers))

    def peer(self, j):
        return lax.rem(self.me + j, self.n)

    def gather_semaphores(self):
        dma = pltpu.SemaphoreType.DMA
        one = [dma((self.outer - 1, self.count)), dma((self.inner - 1, self.outer, self.count)),
               dma((self.inner, self.outer - 1)), dma((self.inner - 1,))]
        return one + one

    def reduce_scratch(self, width):
        dma = pltpu.SemaphoreType.DMA
        one = [dma((self.inner - 1, self.outer, self.count)), dma((self.outer - 1, self.count)),
               dma((self.inner, self.outer - 1)), dma((self.inner - 1,))]
        return [pltpu.VMEM((self.inner - 1, self.outer, self.rows_a, width), F32),
                pltpu.VMEM((self.outer - 1, self.rows_a, width), F32),
                pltpu.VMEM((self.inner, self.outer - 1, self.rows_b, width), F32),
                pltpu.VMEM((self.inner - 1, self.rows_b, width), F32)] + one + one


def remote(src, dst, send, recv, peer):
    return pltpu.make_async_remote_copy(src_ref=src, dst_ref=dst, send_sem=send, recv_sem=recv,
                                        device_id={"tensor": peer}, device_id_type=MESH)


class Gather:
    def __init__(self, ring, view, own, sems):
        self.r, self.view, self.own = ring, view, own
        (self.s_oa, self.s_ia, self.s_ob, self.s_ib, self.r_oa, self.r_ia, self.r_ob, self.r_ib) = sems
        self.sent = []

    def outer_a(self, step, p):
        r = self.r
        row, rows = r.pieces[p]
        shard = r.shard(step)
        src = self.own(row, rows) if step == 0 else self.view(shard, row, rows)
        return remote(src, self.view(shard, row, rows), self.s_oa.at[step, p], self.r_oa.at[step, p], r.shard(-1))

    def inner_a(self, j, step, p):
        r = self.r
        row, rows = r.pieces[p]
        shard = r.shard(step)
        src = self.own(row, rows) if step == 0 else self.view(shard, row, rows)
        return remote(src, self.view(shard, row, rows), self.s_ia.at[j - 1, step, p], self.r_ia.at[j - 1, step, p],
                      r.shard(0, -j))

    def outer_b(self, j, step):
        r = self.r
        shard = r.shard(step, j)
        src = self.own(r.rows_a, r.rows_b) if step == 0 and j == 0 else self.view(shard, r.rows_a, r.rows_b)
        return remote(src, self.view(shard, r.rows_a, r.rows_b), self.s_ob.at[j, step], self.r_ob.at[j, step], r.shard(-1))

    def inner_b(self, j):
        r = self.r
        return remote(self.own(r.rows_a, r.rows_b), self.view(r.shard(0), r.rows_a, r.rows_b),
                      self.s_ib.at[j - 1], self.r_ib.at[j - 1], r.shard(0, -j))

    def go(self, copy):
        copy.start()
        self.sent.append(copy)

    def start_a(self, p):
        self.go(self.outer_a(0, p))
        for j in range(1, self.r.inner):
            self.go(self.inner_a(j, 0, p))

    def start_b(self):
        for j in range(1, self.r.inner):
            self.go(self.inner_b(j))
        self.go(self.outer_b(0, 0))

    def middle(self):
        r = self.r
        for j in range(1, r.inner):
            self.inner_b(j).wait_recv()
            self.go(self.outer_b(j, 0))
        for step in range(1, r.outer):
            for p in range(r.count):
                self.outer_a(step - 1, p).wait_recv()
                if step < r.outer - 1:
                    self.go(self.outer_a(step, p))
                for j in range(1, r.inner):
                    self.go(self.inner_a(j, step, p))
            for j in range(r.inner):
                self.outer_b(j, step - 1).wait_recv()
                if step < r.outer - 1:
                    self.go(self.outer_b(j, step))

    def finish(self):
        r = self.r
        for step in range(r.outer):
            for p in range(r.count):
                for j in range(1, r.inner):
                    self.inner_a(j, step, p).wait_recv()
        for copy in self.sent:
            copy.wait_send()


class Reduce:
    def __init__(self, ring, src, scratch):
        self.r, self.src = ring, src
        (self.ia, self.oa, self.ob, self.ib, self.s_ia, self.s_oa, self.s_ob, self.s_ib,
         self.r_ia, self.r_oa, self.r_ob, self.r_ib) = scratch
        self.sent = []

    def part(self, shard, row, rows):
        return self.src.at[pl.ds(pl.multiple_of(shard * self.r.rows + row, 8), rows), :]

    def inner_a(self, j, step, p):
        r = self.r
        row, rows = r.pieces[p]
        return remote(self.part(r.shard(step + 1, -j), row, rows), self.ia.at[j - 1, step, pl.ds(row, rows), :],
                      self.s_ia.at[j - 1, step, p], self.r_ia.at[j - 1, step, p], r.shard(0, -j))

    def outer_a(self, step, p):
        r = self.r
        row, rows = r.pieces[p]
        src = self.ia.at[0, 0, pl.ds(row, rows), :] if step == 0 else self.oa.at[step - 1, pl.ds(row, rows), :]
        return remote(src, self.oa.at[step, pl.ds(row, rows), :], self.s_oa.at[step, p], self.r_oa.at[step, p], r.shard(-1))

    def outer_b(self, j, step):
        r = self.r
        src = self.part(r.shard(1, j), r.rows_a, r.rows_b) if step == 0 else self.ob.at[j, step - 1]
        return remote(src, self.ob.at[j, step], self.s_ob.at[j, step], self.r_ob.at[j, step], r.shard(-1))

    def inner_b(self, j):
        r = self.r
        return remote(self.ob.at[j, r.outer - 2], self.ib.at[j - 1], self.s_ib.at[j - 1], self.r_ib.at[j - 1], r.shard(0, j))

    def go(self, make, *at):
        make(*at).start()
        self.sent.append((make, at))

    def start(self):
        r = self.r
        for j in range(r.inner):
            self.go(self.outer_b, j, 0)
        for step in range(r.outer):
            for p in range(r.count):
                for j in range(1, r.inner):
                    self.go(self.inner_a, j, step, p)

    def event_a(self, step, p, done_a):
        r = self.r
        last = step == r.outer - 1
        row, rows = r.pieces[p]
        for j in range(1, r.inner):
            self.inner_a(j, step, p).wait_recv()
        total = self.part(r.shard(step + 1), row, rows)[...]
        for j in range(1, r.inner):
            total = total + self.ia[j - 1, step, pl.ds(row, rows), :]
        if step == 0:
            self.ia[0, 0, pl.ds(row, rows), :] = total
        else:
            self.outer_a(step - 1, p).wait_recv()
            total = total + self.oa[step - 1, pl.ds(row, rows), :]
            if not last:
                self.oa[step - 1, pl.ds(row, rows), :] = total
        if last:
            done_a(p, total)
        else:
            self.go(self.outer_a, step, p)

    def event_b(self, step):
        r = self.r
        for j in range(r.inner):
            self.outer_b(j, step - 1).wait_recv()
            total = self.ob[j, step - 1] + self.part(r.shard(step + 1, j), r.rows_a, r.rows_b)[...]
            self.ob[j, step - 1] = total
            if step < r.outer - 1:
                self.go(self.outer_b, j, step)
            elif j > 0:
                self.go(self.inner_b, j)

    def last_b(self, done_b):
        total = self.ob[0, self.r.outer - 2]
        for j in range(1, self.r.inner):
            self.inner_b(j).wait_recv()
            total = total + self.ib[j - 1]
        done_b(total)

    def events(self, done_a, done_b):
        r = self.r
        todo = []
        for step in range(r.outer):
            for p in range(r.count):
                todo.append(functools.partial(self.event_a, step, p, done_a))
            if step >= 1:
                todo.append(functools.partial(self.event_b, step))
        return todo + [functools.partial(self.last_b, done_b)]

    def finish(self):
        for make, at in self.sent:
            make(*at).wait_send()


def on_steps(step, events, share, last):
    done = 0
    for i in range(last):
        upto = min(int(share * (i + 1)), len(events))
        if upto > done:
            @pl.when(step == i)
            def _():
                for event in events[done:upto]:
                    event()

            done = upto

    @pl.when(step == last)
    def _():
        for event in events[done:]:
            event()


def wire(us):
    return pl.CostEstimate(flops=0, bytes_accessed=us * 3_000_000, transcendentals=0)


def params(cid, vmem):
    return pltpu.CompilerParams(collective_id=cid, has_side_effects=True, vmem_limit_bytes=vmem)


def gather_columns(x, n, cid):
    rows, lanes = x.shape
    ring = Ring(n, rows)
    flat = lanes % 128 == 0

    def kernel(x_ref, out, *sems):
        ring.place()
        ring.barrier()

        def view(shard, row, count):
            if flat:
                return out.at[pl.ds(row, count), pl.ds(pl.multiple_of(shard * lanes, 128), lanes)]
            return out.at[shard, pl.ds(row, count), :]

        gather = Gather(ring, view, lambda row, count: x_ref.at[pl.ds(row, count), :], sems[:8])
        keep = pltpu.make_async_copy(x_ref, view(ring.shard(0), 0, rows), sems[8])
        gather.start_b()
        for p in range(ring.count):
            gather.start_a(p)
        keep.start()
        gather.middle()
        gather.finish()
        keep.wait()

    shape = (rows, n * lanes) if flat else (n, rows, lanes)
    out = pl.pallas_call(
        kernel,
        out_shape=jax.ShapeDtypeStruct(shape, F32),
        in_specs=[pl.BlockSpec(memory_space=pltpu.VMEM)],
        out_specs=pl.BlockSpec(memory_space=pl.ANY),
        scratch_shapes=ring.gather_semaphores() + [pltpu.SemaphoreType.DMA],
        compiler_params=params(cid, 16 << 20),
        cost_estimate=wire(90),
        name="gather_columns",
    )(x)
    return out if flat else out.transpose(1, 0, 2).reshape(rows, n * lanes)


class Swap:
    def __init__(self, axis, n, block, got, send, recv):
        self.axis, self.n, self.block, self.got, self.send, self.recv = axis, n, block, got, send, recv

    def copy(self, j):
        me = lax.axis_index(self.axis)
        peer = lax.rem(me + j, self.n)
        return pltpu.make_async_remote_copy(
            src_ref=self.block(peer), dst_ref=self.got.at[j - 1],
            send_sem=self.send.at[j - 1], recv_sem=self.recv.at[j - 1], device_id={self.axis: peer}, device_id_type=MESH)

    def start(self):
        for j in range(1, self.n):
            self.copy(j).start()

    def total(self):
        for j in range(1, self.n):
            self.copy(j).wait()
        value = self.block(lax.axis_index(self.axis))[...]
        for j in range(1, self.n):
            value = value + self.got[j - 1]
        return value

    @staticmethod
    def scratch(n, shape):
        return [pltpu.VMEM((n - 1,) + shape, F32), pltpu.SemaphoreType.DMA((n - 1,)), pltpu.SemaphoreType.DMA((n - 1,))]


def reduce_norm_gather(part, values, upper, gain, small, keep_rows, inner_w, outer_w, n, n_dp, cid):
    total, width = part.shape
    rows = total // n
    ring = Ring(n, rows)
    n_red = len(ring.reduce_scratch(width))
    wide = width // n_dp
    s_rows = small.shape[1]
    in_rows = inner_w.shape[0] // n_dp
    height = outer_w.shape[0]
    out_rows = height // n
    columns = wide % 128 == 0
    if not columns:
        outer_w = outer_w.reshape(height, n_dp, wide).transpose(1, 0, 2)
    swaps = [(n_dp, (s_rows, wide)), (n, (s_rows, wide)), (n_dp, (in_rows, inner_w.shape[1])),
             (n_dp, (height, wide)), (n, (out_rows, wide))]

    def kernel(part_ref, val_ref, up_ref, gain_ref, small_ref, in_ref, ou_ref, out, small_out, in_out, ou_out,
               piece, sm, sm2, ou2, gain_acc, keep_sem, *scratch):
        dp = lax.axis_index("dp")
        ring.place()
        ring.barrier(everyone=True, others=[{"dp": lax.rem(dp + j, n_dp)} for j in range(1, n_dp)])
        one = Swap("dp", n_dp, lambda p: sm.at[p], *scratch[:3])
        two = Swap("tensor", n, lambda p: sm2, *scratch[3:6])
        inner_sum = Swap("dp", n_dp, lambda p: in_ref.at[pl.ds(pl.multiple_of(p * in_rows, 8), in_rows), :], *scratch[6:9])
        ou_one = Swap("dp", n_dp, (lambda p: ou_ref.at[:, pl.ds(pl.multiple_of(p * wide, 128), wide)]) if columns
                      else (lambda p: ou_ref.at[p]), *scratch[9:12])
        ou_two = Swap("tensor", n, lambda p: ou2.at[pl.ds(pl.multiple_of(p * out_rows, 8), out_rows), :], *scratch[12:15])
        reduce = Reduce(ring, part_ref, scratch[15:15 + n_red])
        gather = Gather(ring, lambda shard, row, count: out.at[pl.ds(pl.multiple_of(shard * rows + row, 8), count), :],
                        lambda row, count: piece.at[pl.ds(row, count), :], scratch[15 + n_red:])
        reduce.start()
        ou_one.start()
        inner_sum.start()
        gain_acc[...] = jnp.zeros_like(gain_acc)
        sm[...] = small_ref[...]

        def back(row, count, grad):
            x = val_ref[pl.ds(row, count), :]
            rr = lax.rsqrt(jnp.mean(x * x, axis=1, keepdims=True) + EPSILON)
            scaled = gain_ref[...] * grad
            inner = jnp.mean(scaled * x, axis=1, keepdims=True)
            piece[pl.ds(row, count), :] = up_ref[pl.ds(row, count), :] + rr * scaled - x * (rr * rr * rr * inner)
            gain_acc[...] += jnp.sum(grad * x * rr, axis=0, keepdims=True)

        def done_a(p, value):
            row, count = ring.pieces[p]
            back(row, count, value)
            gather.start_a(p)

        def done_b(value):
            back(ring.rows_a, ring.rows_b, value)
            gather.start_b()

        for event in reduce.events(done_a, done_b):
            event()
        keep = pltpu.make_async_copy(piece, out.at[pl.ds(pl.multiple_of(ring.shard(0) * rows, 8), rows), :], keep_sem)
        keep.start()
        for p in range(n_dp):
            sm[p, 0:1, :] = gain_acc[:, p * wide:(p + 1) * wide]
        one.start()
        ou2[...] = ou_one.total()
        ou_two.start()
        gather.middle()
        sm2[...] = one.total()
        two.start()
        in_out[...] = inner_sum.total()
        gather.finish()
        ou_out[...] = ou_two.total()
        both = two.total()
        last = lax.broadcasted_iota(jnp.int32, both.shape, 0) >= s_rows - keep_rows
        small_out[...] = jnp.where(last, sm2[...], both)
        reduce.finish()
        keep.wait()

    vm = pl.BlockSpec(memory_space=pltpu.VMEM)
    block = (s_rows, wide)
    return pl.pallas_call(
        kernel,
        out_shape=[jax.ShapeDtypeStruct(s, F32) for s in ((total, width), block, (in_rows, inner_w.shape[1]), (out_rows, wide))],
        in_specs=[vm] * 7,
        out_specs=[pl.BlockSpec(memory_space=pl.ANY), vm, vm, vm],
        scratch_shapes=[pltpu.VMEM((rows, width), F32), pltpu.VMEM((n_dp,) + block, F32), pltpu.VMEM(block, F32),
                        pltpu.VMEM((height, wide), F32), pltpu.VMEM((1, width), F32), pltpu.SemaphoreType.DMA]
        + [ref for swap in swaps for ref in Swap.scratch(*swap)]
        + ring.reduce_scratch(width) + ring.gather_semaphores(),
        compiler_params=params(cid, 48 << 20),
        cost_estimate=wire(180),
        name="reduce_norm_gather",
    )(part, values, upper, gain.reshape(1, width), small, inner_w, outer_w)


EXPERTS = 8
CAP = 576
SLOTS = EXPERTS * CAP
LN = 128
GC = math.sqrt(2.0 / math.pi)


def spread(dst, row0, sub, src, rows):
    for j in range(sub):
        dst[pl.ds(row0 * sub + j, rows, stride=sub), :] = src[:, j * LN:(j + 1) * LN].astype(F32)


def tile(ref, row, sub):
    return ref.at[pl.ds(pl.multiple_of(row * sub, sub), sub), :]


def dispatch_kernel(tok, sub, step_slots, with_share, tgt, src, *rest):
    if with_share:
        share, out, share_out, rows_in, rows_out, share_rows = rest
    else:
        out, rows_in, rows_out = rest
    step = pl.program_id(0)

    @pl.when(step == 0)
    def _():
        def load(i, c):
            t0 = pl.multiple_of(i * 64, 64)
            spread(rows_in, t0, sub, src.at[pl.ds(t0, 64), :], 64)
            return c

        lax.fori_loop(0, tok // 64, load, 0)

        def zero(i, c):
            r0 = pl.multiple_of(i * 8 * sub, 8 * sub)
            rows_out[pl.ds(r0, 8 * sub), :] = jnp.zeros((8 * sub, LN), F32)
            if with_share:
                share_rows[pl.ds(pl.multiple_of(i * 8, 8), 8), :] = jnp.zeros((8, LN), F32)
            return c

        lax.fori_loop(0, SLOTS // 8, zero, 0)

        def move(i, c):
            for u in range(8):
                t = i * 8 + u
                row = tile(rows_in, t, sub)[...]
                for choice in range(2):
                    slot = tgt[choice * tok + t]
                    tile(rows_out, slot, sub)[...] = row
                    if with_share:
                        share_rows[pl.ds(slot, 1), :] = share[pl.ds(choice * tok + t, 1), :]
            return c

        lax.fori_loop(0, tok // 8, move, 0)

    base = step * step_slots

    def emit(i, c):
        s0 = pl.multiple_of(i * 64, 64)
        for j in range(sub):
            out[pl.ds(s0, 64), j * LN:(j + 1) * LN] = rows_out[pl.ds((base + s0) * sub + j, 64, stride=sub), :].astype(BF16)
        return c

    lax.fori_loop(0, step_slots // 64, emit, 0)
    if with_share:
        share_out[...] = share_rows[pl.ds(pl.multiple_of(base, step_slots), step_slots), :]


def dispatch(tgt, src, share=None, step_slots=512):
    tok, width = src.shape
    sub = width // LN
    ws = share is not None

    def whole(shape):
        return pl.BlockSpec(shape, lambda i, t: (0, 0), pipeline_mode=pl.Buffered(1))

    out_shape = [jax.ShapeDtypeStruct((SLOTS, width), BF16)]
    out_specs = [pl.BlockSpec((step_slots, width), lambda i, t: (i, 0))]
    scratch = [pltpu.VMEM((tok * sub, LN), F32), pltpu.VMEM(((SLOTS + 1) * sub, LN), F32)]
    in_specs = [whole((tok, width))]
    args = [src]
    if ws:
        in_specs.append(whole((2 * tok, LN)))
        args.append(share)
        out_shape.append(jax.ShapeDtypeStruct((SLOTS, LN), F32))
        out_specs.append(pl.BlockSpec((step_slots, LN), lambda i, t: (i, 0)))
        scratch.append(pltpu.VMEM((SLOTS + 8, LN), F32))
    r = pl.pallas_call(
        functools.partial(dispatch_kernel, tok, sub, step_slots, ws),
        grid_spec=pltpu.PrefetchScalarGridSpec(num_scalar_prefetch=1, grid=(SLOTS // step_slots,), in_specs=in_specs,
                                               out_specs=out_specs, scratch_shapes=scratch),
        out_shape=out_shape,
        compiler_params=pltpu.CompilerParams(vmem_limit_bytes=56 << 20),
        cost_estimate=pl.CostEstimate(flops=0, bytes_accessed=64 << 20, transcendentals=0),
        name="dispatch",
    )(tgt, *args)
    return r if ws else r[0]


def combine_rows(tgt, rows, mix, out, tok, sub, t0, count):
    def body(i, c):
        for u in range(8):
            r = i * 8 + u
            one = rows[pl.ds(pl.multiple_of(tgt[t0 + r] * sub, sub), sub), :]
            two = rows[pl.ds(pl.multiple_of(tgt[tok + t0 + r] * sub, sub), sub), :]
            mix[pl.ds(pl.multiple_of(r * sub, sub), sub), :] = one + two
        return c

    lax.fori_loop(0, count // 8, body, 0)
    for j in range(sub):
        out[:, j * LN:(j + 1) * LN] = mix[pl.ds(j, count, stride=sub), :]


def by_expert(shape):
    return pl.BlockSpec(shape, lambda i, *t: (jnp.minimum(i, EXPERTS - 1),) + (0,) * (len(shape) - 1))


def forward_kernel(tok, sub, count, tgt, x, sh, win, wdn, gate, up, act, mo, rows, mix):
    step = pl.program_id(0)

    @pl.when(step == 0)
    def _():
        rows[SLOTS * sub:, :] = jnp.zeros((sub, LN), F32)

    @pl.when(step < EXPERTS)
    def _():
        g = dot(x[...], win[0, 0], 1, 1)
        u = dot(x[...], win[0, 1], 1, 1)
        gate[0] = g
        up[0] = u
        a = (0.5 * g * (1.0 + jnp.tanh(GC * (g + 0.044715 * (g * g * g)))) * u).astype(BF16)
        act[0] = a
        spread(rows, step * CAP, sub, dot(a, wdn[0], 1, 0) * sh[:, 0:1], CAP)

    @pl.when(step >= EXPERTS)
    def _():
        combine_rows(tgt, rows, mix, mo, tok, sub, (step - EXPERTS) * count, count)


def experts_forward(tgt, x, sh, win, wdn, tok, count=256):
    width = x.shape[1]
    sub = width // LN
    ff = wdn.shape[1]
    mid = by_expert((1, CAP, ff))
    return pl.pallas_call(
        functools.partial(forward_kernel, tok, sub, count),
        grid_spec=pltpu.PrefetchScalarGridSpec(
            num_scalar_prefetch=1, grid=(EXPERTS + tok // count,),
            in_specs=[by_expert((CAP, width)), by_expert((CAP, LN)), by_expert((1, 2, ff, width)), by_expert((1, ff, width))],
            out_specs=[mid, mid, mid, pl.BlockSpec((count, width), lambda i, t: (jnp.maximum(i - EXPERTS, 0), 0))],
            scratch_shapes=[pltpu.VMEM(((SLOTS + 1) * sub, LN), F32), pltpu.VMEM((count * sub, LN), F32)]),
        out_shape=[jax.ShapeDtypeStruct((EXPERTS, CAP, ff), F32)] * 2
        + [jax.ShapeDtypeStruct((EXPERTS, CAP, ff), BF16), jax.ShapeDtypeStruct((tok, width), F32)],
        compiler_params=pltpu.CompilerParams(vmem_limit_bytes=60 << 20),
        cost_estimate=pl.CostEstimate(flops=6 * SLOTS * width * ff, bytes_accessed=100 << 20, transcendentals=SLOTS * ff),
        name="experts_forward",
    )(tgt, x, sh, win, wdn)


def backward_kernel(tok, chunk, ring, share, cot, tgt_row, tgt_col, sh, gate, up, act, win, wdn, part, hid,
                    y, dgu, mi, sg, res, acc, acc_sem, *scratch):
    step = pl.program_id(0)
    width = cot.shape[1]
    first = step * CAP
    ring.place()
    reduce = Reduce(ring, part, scratch)

    @pl.when(step == 0)
    def _():
        ring.barrier()
        reduce.start()
        acc[...] = jnp.zeros_like(acc)
        sg[...] = jnp.zeros_like(sg)

    slot = lax.broadcasted_iota(jnp.int32, (CAP, chunk), 0) + first

    def fetch(i, rows):
        t0 = pl.multiple_of(i * chunk, chunk)
        held = (tgt_row[0:1, pl.ds(t0, chunk)] == slot) | (tgt_row[1:2, pl.ds(t0, chunk)] == slot)
        return rows + dot(jnp.where(held, 1.0, 0.0).astype(BF16), cot[pl.ds(t0, chunk), :], 1, 0)

    rows = lax.fori_loop(0, tok // chunk, fetch, jnp.zeros((CAP, width), F32)).astype(BF16)
    y[...] = rows
    h = dot(rows, wdn[0], 1, 1)
    g, u = gate[0], up[0]
    g2 = g * g
    t = jnp.tanh(GC * (g + 0.044715 * g2 * g))
    half = 0.5 * (1.0 + t)
    sgrow = jnp.sum(act[0].astype(F32) * h, axis=1, keepdims=True)
    da = sh[:, 0:1] * h
    slope = half + (0.5 * GC) * g * (1.0 - t * t) * (1.0 + (3 * 0.044715) * g2)
    dg = (da * u * slope).astype(BF16)
    du = (da * (g * half)).astype(BF16)
    dgu[0, 0] = dg
    dgu[0, 1] = du
    dx = (dot(dg, win[0, 0], 1, 0) + dot(du, win[0, 1], 1, 0)).astype(BF16)
    lane = lax.broadcasted_iota(jnp.int32, (CAP, LN), 1)
    high = sgrow.astype(BF16).astype(F32)
    aux = jnp.where(lane == 0, high, jnp.where(lane == 1, sgrow - high, 0.0)).astype(BF16)
    slots = lax.broadcasted_iota(jnp.int32, (chunk, CAP), 1) + first
    lanes = lax.broadcasted_iota(jnp.int32, (chunk, LN), 1)

    def hand_back(i, c):
        t0 = pl.multiple_of(i * chunk, chunk)
        one, two = tgt_col[pl.ds(t0, chunk), 0:1], tgt_col[pl.ds(t0, chunk), 1:2]
        held = jnp.where((one == slots) | (two == slots), 1.0, 0.0).astype(BF16)
        acc[pl.ds(t0, chunk), :] += dot(held, dx, 1, 0)
        value = dot(held, aux, 1, 0)
        value = value[:, 0:1] + value[:, 1:2]
        pair = jnp.where(lanes == 0, one, jnp.where(lanes == 1, two, SLOTS))
        sg[pl.ds(t0, chunk), :] += jnp.where((pair >= first) & (pair < first + CAP), value, 0.0)
        return c

    lax.fori_loop(0, tok // chunk, hand_back, 0)

    def done_a(p, value):
        row, n = ring.pieces[p]
        res[pl.ds(row, n), :] = value + hid[pl.ds(row, n), :]

    def done_b(value):
        res[pl.ds(ring.rows_a, ring.rows_b), :] = value + hid[pl.ds(ring.rows_a, ring.rows_b), :]

    @pl.when(step == EXPERTS - 1)
    def _():
        pltpu.make_async_copy(acc, mi, acc_sem).start()

    on_steps(step, reduce.events(done_a, done_b), share, EXPERTS - 1)

    @pl.when(step == EXPERTS - 1)
    def _():
        pltpu.make_async_copy(acc, mi, acc_sem).wait()
        reduce.finish()


def whole(shape):
    return pl.BlockSpec(shape, lambda i, *t: (0,) * len(shape), pipeline_mode=pl.Buffered(1))


def experts_backward(tgt, cot, sh, gate, up, act, win, wdn, part, hid, n, cid, chunk=512, share=1.6):
    tok, width = part.shape
    ff = wdn.shape[1]
    ring = Ring(n, tok // n)
    mid = by_expert((1, CAP, ff))
    tgt_row = tgt.reshape(2, tok)
    return pl.pallas_call(
        functools.partial(backward_kernel, tok, chunk, ring, share),
        grid=(EXPERTS,),
        in_specs=[whole(cot.shape), whole((2, tok)), whole((tok, 2)), by_expert((CAP, LN)), mid, mid, mid,
                  by_expert((1, 2, ff, width)), by_expert((1, ff, width)), whole(part.shape), whole(hid.shape)],
        out_specs=[by_expert((CAP, width)), by_expert((1, 2, CAP, ff)), pl.BlockSpec(memory_space=pl.ANY),
                   pl.BlockSpec((tok, LN), lambda i: (0, 0)), pl.BlockSpec(hid.shape, lambda i: (0, 0))],
        scratch_shapes=[pltpu.VMEM((tok, width), F32), pltpu.SemaphoreType.DMA] + ring.reduce_scratch(width),
        out_shape=[jax.ShapeDtypeStruct((SLOTS, width), BF16), jax.ShapeDtypeStruct((EXPERTS, 2, CAP, ff), BF16),
                   jax.ShapeDtypeStruct((tok, width), F32), jax.ShapeDtypeStruct((tok, LN), F32),
                   jax.ShapeDtypeStruct(hid.shape, F32)],
        compiler_params=params(cid, 63 << 20),
        cost_estimate=wire(90),
        name="experts_backward",
    )(cot, tgt_row, tgt_row.T, sh, gate, up, act, win, wdn, part, hid)


def exclusive_or(a, b, bound):
    value, bit = 0, 1
    while bit < bound:
        value = value + lax.rem(lax.div(a, bit) + lax.div(b, bit), 2) * bit
        bit *= 2
    return value


def weights_kernel(parts, ring, n, share, x, y, sh, act, dgu, part, small, keep, give, out, small_out,
                   kept, gave, got, g_send, g_recv, sw_got, sw_send, sw_recv, *scratch):
    step = pl.program_id(0)
    dp = lax.axis_index("dp")
    mine = lax.rem(dp, 2)
    upper = lax.div(dp, 2)
    blocks = parts // 2
    half = blocks // 2
    ring.place()
    reduce = Reduce(ring, part, scratch)
    swap = Swap("tensor", n, lambda p: small.at[p], sw_got, sw_send, sw_recv)

    def to_partner(slot):
        return pltpu.make_async_remote_copy(
            src_ref=gave.at[slot], dst_ref=got.at[slot], send_sem=g_send.at[slot], recv_sem=g_recv.at[slot],
            device_id={"dp": dp + 1 - 2 * mine}, device_id_type=MESH)

    @pl.when(step == 0)
    def _():
        ring.barrier(everyone=True, others=[{"dp": dp + 1 - 2 * mine}])
        swap.start()
        reduce.start()

    @pl.when(step >= 1)
    def _():
        slot = lax.rem(step + 1, 2)
        to_partner(slot).wait()
        for q in range(blocks):
            to = exclusive_or(q, upper, blocks)

            @pl.when(to < half)
            def _():
                keep[to, 0] = kept[slot, q] + got[slot, q]

            @pl.when(to >= half)
            def _():
                give[to - half, 0] = kept[slot, q] + got[slot, q]

    @pl.when(step < EXPERTS)
    def _():
        slot = lax.rem(step, 2)
        og = (y[...].astype(F32) * sh[:, 0:1]).astype(BF16)
        wide = x.shape[1] // parts
        grads = [dot(dgu[0, 0], x[...], 0, 0), dot(dgu[0, 1], x[...], 0, 0), dot(act[0], og, 0, 0)]
        for bit in range(2):
            @pl.when(mine == bit)
            def _():
                for p in range(parts):
                    to = kept if p % 2 == bit else gave
                    for g in range(3):
                        to[slot, p // 2, g] = grads[g][:, p * wide:(p + 1) * wide]
        to_partner(slot).start()

    def done_a(p, value):
        row, count = ring.pieces[p]
        out[pl.ds(row, count), :] = value

    def done_b(value):
        out[pl.ds(ring.rows_a, ring.rows_b), :] = value

    on_steps(step, reduce.events(done_a, done_b), share, EXPERTS)

    @pl.when(step == EXPERTS)
    def _():
        small_out[...] = swap.total()
        reduce.finish()


def experts_weights(x, y, sh, act, dgu, part, small, n, parts, cid, share=1.3):
    tok, width = part.shape
    ff = act.shape[2]
    wide = width // parts
    ring = Ring(n, tok // n)
    half = parts // 4
    o_w = jax.ShapeDtypeStruct((half, EXPERTS, 3, ff, wide), F32)
    b_w = pl.BlockSpec((half, 1, 3, ff, wide), lambda i, *t: (0, jnp.maximum(i - 1, 0), 0, 0, 0))
    slots = pltpu.VMEM((2, parts // 2, 3, ff, wide), F32)
    dma = pltpu.SemaphoreType.DMA
    return pl.pallas_call(
        functools.partial(weights_kernel, parts, ring, n, share),
        grid=(EXPERTS + 1,),
        in_specs=[by_expert((CAP, width)), by_expert((CAP, width)), by_expert((CAP, LN)),
                  by_expert((1, CAP, ff)), by_expert((1, 2, CAP, ff)), whole(part.shape), whole(small.shape)],
        out_specs=[b_w, b_w, pl.BlockSpec((tok // n, width), lambda i: (0, 0)),
                   pl.BlockSpec(small.shape[1:], lambda i: (0, 0))],
        scratch_shapes=[slots, slots, slots, dma((2,)), dma((2,))]
        + Swap.scratch(n, small.shape[1:]) + ring.reduce_scratch(width),
        out_shape=[o_w, o_w, jax.ShapeDtypeStruct((tok // n, width), F32), jax.ShapeDtypeStruct(small.shape[1:], F32)],
        compiler_params=params(cid, 63 << 20),
        cost_estimate=wire(90),
        name="experts_weights",
    )(x, y, sh, act, dgu, part, small)


def slot_targets(routes, order):
    tok = routes.shape[0]
    pos = jnp.arange(tok, dtype=jnp.int32)
    rank = jnp.sum(jnp.where(order[:, None] == pos[None, :], pos[:, None], 0), axis=0)
    earlier = (rank[:, None] > rank[None, :]).astype(BF16)
    ex = jnp.arange(EXPERTS, dtype=jnp.int32)
    onehot = (routes[:, :, None] == ex[None, None, :]).astype(BF16)
    before = dot(earlier, onehot.reshape(tok, 2 * EXPERTS), 1, 0).reshape(tok, 2, EXPERTS)
    first = jnp.sum(onehot[:, 0].astype(F32), axis=0)
    before = before + jnp.stack([jnp.zeros((EXPERTS,), F32), first])[None]
    slot = jnp.sum(before * onehot.astype(F32), axis=2).astype(jnp.int32)
    return jnp.where(slot < CAP, routes * CAP + slot, SLOTS).T.reshape(-1)


EPSILON = 1e-06
PRECISE = lax.Precision.HIGHEST


def rms_norm(values, gain):
    return values * lax.rsqrt(jnp.mean(values * values, axis=-1, keepdims=True) + EPSILON) * gain


def rms_back(values, gain, grad):
    rr = lax.rsqrt(jnp.mean(values * values, axis=-1, keepdims=True) + EPSILON)
    scaled = gain * grad
    back = rr * scaled - values * (rr * rr * rr) * jnp.mean(scaled * values, axis=-1, keepdims=True)
    return back, jnp.sum(grad * values * rr, axis=0)


def make_shards(mesh):
    n_tensor = mesh.shape["tensor"]
    n_dp = mesh.shape["dp"]

    def layer(tokens, cotangent, gain_attn, gain_moe, w_qkv, w_out, rel_bias, w_router, w_in, w_down,
              segment_ids, routes, order):
        tok, width = tokens.shape
        lanes = w_qkv.shape[2]
        share_rows = tok // n_tensor
        row0 = lax.axis_index("tensor") * share_rows

        def halve(keep, give):
            while True:
                blocks = keep.shape[0]
                came = lax.ppermute(give, "dp", [(d, d ^ (2 * blocks)) for d in range(n_dp)])
                if blocks == 1:
                    return keep[0], came[0]
                a = keep + came
                keep, give = a[:blocks // 2], a[blocks // 2:]

        def own(a):
            return lax.dynamic_slice_in_dim(a, row0, share_rows, 0)

        one = (order[0, 0] >= 0).astype(F32)
        w_out_cols = lax.dynamic_slice_in_dim(w_out, lax.axis_index("dp") * (width // n_dp), width // n_dp, 1).astype(F32)
        w_out_rows = lax.all_gather(w_out_cols, "tensor", axis=0, tiled=True)
        x = tokens.astype(F32)
        attn_input = rms_norm(x, gain_attn).astype(BF16)
        qkv = jnp.dot(attn_input, w_qkv.reshape(width, 3 * lanes), preferred_element_type=F32).astype(BF16)
        q, k, v = (qkv[:, i * lanes:(i + 1) * lanes] for i in range(3))
        rb = rel_bias.astype(F32).reshape(-1)
        attended = attention_fwd(q, k, v.T, segment_ids, rb)
        tgt = slot_targets(routes, order[0])

        attended, w_out_rows = lax.optimization_barrier((attended, w_out_rows))
        w_out_all = lax.all_gather(w_out_rows, "dp", axis=1, tiled=True) * one
        attended_all = gather_columns(attended, n_tensor, 0)
        hidden_one = x + jnp.dot(attended_all, w_out_all, preferred_element_type=F32)
        moe_input = rms_norm(hidden_one, gain_moe).astype(BF16)
        logits = jnp.dot(moe_input, w_router, preferred_element_type=F32)
        picked = (routes[:, :, None] == jnp.arange(EXPERTS, dtype=jnp.int32)[None, None, :]).astype(F32)

        def route(logit_rows, picked_rows):
            soft = jax.nn.softmax(logit_rows, axis=-1)
            chosen = jnp.sum(soft[:, None, :] * picked_rows, axis=-1)
            return soft, chosen, jnp.sum(chosen, axis=-1, keepdims=True)

        soft, chosen, both = route(logits, picked)
        pair_share = chosen / both
        xs, slot_share = dispatch(tgt, moe_input, jnp.broadcast_to(pair_share.T.reshape(-1, 1), (2 * tok, LN)))
        w_in_t = jnp.swapaxes(w_in, 2, 3)
        gate, up, act, moe_part = experts_forward(tgt, xs, slot_share, w_in_t, w_down, tok)
        hidden_s = own(hidden_one)
        y, gate_up_grad, moe_in_part, share_part, result_s = experts_backward(
            tgt, cotangent, slot_share, gate, up, act, w_in_t, w_down, moe_part, hidden_s, n_tensor, 1)
        share_blocks = jnp.pad(share_part[:, :2].T.reshape(2, n_tensor, share_rows).transpose(1, 0, 2), ((0, 0), (0, 6), (0, 0)))
        keep, give, moe_in_sum, share_sum = experts_weights(
            xs, y, slot_share, act, gate_up_grad, moe_in_part, share_blocks, n_tensor, n_dp, 3)
        keep, came = halve(keep, give)
        share_grad = share_sum[0:2].T
        result_s, moe_in_sum = lax.optimization_barrier((result_s, moe_in_sum))
        result = lax.all_gather(result_s, "tensor", axis=0, tiled=True)

        soft_s, chosen_s, both_s, picked_s = own(soft), own(chosen), own(both), own(picked)
        chosen_grad = share_grad / both_s - jnp.sum(share_grad * chosen_s, axis=-1, keepdims=True) / (both_s * both_s)
        prob_grad = jnp.sum(chosen_grad[:, :, None] * picked_s, axis=1)
        logits_grad = soft_s * (prob_grad - jnp.sum(soft_s * prob_grad, axis=-1, keepdims=True))
        moe_input_s = own(moe_input)
        router_part = jnp.dot(moe_input_s.astype(F32).T, logits_grad, precision=PRECISE)
        moe_input_grad = moe_in_sum + jnp.dot(logits_grad, w_router.astype(F32).T, precision=PRECISE)
        norm_grad, gain_moe_part = rms_back(hidden_s, gain_moe, moe_input_grad)
        hidden_grad = own(cotangent).astype(F32) + norm_grad
        proj_grad = hidden_grad.astype(BF16)
        att_grad_s = lax.dot_general(proj_grad, w_out_all.astype(BF16), (((1,), (1,)), ((), ())), preferred_element_type=F32)
        att_grad_s = att_grad_s.astype(BF16).astype(F32)
        pieces = att_grad_s.reshape(share_rows, n_tensor, lanes).transpose(1, 0, 2)
        attended_grad = lax.all_to_all(pieces, "tensor", 0, 0, tiled=False).reshape(tok, lanes)
        w_out_part = lax.dot_general(own(attended_all).astype(BF16), proj_grad, (((0,), (0,)), ((), ())), preferred_element_type=F32)

        dq, dk, dv, bias_part = attention_bwd(q, k, v, k.T, attended_grad, segment_ids, rb)
        qkv_grad = jnp.concatenate([dq, dk, dv], axis=1)
        attn_in_part = lax.dot_general(qkv_grad, w_qkv.reshape(width, 3 * lanes), (((1,), (1,)), ((), ())), preferred_element_type=F32)
        w_qkv_part = lax.dot_general(attn_input, qkv_grad, (((0,), (0,)), ((), ())), preferred_element_type=F32)

        heads = lanes // HD
        wide = width // n_dp
        bias_rows = bias_part[:, :, 0].reshape(heads, n_dp, NB // n_dp).transpose(1, 0, 2)
        bias_rows = jnp.pad(bias_rows, ((0, 0), (0, 0), (0, wide - NB // n_dp)))
        sums = jnp.concatenate([jnp.zeros((1, width), F32), gain_moe_part[None], router_part.T], axis=0)
        sums = sums.reshape(sums.shape[0], n_dp, wide).transpose(1, 0, 2)
        small = jnp.concatenate([sums, jnp.zeros((n_dp, -(sums.shape[1] + heads) % 8, wide), F32), bias_rows], axis=1)
        input_grad, small, w_qkv_grad, w_out_grad = reduce_norm_gather(
            attn_in_part, own(tokens).astype(F32), hidden_grad, gain_attn, small, heads, w_qkv_part, w_out_part, n_tensor, n_dp, 2)

        small, keep = lax.optimization_barrier((small, keep))
        w_in_grad = jnp.swapaxes(keep[:, :2] + came[:, :2], 2, 3)
        w_down_grad = keep[:, 2] + came[:, 2]
        w_qkv_grad = w_qkv_grad.reshape(width // n_dp, 3, lanes)
        rel_bias_grad = small[small.shape[0] - heads:, :NB // n_dp].T
        return (result, input_grad, small[0], small[1], w_qkv_grad, w_out_grad, rel_bias_grad,
                small[2:2 + EXPERTS].T, w_in_grad, w_down_grad)

    return layer


def solution(mesh):
    return jax.shard_map(
        make_shards(mesh),
        mesh=mesh,
        in_specs=(
            P("dp", None),
            P("dp", None),
            P(),
            P(),
            P(None, None, "tensor"),
            P("tensor", None),
            P(None, "tensor"),
            P(),
            P(None, None, None, "tensor"),
            P(None, "tensor", None),
            P("dp", None),
            P("dp", None),
            P("dp", None),
        ),
        out_specs=(
            P("dp", None),
            P("dp", None),
            P("dp"),
            P("dp"),
            P("dp", None, "tensor"),
            P("tensor", "dp"),
            P("dp", "tensor"),
            P("dp", None),
            P(None, None, "dp", "tensor"),
            P(None, "tensor", "dp"),
        ),
        check_vma=False,
    )
```

time: 1170 us -> 828 us (0.71)
  blocking collectives: 221 us -> 0 us
  waiting for transfers between devices: 141 us -> 56.7 us
  Pallas kernels: 558 us -> 636 us
  local copies, waits for them, and re-layouts: 122 us -> 46.9 us
  other arithmetic: 56.7 us -> 27.2 us
    unnamed x1 -> x0, blocking collectives: 181 us -> none
    pallas_call x4, Pallas kernels: 357 us -> 479 us  [the longest x1 214 us: reduce_norm_gather(): pl.pallas_call(kernel, out_shape=[jax.ShapeDtypeStruct(s, F32) for s in (...]
    psum x1 -> x0, waiting for transfers between devices: 51.7 us -> none  [shards(): result = hidden_one + lax.psum(moe_part, 'tensor')]
    dynamic_slice x4 -> x0, local copies, waits for them, and re-layouts: 44.4 us -> none  [the longest x2 30.8 us: halve(): keep = lax.dynamic_index_in_dim(pairs, side, 1, keepdims=False)]
    reduce_scatter x4 -> x0, waiting for transfers between devices: 43.7 us -> none  [the longest x1 43.7 us: shards(): lax.psum_scatter(over_dp(w_out_part, 1), 'tensor', scatter_dimension=0, t...]
    psum x1 -> x0, blocking collectives: 39.6 us -> none  [shards(): small = over_dp(lax.psum(small, 'tensor'), 0)]
    unnamed x8 -> x3, waiting for transfers between devices: 28.9 us -> 0.05 us
    all_to_all x1, waiting for transfers between devices: 16.3 us -> 44.2 us  [layer(): lax.all_to_all(pieces, 'tensor', 0, 0, tiled=False).reshape(tok, lanes)]
  transfers between devices with their start and end apart: 12 -> 5, of which waited for: 4 -> 2; matrix products, arithmetic and copies ran while one was open for 14% -> 8% of each run, Pallas kernels for 42% -> 42%
where the time goes in v2:
time: 828 us; the launch traced here: 822 us
  Pallas kernels  636 us (77%)
  waiting for transfers between devices  56.7 us (7%)
  local copies, waits for them, and re-layouts  46.9 us (6%)
  matrix products  34 us (4%)
  other arithmetic  27.2 us (3%)
  between operations  15.1 us (2%)
    pallas_call x1, Pallas kernels, reduce_norm_gather(): pl.pallas_call(kernel, out_shape=[jax.ShapeDtypeStruct(s, F32) for s in (...  214 us
    pallas_call x1, Pallas kernels, experts_backward(): pl.pallas_call(functools.partial(backward_kernel, tok, chunk, ring, share...  136 us
    pallas_call x1, Pallas kernels, experts_weights(): pl.pallas_call(functools.partial(weights_kernel, parts, ring, n, share),...  96.3 us
    pallas_call x1, Pallas kernels, gather_columns(): pl.pallas_call(kernel, out_shape=jax.ShapeDtypeStruct(shape, F32), in_spe...  82.8 us
    all_to_all x1, waiting for transfers between devices, layer(): lax.all_to_all(pieces, 'tensor', 0, 0, tiled=False).reshape(tok, lanes)  44.2 us
    pallas_call x1, Pallas kernels, experts_forward(): pl.pallas_call(functools.partial(forward_kernel, tok, sub, count), grid_s...  32.3 us
    pallas_call x1, Pallas kernels, attention_bwd(): pl.pallas_call(functools.partial(bwd_kernel, heads, length, block), grid=...  30.8 us
    unnamed x51, local copies, waits for them, and re-layouts  28.9 us
  transfers between devices with their start and end apart: 5, of which 2 were waited for; matrix products, arithmetic and copies ran while one was open for 8% of the time, Pallas kernels for 42%

profile of v2, /device:TPU:0, one launch (start us, length us, event | category | flops | bytes accessed | tf_op | source)
XLA Modules:
  0.0 821.8 jit_solution(909612135761766793)
XLA Ops:
  7.3 1.5 dynamic-slice_convert_fusion.3
  8.8 1.4 copy.111
  10.3 3.4 fusion.3
  14.0 2.0 convolution_convert_fusion
  22.0 19.6 %attn_fwd.1.x_ref = f32[2048,128]{1,0:T(8,128)} custom-call(f32[64]{0:T(128)} %reshape.135.rb_ref, bf16[2048,128]{1,0:T(8,128)(2,1)} %copy.113.q_ref, bf16[2048,128]{1,0:T(8,128)(2,1)} %copy.114.k_ref, bf16[128,2048]{1,0:T(8,128)(2,1)} %get-tuple-element.127.vt_ref, s32[2,1,1024]{2,1,0:T(1,128)} %reshape.128.segr_ref, s32[2048,1]{1,0:T(8,128)} %bitcast.97), custom_call_target="tpu_custom_call" | custom-call | flops 1073741824 | bytes 2621440 | tf_op jit(solution)/shard_map/attn_fwd/pallas_call | solution.py:198
  41.6 12.5 %all-gather.4.cloned.1.call-done = f32[1024,256]{1,0:T(8,128)} async-done(((f32[128,256]{1,0:T(8,128)}), f32[1024,256]{1,0:T(8,128)}) %all-gather.4.cloned.1.call-update) | async-done | bytes 1048592 | tf_op jit(solution)/shard_map/all_gather | solution.py:1069
  56.1 1.7 select_reduce_fusion
  57.8 2.7 fusion.29
  62.8 1.6 add_select_fusion.tgt_col
  65.3 82.8 %gather_columns.1 = f32[2048,1024]{1,0:T(8,128)S(1)} custom-call(f32[2048,128]{1,0:T(8,128)S(1)} %copy-done.2), custom_call_target="tpu_custom_call" | custom-call | bytes 270000000 | tf_op jit(solution)/shard_map/gather_columns/pallas_call | solution.py:521
  148.2 3.4 copy-done.1
  151.6 11.2 %multiply_reduce_fusion = (f32[2048]{0:T(1024)S(1)}, f32[2048,1024]{1,0:T(8,128)S(1)}) fusion(f32[2048,1024]{1,0:T(8,128)} %copy-done.1, f32[1024,1024]{1,0:T(8,128)} %all-gather.6.cloned.1.call-done, f32[]{:T(128)} %bitcast.9, bf16[2048,1024]{1,0:T(8,128)(2,1)} %param.13), kind=kOutput, calls=%fused_computation.12 | convolution fusion | flops 4304402432 | bytes 25174020 | tf_op jit(solution)/shard_map/dot_general | solution.py:1081
  166.1 1.9 broadcast_in_dim.30.rest_0_
  168.1 23.8 %dispatch.1 = (bf16[4608,1024]{1,0:T(8,128)(2,1)}, f32[4608,128]{1,0:T(8,128)}) custom-call(s32[4096]{0:T(1024)} %bitcast.104, bf16[2048,1024]{1,0:T(8,128)(2,1)} %copy-done.4, f32[4096,128]{1,0:T(8,128)} %broadcast_in_dim.30.rest_0_), custom_call_target="tpu_custom_call" | custom-call | bytes 67108864 | tf_op jit(solution)/shard_map/dispatch/pallas_call | solution.py:739
  191.9 32.3 %experts_forward.1 = (f32[8,576,352]{2,1,0:T(8,128)}, f32[8,576,352]{2,1,0:T(8,128)}, bf16[8,576,352]{2,1,0:T(8,128)(2,1)}, f32[2048,1024]{1,0:T(8,128)}) custom-call(s32[4096]{0:T(1024)} %bitcast.105, bf16[4608,1024]{1,0:T(8,128)(2,1)} %get-tuple-element.42.x, f32[4608,128]{1,0:T(8,128)} %get-tuple-element.41.sh, bf16[8,2,352,1024]{3,2,1,0:T(8,128)(2,1)} %bitcast.89, ...), custom_call_target="tpu_custom_call" | custom-call | flops 9965666304 | bytes 104857600 | tf_op jit(solution)/shard_map/experts_forward/pallas_call | solution.py:796
  224.2 136.3 %experts_backward.1 = (bf16[4608,1024]{1,0:T(8,128)(2,1)}, bf16[8,2,576,352]{3,2,1,0:T(8,128)(2,1)}, f32[2048,1024]{1,0:T(8,128)}, f32[2048,128]{1,0:T(8,128)}, f32[256,1024]{1,0:T(8,128)}) custom-call(bf16[2048,1024]{1,0:T(8,128)(2,1)} %cot.1, s32[2,2048]{1,0:T(2,128)} %copy-done.14, s32[2048,2]{1,0:T(8,128)} %copy-done.6, ...), custom_call_target="tpu_custom_call" | custom-call | bytes 270000000 | tf_op jit(solution)/shard_map/experts_backward/pallas_call | solution.py:896
  360.5 1.6 copy.119
  362.7 96.3 %experts_weights.1 = (f32[1,8,3,352,256]{4,3,2,1,0:T(8,128)}, f32[1,8,3,352,256]{4,3,2,1,0:T(8,128)}, f32[256,1024]{1,0:T(8,128)}, f32[8,256]{1,0:T(8,128)}) custom-call(bf16[4608,1024]{1,0:T(8,128)(2,1)} %get-tuple-element.42.x, bf16[4608,1024]{1,0:T(8,128)(2,1)} %get-tuple-element.48.y, f32[4608,128]{1,0:T(8,128)} %get-tuple-element.41.sh, ...), custom_call_target="tpu_custom_call" | custom-call | bytes 270000000 | tf_op jit(solution)/shard_map/experts_weights/pallas_call | solution.py:999
  459.1 1.7 collective-permute-start
  462.4 2.5 multiply_reduce_fusion.1
  464.9 1.4 subtract_add_fusion.up_ref
  468.2 3.6 all-to-all-start
  475.5 4.0 fusion.32.ou_ref
  479.5 44.2 %all-to-all-done = f32[8,256,128]{2,1,0:T(8,128)S(1)} async-done(((f32[8,256,128]{2,1,0:T(8,128)}), f32[8,256,128]{2,1,0:T(8,128)S(1)}, u32[]{:S(2)}, u32[]{:S(2)}) %all-to-all-start) | async-done | bytes 1048608 | tf_op jit(solution)/shard_map/all_to_all | solution.py:1120
  524.6 30.8 %attn_bwd.1 = (bf16[2048,128]{1,0:T(8,128)(2,1)}, bf16[2048,128]{1,0:T(8,128)(2,1)}, bf16[2048,128]{1,0:T(8,128)(2,1)}, f32[2,32,128]{2,1,0:T(8,128)}) custom-call(f32[64]{0:T(128)} %reshape.135.rb_ref, bf16[2048,128]{1,0:T(8,128)(2,1)} %copy.113.q_ref, bf16[2048,128]{1,0:T(8,128)(2,1)} %copy.114.k_ref, bf16[2048,128]{1,0:T(8,128)(2,1)} %copy.123.v_ref, ...), custom_call_target="tpu_custom_call" | custom-call | flops 2684354560 | bytes 5242880 | tf_op jit(solution)/shard_map/attn_bwd/pallas_call | solution.py:220
  560.0 5.7 fusion.51.part_ref
  565.8 2.6 fusion.26.in_ref
  568.3 214.0 %reduce_norm_gather.1 = (f32[2048,1024]{1,0:T(8,128)}, f32[16,256]{1,0:T(8,128)S(1)}, f32[256,384]{1,0:T(8,128)S(1)}, f32[128,256]{1,0:T(8,128)S(1)}) custom-call(f32[2048,1024]{1,0:T(8,128)} %fusion.51.part_ref, f32[256,1024]{1,0:T(8,128)S(1)} %dynamic-slice_convert_fusion.2.val_ref, f32[256,1024]{1,0:T(8,128)S(1)} %subtract_add_fusion.up_ref, ...), custom_call_target="tpu_custom_call" | custom-call | bytes 540000000 | tf_op jit(solution)/shard_map/reduce_norm_gather/pallas_call | solution.py:638
  785.2 4.6 fusion.13
  789.8 7.7 fusion.8
  797.5 8.4 %copy.146 = f32[2048,1024]{1,0:T(8,128)} copy(f32[2048,1024]{1,0:T(8,128)} %all-gather.8.cloned.1.call-done) | data formatting | bytes 16777216
  806.0 8.4 %copy.147 = f32[2048,1024]{1,0:T(8,128)} copy(f32[2048,1024]{1,0:T(8,128)} %get-tuple-element.153) | data formatting | bytes 16777216
  (110 shorter events, 31.0 us)
Async XLA Ops:
  7.2 156.5 %copy-start = (bf16[1024,8]{0,1:T(8,128)(2,1)S(1)}, bf16[1024,8]{0,1:T(8,128)(2,1)}, u32[]{:S(2)}) copy-start(bf16[1024,8]{0,1:T(8,128)(2,1)} %param.20) | copy-start | bytes 49156
  7.2 6.5 copy-start.3
  7.2 46.8 %all-gather.4.cloned.1.call-start = ((), (), s32[]{:S(2)}) async-start(), calls=%async_computation.1 | async-start | bytes 1179648 | tf_op jit(solution)/shard_map/all_gather | solution.py:1069
  8.8 142.8 %all-gather.6.cloned.1.call-start = ((), (), s32[]{:S(2)}) async-start(), calls=%async_computation.2 | async-start | bytes 5242880 | tf_op jit(solution)/shard_map/all_gather | solution.py:1079
  10.3 5.7 copy-start.10
  10.3 3.7 copy-start.7
  16.0 3.3 copy-start.17
  16.0 5.3 copy-start.18
  22.0 32.6 %copy-start.19 = (s32[1,2048]{1,0:T(1,128)S(1)}, s32[1,2048]{1,0:T(1,128)}, u32[]{:S(2)}) copy-start(s32[1,2048]{1,0:T(1,128)} %param.25) | copy-start | bytes 24580
  22.0 33.9 %copy-start.15 = (s32[2048,2]{0,1:T(2,128)S(1)}, s32[2048,2]{0,1:T(2,128)}, u32[]{:S(2)}) copy-start(s32[2048,2]{0,1:T(2,128)} %param.24) | copy-start | bytes 49156
  54.0 743.5 %all-gather.8.cloned.1.call-start = ((), (), s32[]{:S(2)}) async-start(), calls=%async_computation.3 | async-start | bytes 9437184 | tf_op jit(solution)/shard_map/all_gather | solution.py:1105
  60.5 4.8 copy-start.2
  64.4 83.8 %copy-start.6 = (s32[2048,2]{1,0:T(8,128)}, s32[2048,2]{1,0:T(8,128)S(1)}, u32[]{:S(2)}) copy-start(s32[2048,2]{1,0:T(8,128)S(1)} %add_select_fusion.tgt_col) | copy-start | bytes 49156
  64.7 83.5 %copy-start.14 = (s32[2,2048]{1,0:T(2,128)}, s32[2,2048]{1,0:T(2,128)S(1)}, u32[]{:S(2)}) copy-start(s32[2,2048]{1,0:T(2,128)S(1)} %copy.117.tgt_row) | copy-start | bytes 49156
  148.2 3.4 copy-start.1
  151.6 11.2 %copy-start.16 = (f32[1024]{0:T(1024)S(1)}, f32[1024]{0:T(1024)}, u32[]{:S(2)}) copy-start(f32[1024]{0:T(1024)} %param.16) | copy-start | bytes 12292
  163.7 2.4 copy-start.4
  459.0 5.8 copy-start.5
  459.1 7.2 copy-start.9
  459.1 326.1 %collective-permute-start = (f32[1,8,3,352,256]{4,3,2,1,0:T(8,128)}, f32[1,8,3,352,256]{4,3,2,1,0:T(8,128)}, u32[]{:S(2)}, u32[]{:S(2)}) collective-permute-start(f32[1,8,3,352,256]{4,3,2,1,0:T(8,128)} %get-tuple-element.67), channel_id=1, source_target_pairs={{0,16},{8,24},{16,0},{24,8},{1,17},{9,25},{17,1},{25,9},{2,18},{10... | collective-permute-start | bytes 25952264 | tf_op jit(solution)/shard_map/ppermute | solution.py:1058
  466.3 5.5 copy-start.12
  468.2 55.5 %all-to-all-start = ((f32[8,256,128]{2,1,0:T(8,128)}), f32[8,256,128]{2,1,0:T(8,128)S(1)}, u32[]{:S(2)}, u32[]{:S(2)}) async-start(f32[8,256,128]{2,1,0:T(8,128)} %bitcast.85), calls=%async_computation | async-start | bytes 2097152 | tf_op jit(solution)/shard_map/all_to_all | solution.py:1120
  523.7 1.0 copy-start.13
  524.6 35.4 %copy-start.11 = (bf16[1024,3,128]{0,2,1:T(8,128)(2,1)S(1)}, bf16[1024,3,128]{0,2,1:T(8,128)(2,1)}, u32[]{:S(2)}) copy-start(bf16[1024,3,128]{0,2,1:T(8,128)(2,1)} %copy-done.10) | copy-start | bytes 2359300
  560.0 5.8 copy-start.8
Sparse Core Ops, SparseCore 0:
  10.7 43.2 all-gather.3
  55.6 32.9 all-gather.5
  459.2 251.7 all-gather.7

commit v3 on v2

--- a/solution.py
+++ b/solution.py
@@ -468,9 +468,11 @@
 
 
 def on_steps(step, events, share, last):
-    done = 0
+    due, done, total = [], 0, 0.0
     for i in range(last):
-        upto = min(int(share * (i + 1)), len(events))
+        total += share[0] if i < 8 else share[1]
+        due.append(min(int(total), len(events)))
+    for i, upto in enumerate(due):
         if upto > done:
             @pl.when(step == i)
             def _():
@@ -666,88 +668,6 @@
     return ref.at[pl.ds(pl.multiple_of(row * sub, sub), sub), :]
 
 
-def dispatch_kernel(tok, sub, step_slots, with_share, tgt, src, *rest):
-    if with_share:
-        share, out, share_out, rows_in, rows_out, share_rows = rest
-    else:
-        out, rows_in, rows_out = rest
-    step = pl.program_id(0)
-
-    @pl.when(step == 0)
-    def _():
-        def load(i, c):
-            t0 = pl.multiple_of(i * 64, 64)
-            spread(rows_in, t0, sub, src.at[pl.ds(t0, 64), :], 64)
-            return c
-
-        lax.fori_loop(0, tok // 64, load, 0)
-
-        def zero(i, c):
-            r0 = pl.multiple_of(i * 8 * sub, 8 * sub)
-            rows_out[pl.ds(r0, 8 * sub), :] = jnp.zeros((8 * sub, LN), F32)
-            if with_share:
-                share_rows[pl.ds(pl.multiple_of(i * 8, 8), 8), :] = jnp.zeros((8, LN), F32)
-            return c
-
-        lax.fori_loop(0, SLOTS // 8, zero, 0)
-
-        def move(i, c):
-            for u in range(8):
-                t = i * 8 + u
-                row = tile(rows_in, t, sub)[...]
-                for choice in range(2):
-                    slot = tgt[choice * tok + t]
-                    tile(rows_out, slot, sub)[...] = row
-                    if with_share:
-                        share_rows[pl.ds(slot, 1), :] = share[pl.ds(choice * tok + t, 1), :]
-            return c
-
-        lax.fori_loop(0, tok // 8, move, 0)
-
-    base = step * step_slots
-
-    def emit(i, c):
-        s0 = pl.multiple_of(i * 64, 64)
-        for j in range(sub):
-            out[pl.ds(s0, 64), j * LN:(j + 1) * LN] = rows_out[pl.ds((base + s0) * sub + j, 64, stride=sub), :].astype(BF16)
-        return c
-
-    lax.fori_loop(0, step_slots // 64, emit, 0)
-    if with_share:
-        share_out[...] = share_rows[pl.ds(pl.multiple_of(base, step_slots), step_slots), :]
-
-
-def dispatch(tgt, src, share=None, step_slots=512):
-    tok, width = src.shape
-    sub = width // LN
-    ws = share is not None
-
-    def whole(shape):
-        return pl.BlockSpec(shape, lambda i, t: (0, 0), pipeline_mode=pl.Buffered(1))
-
-    out_shape = [jax.ShapeDtypeStruct((SLOTS, width), BF16)]
-    out_specs = [pl.BlockSpec((step_slots, width), lambda i, t: (i, 0))]
-    scratch = [pltpu.VMEM((tok * sub, LN), F32), pltpu.VMEM(((SLOTS + 1) * sub, LN), F32)]
-    in_specs = [whole((tok, width))]
-    args = [src]
-    if ws:
-        in_specs.append(whole((2 * tok, LN)))
-        args.append(share)
-        out_shape.append(jax.ShapeDtypeStruct((SLOTS, LN), F32))
-        out_specs.append(pl.BlockSpec((step_slots, LN), lambda i, t: (i, 0)))
-        scratch.append(pltpu.VMEM((SLOTS + 8, LN), F32))
-    r = pl.pallas_call(
-        functools.partial(dispatch_kernel, tok, sub, step_slots, ws),
-        grid_spec=pltpu.PrefetchScalarGridSpec(num_scalar_prefetch=1, grid=(SLOTS // step_slots,), in_specs=in_specs,
-                                               out_specs=out_specs, scratch_shapes=scratch),
-        out_shape=out_shape,
-        compiler_params=pltpu.CompilerParams(vmem_limit_bytes=56 << 20),
-        cost_estimate=pl.CostEstimate(flops=0, bytes_accessed=64 << 20, transcendentals=0),
-        name="dispatch",
-    )(tgt, *args)
-    return r if ws else r[0]
-
-
 def combine_rows(tgt, rows, mix, out, tok, sub, t0, count):
     def body(i, c):
         for u in range(8):
@@ -766,53 +686,91 @@
     return pl.BlockSpec(shape, lambda i, *t: (jnp.minimum(i, EXPERTS - 1),) + (0,) * (len(shape) - 1))
 
 
-def forward_kernel(tok, sub, count, tgt, x, sh, win, wdn, gate, up, act, mo, rows, mix):
+def whole(shape):
+    return pl.BlockSpec(shape, lambda i, *t: (0,) * len(shape), pipeline_mode=pl.Buffered(1))
+
+
+def forward_kernel(tok, sub, count, tgt, held, src, share, win, wdn, x, sh, gate, up, act, mo, rows_in, rows, shares, mix):
     step = pl.program_id(0)
+    row0 = pl.multiple_of(step * CAP, 8)
 
     @pl.when(step == 0)
     def _():
         rows[SLOTS * sub:, :] = jnp.zeros((sub, LN), F32)
 
+        def load(i, c):
+            t0 = pl.multiple_of(i * 64, 64)
+            spread(rows_in, t0, sub, src.at[pl.ds(t0, 64), :], 64)
+            return c
+
+        lax.fori_loop(0, tok // 64, load, 0)
+
+        def move(i, c):
+            for u in range(8):
+                t = i * 8 + u
+                row = tile(rows_in, t, sub)[...]
+                for choice in range(2):
+                    slot = tgt[choice * tok + t]
+                    tile(rows, slot, sub)[...] = row
+                    shares[pl.ds(slot, 1), :] = share[pl.ds(choice * tok + t, 1), :]
+            return c
+
+        lax.fori_loop(0, tok // 8, move, 0)
+        rows[SLOTS * sub:, :] = jnp.zeros((sub, LN), F32)
+
+        for e in range(EXPERTS):
+            def clear(s, c):
+                tile(rows, e * CAP + s, sub)[...] = jnp.zeros((sub, LN), F32)
+                shares[pl.ds(e * CAP + s, 1), :] = jnp.zeros((1, LN), F32)
+                return c
+
+            lax.fori_loop(held[e], CAP, clear, 0)
+
     @pl.when(step < EXPERTS)
     def _():
+        for j in range(sub):
+            x[:, j * LN:(j + 1) * LN] = rows[pl.ds(row0 * sub + j, CAP, stride=sub), :].astype(BF16)
+        sh[...] = shares[pl.ds(row0, CAP), :]
         g = dot(x[...], win[0, 0], 1, 1)
         u = dot(x[...], win[0, 1], 1, 1)
         gate[0] = g
         up[0] = u
         a = (0.5 * g * (1.0 + jnp.tanh(GC * (g + 0.044715 * (g * g * g)))) * u).astype(BF16)
         act[0] = a
-        spread(rows, step * CAP, sub, dot(a, wdn[0], 1, 0) * sh[:, 0:1], CAP)
+        spread(rows, row0, sub, dot(a, wdn[0], 1, 0) * sh[:, 0:1], CAP)
 
     @pl.when(step >= EXPERTS)
     def _():
         combine_rows(tgt, rows, mix, mo, tok, sub, (step - EXPERTS) * count, count)
 
 
-def experts_forward(tgt, x, sh, win, wdn, tok, count=256):
-    width = x.shape[1]
+def experts_forward(tgt, held, src, share, win, wdn, count=256):
+    tok, width = src.shape
     sub = width // LN
     ff = wdn.shape[1]
     mid = by_expert((1, CAP, ff))
     return pl.pallas_call(
         functools.partial(forward_kernel, tok, sub, count),
         grid_spec=pltpu.PrefetchScalarGridSpec(
-            num_scalar_prefetch=1, grid=(EXPERTS + tok // count,),
-            in_specs=[by_expert((CAP, width)), by_expert((CAP, LN)), by_expert((1, 2, ff, width)), by_expert((1, ff, width))],
-            out_specs=[mid, mid, mid, pl.BlockSpec((count, width), lambda i, t: (jnp.maximum(i - EXPERTS, 0), 0))],
-            scratch_shapes=[pltpu.VMEM(((SLOTS + 1) * sub, LN), F32), pltpu.VMEM((count * sub, LN), F32)]),
-        out_shape=[jax.ShapeDtypeStruct((EXPERTS, CAP, ff), F32)] * 2
+            num_scalar_prefetch=2, grid=(EXPERTS + tok // count,),
+            in_specs=[whole(src.shape), whole(share.shape), by_expert((1, 2, ff, width)), by_expert((1, ff, width))],
+            out_specs=[by_expert((CAP, width)), by_expert((CAP, LN)), mid, mid, mid,
+                       pl.BlockSpec((count, width), lambda i, *t: (jnp.maximum(i - EXPERTS, 0), 0))],
+            scratch_shapes=[pltpu.VMEM((tok * sub, LN), F32), pltpu.VMEM(((SLOTS + 1) * sub, LN), F32),
+                            pltpu.VMEM((SLOTS + 8, LN), F32), pltpu.VMEM((count * sub, LN), F32)]),
+        out_shape=[jax.ShapeDtypeStruct((SLOTS, width), BF16), jax.ShapeDtypeStruct((SLOTS, LN), F32)]
+        + [jax.ShapeDtypeStruct((EXPERTS, CAP, ff), F32)] * 2
         + [jax.ShapeDtypeStruct((EXPERTS, CAP, ff), BF16), jax.ShapeDtypeStruct((tok, width), F32)],
-        compiler_params=pltpu.CompilerParams(vmem_limit_bytes=60 << 20),
-        cost_estimate=pl.CostEstimate(flops=6 * SLOTS * width * ff, bytes_accessed=100 << 20, transcendentals=SLOTS * ff),
+        compiler_params=pltpu.CompilerParams(vmem_limit_bytes=62 << 20),
+        cost_estimate=pl.CostEstimate(flops=6 * SLOTS * width * ff, bytes_accessed=120 << 20, transcendentals=SLOTS * ff),
         name="experts_forward",
-    )(tgt, x, sh, win, wdn)
+    )(tgt, held, src, share, win, wdn)
 
 
 def backward_kernel(tok, chunk, ring, share, cot, tgt_row, tgt_col, sh, gate, up, act, win, wdn, part, hid,
-                    y, dgu, mi, sg, res, acc, acc_sem, *scratch):
+                    y, dgu, mi, sg, res, dxs, aux, mask, *scratch):
     step = pl.program_id(0)
-    width = cot.shape[1]
-    first = step * CAP
+    last = EXPERTS + tok // chunk - 1
     ring.place()
     reduce = Reduce(ring, part, scratch)
 
@@ -820,49 +778,57 @@
     def _():
         ring.barrier()
         reduce.start()
-        acc[...] = jnp.zeros_like(acc)
-        sg[...] = jnp.zeros_like(sg)
-
-    slot = lax.broadcasted_iota(jnp.int32, (CAP, chunk), 0) + first
-
-    def fetch(i, rows):
-        t0 = pl.multiple_of(i * chunk, chunk)
-        held = (tgt_row[0:1, pl.ds(t0, chunk)] == slot) | (tgt_row[1:2, pl.ds(t0, chunk)] == slot)
-        return rows + dot(jnp.where(held, 1.0, 0.0).astype(BF16), cot[pl.ds(t0, chunk), :], 1, 0)
-
-    rows = lax.fori_loop(0, tok // chunk, fetch, jnp.zeros((CAP, width), F32)).astype(BF16)
-    y[...] = rows
-    h = dot(rows, wdn[0], 1, 1)
-    g, u = gate[0], up[0]
-    g2 = g * g
-    t = jnp.tanh(GC * (g + 0.044715 * g2 * g))
-    half = 0.5 * (1.0 + t)
-    sgrow = jnp.sum(act[0].astype(F32) * h, axis=1, keepdims=True)
-    da = sh[:, 0:1] * h
-    slope = half + (0.5 * GC) * g * (1.0 - t * t) * (1.0 + (3 * 0.044715) * g2)
-    dg = (da * u * slope).astype(BF16)
-    du = (da * (g * half)).astype(BF16)
-    dgu[0, 0] = dg
-    dgu[0, 1] = du
-    dx = (dot(dg, win[0, 0], 1, 0) + dot(du, win[0, 1], 1, 0)).astype(BF16)
-    lane = lax.broadcasted_iota(jnp.int32, (CAP, LN), 1)
-    high = sgrow.astype(BF16).astype(F32)
-    aux = jnp.where(lane == 0, high, jnp.where(lane == 1, sgrow - high, 0.0)).astype(BF16)
-    slots = lax.broadcasted_iota(jnp.int32, (chunk, CAP), 1) + first
-    lanes = lax.broadcasted_iota(jnp.int32, (chunk, LN), 1)
-
-    def hand_back(i, c):
-        t0 = pl.multiple_of(i * chunk, chunk)
+
+    @pl.when(step < EXPERTS)
+    def _():
+        first = pl.multiple_of(step * CAP, 8)
+        slot = lax.broadcasted_iota(jnp.int32, (CAP, LN), 0) + first
+
+        def fill(i, c):
+            t0 = pl.multiple_of(i * LN, LN)
+            held = (tgt_row[0:1, pl.ds(t0, LN)] == slot) | (tgt_row[1:2, pl.ds(t0, LN)] == slot)
+            mask[:, pl.ds(t0, LN)] = jnp.where(held, 1.0, 0.0).astype(BF16)
+            return c
+
+        lax.fori_loop(0, tok // LN, fill, 0)
+        rows = dot(mask[...], cot[...], 1, 0).astype(BF16)
+        y[...] = rows
+        h = dot(rows, wdn[0], 1, 1)
+        g, u = gate[0], up[0]
+        g2 = g * g
+        t = jnp.tanh(GC * (g + 0.044715 * g2 * g))
+        half = 0.5 * (1.0 + t)
+        sgrow = jnp.sum(act[0].astype(F32) * h, axis=1, keepdims=True)
+        da = sh[:, 0:1] * h
+        slope = half + (0.5 * GC) * g * (1.0 - t * t) * (1.0 + (3 * 0.044715) * g2)
+        dg = (da * u * slope).astype(BF16)
+        du = (da * (g * half)).astype(BF16)
+        dgu[0, 0] = dg
+        dgu[0, 1] = du
+        dxs[pl.ds(first, CAP), :] = (dot(dg, win[0, 0], 1, 0) + dot(du, win[0, 1], 1, 0)).astype(BF16)
+        lane = lax.broadcasted_iota(jnp.int32, (CAP, LN), 1)
+        high = sgrow.astype(BF16).astype(F32)
+        low = jnp.where(lane == 2 * step + 1, sgrow - high, 0.0)
+        aux[pl.ds(first, CAP), :] = jnp.where(lane == 2 * step, high, low).astype(BF16)
+
+    @pl.when(step >= EXPERTS)
+    def _():
+        t0 = pl.multiple_of((step - EXPERTS) * chunk, chunk)
+        span = 4 * CAP
+        slots = lax.broadcasted_iota(jnp.int32, (chunk, span), 1)
         one, two = tgt_col[pl.ds(t0, chunk), 0:1], tgt_col[pl.ds(t0, chunk), 1:2]
-        held = jnp.where((one == slots) | (two == slots), 1.0, 0.0).astype(BF16)
-        acc[pl.ds(t0, chunk), :] += dot(held, dx, 1, 0)
-        value = dot(held, aux, 1, 0)
-        value = value[:, 0:1] + value[:, 1:2]
-        pair = jnp.where(lanes == 0, one, jnp.where(lanes == 1, two, SLOTS))
-        sg[pl.ds(t0, chunk), :] += jnp.where((pair >= first) & (pair < first + CAP), value, 0.0)
-        return c
-
-    lax.fori_loop(0, tok // chunk, hand_back, 0)
+        rows = jnp.zeros((chunk, cot.shape[1]), F32)
+        value = jnp.zeros((chunk, LN), F32)
+        for s0 in range(0, SLOTS, span):
+            held = (one - s0 == slots) | (two - s0 == slots)
+            both = jnp.where(held, 1.0, 0.0).astype(BF16)
+            rows = rows + dot(both, dxs[s0:s0 + span, :], 1, 0)
+            value = value + dot(both, aux[s0:s0 + span, :], 1, 0)
+        mi[...] = rows
+        lane = lax.broadcasted_iota(jnp.int32, (chunk, LN), 1)
+        low = lax.div(lane, 2) * CAP
+        sums = [jnp.sum(jnp.where((c >= low) & (c < low + CAP), value, 0.0), axis=1, keepdims=True) for c in (one, two)]
+        sg[...] = jnp.where(lane == 0, sums[0], sums[1])
 
     def done_a(p, value):
         row, n = ring.pieces[p]
@@ -871,36 +837,32 @@
     def done_b(value):
         res[pl.ds(ring.rows_a, ring.rows_b), :] = value + hid[pl.ds(ring.rows_a, ring.rows_b), :]
 
-    @pl.when(step == EXPERTS - 1)
-    def _():
-        pltpu.make_async_copy(acc, mi, acc_sem).start()
-
-    on_steps(step, reduce.events(done_a, done_b), share, EXPERTS - 1)
-
-    @pl.when(step == EXPERTS - 1)
-    def _():
-        pltpu.make_async_copy(acc, mi, acc_sem).wait()
+    on_steps(step, reduce.events(done_a, done_b), share, last)
+
+    @pl.when(step == last)
+    def _():
         reduce.finish()
 
 
-def whole(shape):
-    return pl.BlockSpec(shape, lambda i, *t: (0,) * len(shape), pipeline_mode=pl.Buffered(1))
-
-
-def experts_backward(tgt, cot, sh, gate, up, act, win, wdn, part, hid, n, cid, chunk=512, share=1.6):
+def experts_backward(tgt, cot, sh, gate, up, act, win, wdn, part, hid, n, cid, chunk=256, share=(1.4, 0.65)):
     tok, width = part.shape
     ff = wdn.shape[1]
     ring = Ring(n, tok // n)
     mid = by_expert((1, CAP, ff))
     tgt_row = tgt.reshape(2, tok)
+
+    def by_chunk(lanes):
+        return pl.BlockSpec((chunk, lanes), lambda i: (jnp.maximum(i - EXPERTS, 0), 0))
+
     return pl.pallas_call(
         functools.partial(backward_kernel, tok, chunk, ring, share),
-        grid=(EXPERTS,),
+        grid=(EXPERTS + tok // chunk,),
         in_specs=[whole(cot.shape), whole((2, tok)), whole((tok, 2)), by_expert((CAP, LN)), mid, mid, mid,
                   by_expert((1, 2, ff, width)), by_expert((1, ff, width)), whole(part.shape), whole(hid.shape)],
-        out_specs=[by_expert((CAP, width)), by_expert((1, 2, CAP, ff)), pl.BlockSpec(memory_space=pl.ANY),
-                   pl.BlockSpec((tok, LN), lambda i: (0, 0)), pl.BlockSpec(hid.shape, lambda i: (0, 0))],
-        scratch_shapes=[pltpu.VMEM((tok, width), F32), pltpu.SemaphoreType.DMA] + ring.reduce_scratch(width),
+        out_specs=[by_expert((CAP, width)), by_expert((1, 2, CAP, ff)), by_chunk(width), by_chunk(LN),
+                   pl.BlockSpec(hid.shape, lambda i: (0, 0))],
+        scratch_shapes=[pltpu.VMEM((SLOTS, width), BF16), pltpu.VMEM((SLOTS, LN), BF16), pltpu.VMEM((CAP, tok), BF16)]
+        + ring.reduce_scratch(width),
         out_shape=[jax.ShapeDtypeStruct((SLOTS, width), BF16), jax.ShapeDtypeStruct((EXPERTS, 2, CAP, ff), BF16),
                    jax.ShapeDtypeStruct((tok, width), F32), jax.ShapeDtypeStruct((tok, LN), F32),
                    jax.ShapeDtypeStruct(hid.shape, F32)],
@@ -986,7 +948,7 @@
         reduce.finish()
 
 
-def experts_weights(x, y, sh, act, dgu, part, small, n, parts, cid, share=1.3):
+def experts_weights(x, y, sh, act, dgu, part, small, n, parts, cid, share=(1.3, 0)):
     tok, width = part.shape
     ff = act.shape[2]
     wide = width // parts
@@ -1023,7 +985,8 @@
     first = jnp.sum(onehot[:, 0].astype(F32), axis=0)
     before = before + jnp.stack([jnp.zeros((EXPERTS,), F32), first])[None]
     slot = jnp.sum(before * onehot.astype(F32), axis=2).astype(jnp.int32)
-    return jnp.where(slot < CAP, routes * CAP + slot, SLOTS).T.reshape(-1)
+    held = jnp.minimum(jnp.sum(onehot.astype(F32), axis=(0, 1)), CAP).astype(jnp.int32)
+    return jnp.where(slot < CAP, routes * CAP + slot, SLOTS).T.reshape(-1), held
 
 
 EPSILON = 1e-06
@@ -1073,9 +1036,9 @@
         q, k, v = (qkv[:, i * lanes:(i + 1) * lanes] for i in range(3))
         rb = rel_bias.astype(F32).reshape(-1)
         attended = attention_fwd(q, k, v.T, segment_ids, rb)
-        tgt = slot_targets(routes, order[0])
-
-        attended, w_out_rows = lax.optimization_barrier((attended, w_out_rows))
+        tgt, held = slot_targets(routes, order[0])
+
+        attended, w_out_rows, tgt, held = lax.optimization_barrier((attended, w_out_rows, tgt, held))
         w_out_all = lax.all_gather(w_out_rows, "dp", axis=1, tiled=True) * one
         attended_all = gather_columns(attended, n_tensor, 0)
         hidden_one = x + jnp.dot(attended_all, w_out_all, preferred_element_type=F32)
@@ -1090,9 +1053,9 @@
 
         soft, chosen, both = route(logits, picked)
         pair_share = chosen / both
-        xs, slot_share = dispatch(tgt, moe_input, jnp.broadcast_to(pair_share.T.reshape(-1, 1), (2 * tok, LN)))
         w_in_t = jnp.swapaxes(w_in, 2, 3)
-        gate, up, act, moe_part = experts_forward(tgt, xs, slot_share, w_in_t, w_down, tok)
+        share_rep = jnp.broadcast_to(pair_share.T.reshape(-1, 1), (2 * tok, LN))
+        xs, slot_share, gate, up, act, moe_part = experts_forward(tgt, held, moe_input, share_rep, w_in_t, w_down)
         hidden_s = own(hidden_one)
         y, gate_up_grad, moe_in_part, share_part, result_s = experts_backward(
             tgt, cotangent, slot_share, gate, up, act, w_in_t, w_down, moe_part, hidden_s, n_tensor, 1)

time: 828 us -> 778 us (0.940)
  Pallas kernels: 636 us -> 592 us
    pallas_call x1, Pallas kernels: 136 us -> 99.4 us  [experts_backward(): pl.pallas_call(functools.partial(backward_kernel, tok, chunk, ring, share...]
    pallas_call x1 -> x0, Pallas kernels: 23.8 us -> none  [dispatch(): pl.pallas_call(functools.partial(dispatch_kernel, tok, sub, step_slots, w...]
    pallas_call x1, Pallas kernels: 32.3 us -> 47.5 us  [experts_forward(): pl.pallas_call(functools.partial(forward_kernel, tok, sub, count), grid_s...]
    unnamed x51 -> x45, local copies, waits for them, and re-layouts: 28.9 us -> 28.4 us
  transfers between devices with their start and end apart: 5 -> 5, of which waited for: 2 -> 2; matrix products, arithmetic and copies ran while one was open for 8% -> 8% of each run, Pallas kernels for 42% -> 45%
where the time goes in v3:
time: 778 us; the launch traced here: 769 us
  Pallas kernels  592 us (76%)
  waiting for transfers between devices  50.5 us (6%)
  local copies, waits for them, and re-layouts  45.3 us (6%)
  matrix products  34.1 us (4%)
  other arithmetic  26 us (3%)
  between operations  15.1 us (2%)
    pallas_call x1, Pallas kernels, reduce_norm_gather(): pl.pallas_call(kernel, out_shape=[jax.ShapeDtypeStruct(s, F32) for s in (...  214 us
    pallas_call x1, Pallas kernels, experts_backward(): pl.pallas_call(functools.partial(backward_kernel, tok, chunk, ring, share...  99.4 us
    pallas_call x1, Pallas kernels, experts_weights(): pl.pallas_call(functools.partial(weights_kernel, parts, ring, n, share),...  97 us
    pallas_call x1, Pallas kernels, gather_columns(): pl.pallas_call(kernel, out_shape=jax.ShapeDtypeStruct(shape, F32), in_spe...  83.2 us
    pallas_call x1, Pallas kernels, experts_forward(): pl.pallas_call(functools.partial(forward_kernel, tok, sub, count), grid_s...  47.5 us
    all_to_all x1, waiting for transfers between devices, layer(): lax.all_to_all(pieces, 'tensor', 0, 0, tiled=False).reshape(tok, lanes)  43.4 us
    pallas_call x1, Pallas kernels, attention_bwd(): pl.pallas_call(functools.partial(bwd_kernel, heads, length, block), grid=...  30.8 us
    unnamed x45, local copies, waits for them, and re-layouts  28.4 us
  transfers between devices with their start and end apart: 5, of which 2 were waited for; matrix products, arithmetic and copies ran while one was open for 8% of the time, Pallas kernels for 45%

profile of v3, /device:TPU:0, one launch (start us, length us, event | category | flops | bytes accessed | tf_op | source)
XLA Modules:
  0.0 769.0 jit_solution(8556628216577123913)
XLA Ops:
  7.3 1.5 dynamic-slice_convert_fusion.3
  8.8 1.4 copy.54
  10.3 3.2 fusion.3
  13.7 1.9 convolution_convert_fusion
  22.0 1.7 select_reduce_fusion
  23.7 2.7 fusion.29
  26.5 19.6 %attn_fwd.1.x_ref = f32[2048,128]{1,0:T(8,128)} custom-call(f32[64]{0:T(128)} %reshape.139.rb_ref, bf16[2048,128]{1,0:T(8,128)(2,1)} %copy.56.q_ref, bf16[2048,128]{1,0:T(8,128)(2,1)} %copy.57.k_ref, bf16[128,2048]{1,0:T(8,128)(2,1)} %get-tuple-element.111.vt_ref, s32[2,1,1024]{2,1,0:T(1,128)} %reshape.130.segr_ref, s32[2048,1]{1,0:T(8,128)} %bitcast.99), custom_call_target="tpu_custom_call" | custom-call | flops 1073741824 | bytes 2621440 | tf_op jit(solution)/shard_map/attn_fwd/pallas_call | solution.py:198
  46.7 7.1 all-gather.4.cloned.1.call-done
  56.4 83.2 %gather_columns.1 = f32[2048,1024]{1,0:T(8,128)S(1)} custom-call(f32[2048,128]{1,0:T(8,128)S(1)} %copy-done.2), custom_call_target="tpu_custom_call" | custom-call | bytes 270000000 | tf_op jit(solution)/shard_map/gather_columns/pallas_call | solution.py:523
  139.7 3.4 copy-done.1
  143.1 1.4 copy.59
  144.5 11.2 %multiply_reduce_fusion = (f32[2048]{0:T(1024)S(1)}, f32[2048,1024]{1,0:T(8,128)S(1)}) fusion(f32[2048,1024]{1,0:T(8,128)} %copy-done.1, f32[1024,1024]{1,0:T(8,128)} %all-gather.6.cloned.1.call-done, f32[]{:T(128)} %bitcast.10, bf16[2048,1024]{1,0:T(8,128)(2,1)} %param.13), kind=kOutput, calls=%fused_computation.12 | convolution fusion | flops 4304402432 | bytes 25174020 | tf_op jit(solution)/shard_map/dot_general | solution.py:1044
  159.0 1.9 broadcast_in_dim.30.share
  160.9 47.5 %experts_forward.1 = (bf16[4608,1024]{1,0:T(8,128)(2,1)}, f32[4608,128]{1,0:T(8,128)}, f32[8,576,352]{2,1,0:T(8,128)}, f32[8,576,352]{2,1,0:T(8,128)}, bf16[8,57...) custom-call(s32[4096]{0:T(1024)} %bitcast.106, s32[8]{0:T(128)} %minimum_convert_fusion.held, bf16[2048,1024]{1,0:T(8,128)(2,1)} %copy-done.4, ...), custom_call_target="tpu_custom_call" | custom-call | flops 9965666304 | bytes 125829120 | tf_op jit(solution)/shard_map/experts_forward/pallas_call | solution.py:752
  208.5 99.4 %experts_backward.1 = (bf16[4608,1024]{1,0:T(8,128)(2,1)}, bf16[8,2,576,352]{3,2,1,0:T(8,128)(2,1)}, f32[2048,1024]{1,0:T(8,128)}, f32[2048,128]{1,0:T(8,128)}, f32[256,1024]{1,0:T(8,128)}) custom-call(bf16[2048,1024]{1,0:T(8,128)(2,1)} %cot.1, s32[2,2048]{1,0:T(2,128)} %copy-done.11, s32[2048,2]{1,0:T(8,128)} %bitcast.95, ...), custom_call_target="tpu_custom_call" | custom-call | bytes 270000000 | tf_op jit(solution)/shard_map/experts_backward/pallas_call | solution.py:857
  307.9 1.6 copy.62
  310.1 97.0 %experts_weights.1 = (f32[1,8,3,352,256]{4,3,2,1,0:T(8,128)}, f32[1,8,3,352,256]{4,3,2,1,0:T(8,128)}, f32[256,1024]{1,0:T(8,128)}, f32[8,256]{1,0:T(8,128)}) custom-call(bf16[4608,1024]{1,0:T(8,128)(2,1)} %get-tuple-element.51.x, bf16[4608,1024]{1,0:T(8,128)(2,1)} %get-tuple-element.52.y, f32[4608,128]{1,0:T(8,128)} %get-tuple-element.45.sh, ...), custom_call_target="tpu_custom_call" | custom-call | bytes 270000000 | tf_op jit(solution)/shard_map/experts_weights/pallas_call | solution.py:961
  407.1 1.5 collective-permute-start
  410.2 2.6 multiply_reduce_fusion.1
  412.8 1.4 subtract_add_fusion.up_ref
  416.1 4.3 all-to-all-start
  422.7 1.4 fusion.33
  424.1 4.0 fusion.32.ou_ref
  428.1 43.4 %all-to-all-done = f32[8,256,128]{2,1,0:T(8,128)} async-done(((f32[8,256,128]{2,1,0:T(8,128)}), f32[8,256,128]{2,1,0:T(8,128)}, u32[]{:S(2)}, u32[]{:S(2)}) %all-to-all-start) | async-done | bytes 1048608 | tf_op jit(solution)/shard_map/all_to_all | solution.py:1083
  471.5 30.8 %attn_bwd.1 = (bf16[2048,128]{1,0:T(8,128)(2,1)}, bf16[2048,128]{1,0:T(8,128)(2,1)}, bf16[2048,128]{1,0:T(8,128)(2,1)}, f32[2,32,128]{2,1,0:T(8,128)}) custom-call(f32[64]{0:T(128)} %reshape.139.rb_ref, bf16[2048,128]{1,0:T(8,128)(2,1)} %copy.56.q_ref, bf16[2048,128]{1,0:T(8,128)(2,1)} %copy.57.k_ref, bf16[2048,128]{1,0:T(8,128)(2,1)} %copy.66.v_ref, ...), custom_call_target="tpu_custom_call" | custom-call | flops 2684354560 | bytes 5242880 | tf_op jit(solution)/shard_map/attn_bwd/pallas_call | solution.py:220
  506.9 5.7 fusion.52.part_ref
  512.6 2.6 fusion.26.in_ref
  515.2 214.4 %reduce_norm_gather.1 = (f32[2048,1024]{1,0:T(8,128)}, f32[16,256]{1,0:T(8,128)S(1)}, f32[256,384]{1,0:T(8,128)S(1)}, f32[128,256]{1,0:T(8,128)S(1)}) custom-call(f32[2048,1024]{1,0:T(8,128)} %fusion.52.part_ref, f32[256,1024]{1,0:T(8,128)S(1)} %dynamic-slice_convert_fusion.2.val_ref, f32[256,1024]{1,0:T(8,128)S(1)} %subtract_add_fusion.up_ref, ...), custom_call_target="tpu_custom_call" | custom-call | bytes 540000000 | tf_op jit(solution)/shard_map/reduce_norm_gather/pallas_call | solution.py:640
  732.4 4.6 fusion.13
  737.0 7.7 %fusion.8 = f32[8,2,256,352]{2,3,1,0:T(8,128)} fusion(f32[8,3,352,256]{3,2,1,0:T(8,128)} %bitcast.31, f32[8,3,352,256]{3,2,1,0:T(8,128)} %bitcast.94), kind=kLoop, calls=%fused_computation.16 | loop fusion | flops 1441792 | bytes 17301504 | tf_op jit(solution)/shard_map/transpose | solution.py:1102
  744.8 8.4 %copy.89 = f32[2048,1024]{1,0:T(8,128)} copy(f32[2048,1024]{1,0:T(8,128)} %all-gather.8.cloned.1.call-done) | data formatting | bytes 16777216
  753.2 8.4 %copy.90 = f32[2048,1024]{1,0:T(8,128)} copy(f32[2048,1024]{1,0:T(8,128)} %get-tuple-element.137) | data formatting | bytes 16777216
  (100 shorter events, 27.0 us)
Async XLA Ops:
  7.2 149.4 %copy-start = (bf16[1024,8]{0,1:T(8,128)(2,1)S(1)}, bf16[1024,8]{0,1:T(8,128)(2,1)}, u32[]{:S(2)}) copy-start(bf16[1024,8]{0,1:T(8,128)(2,1)} %param.20) | copy-start | bytes 49156
  7.2 6.3 copy-start.3
  7.2 46.6 %all-gather.4.cloned.1.call-start = ((), (), s32[]{:S(2)}) async-start(), calls=%async_computation.1 | async-start | bytes 1179648 | tf_op jit(solution)/shard_map/all_gather | solution.py:1032
  8.8 135.7 %all-gather.6.cloned.1.call-start = ((), (), s32[]{:S(2)}) async-start(), calls=%async_computation.2 | async-start | bytes 5242880 | tf_op jit(solution)/shard_map/all_gather | solution.py:1042
  10.3 3.5 copy-start.6
  15.7 3.4 copy-start.14
  15.7 5.3 copy-start.15
  15.7 6.1 copy-start.10
  15.7 6.3 copy-start.16
  26.5 113.2 %copy-start.12 = (s32[1,16,2,128]{3,1,2,0:T(8,128)}, s32[1,16,2,128]{3,1,2,0:T(8,128)S(1)}, u32[]{:S(2)}) copy-start(s32[1,16,2,128]{3,1,2,0:T(8,128)S(1)} %copy.78) | copy-start | bytes 49156
  53.8 691.0 %all-gather.8.cloned.1.call-start = ((), (), s32[]{:S(2)}) async-start(), calls=%async_computation.3 | async-start | bytes 9437184 | tf_op jit(solution)/shard_map/all_gather | solution.py:1068
  55.2 1.2 copy-start.2
  139.7 3.4 copy-start.1
  143.1 12.6 %copy-start.11 = (s32[2,2048]{1,0:T(2,128)}, s32[2,2048]{1,0:T(2,128)S(1)}, u32[]{:S(2)}) copy-start(s32[2,2048]{1,0:T(2,128)S(1)} %reshape.133.tgt_row) | copy-start | bytes 49156
  144.5 11.2 %copy-start.13 = (f32[1024]{0:T(1024)S(1)}, f32[1024]{0:T(1024)}, u32[]{:S(2)}) copy-start(f32[1024]{0:T(1024)} %param.16) | copy-start | bytes 12292
  156.6 2.4 copy-start.4
  407.1 5.7 copy-start.5
  407.1 7.1 copy-start.8
  407.1 325.3 %collective-permute-start = (f32[1,8,3,352,256]{4,3,2,1,0:T(8,128)}, f32[1,8,3,352,256]{4,3,2,1,0:T(8,128)}, u32[]{:S(2)}, u32[]{:S(2)}) collective-permute-start(f32[1,8,3,352,256]{4,3,2,1,0:T(8,128)} %get-tuple-element.71), channel_id=1, source_target_pairs={{0,16},{8,24},{16,0},{24,8},{1,17},{9,25},{17,1},{25,9},{2,18},{10... | collective-permute-start | bytes 25952264 | tf_op jit(solution)/shard_map/ppermute | solution.py:1021
  414.2 6.2 copy-start.9
  416.1 55.4 %all-to-all-start = ((f32[8,256,128]{2,1,0:T(8,128)}), f32[8,256,128]{2,1,0:T(8,128)}, u32[]{:S(2)}, u32[]{:S(2)}) async-start(f32[8,256,128]{2,1,0:T(8,128)} %bitcast.87), calls=%async_computation | async-start | bytes 2097152 | tf_op jit(solution)/shard_map/all_to_all | solution.py:1083
  506.8 5.8 copy-start.7
Sparse Core Ops, SparseCore 0:
  10.7 43.0 all-gather.3
  55.3 33.2 all-gather.5
  407.2 170.1 all-gather.7

commit v4 on v3

--- a/solution.py
+++ b/solution.py
@@ -102,7 +102,7 @@
 
 
 def bwd_kernel(heads, length, block, rb_ref, q_ref, k_ref, v_ref, kt_ref, do_ref, segr_ref, segc_ref,
-               dq_ref, dk_ref, dv_ref, db_ref, bias, dbias, dk, dv):
+               out_ref, db_ref, bias, dbias, dk, dv):
     step_id = pl.program_id(0)
     total_rows = 2 * length - block
 
@@ -137,12 +137,12 @@
             dv[...] += dot(p.astype(BF16), dom, 1, 0)
             pieces.append(dot(kt_ref[h * HD:(h + 1) * HD, :], ds, 1, 0))
         dq = jnp.concatenate(pieces, axis=0) if heads > 1 else pieces[0]
-        dq_ref[pl.ds(q0, block), :] = (dq * 0.125).T.astype(BF16)
+        out_ref[pl.ds(q0, block), 0:lanes] = (dq * 0.125).T.astype(BF16)
         return carry
 
     lax.fori_loop(0, length // block, step, 0)
-    dk_ref[...] = dk[...].astype(BF16)
-    dv_ref[...] = dv[...].astype(BF16)
+    out_ref[:, lanes:2 * lanes] = dk[...].astype(BF16)
+    out_ref[:, 2 * lanes:] = dv[...].astype(BF16)
 
     @pl.when(step_id == pl.num_programs(0) - 1)
     def _():
@@ -216,16 +216,15 @@
     seqs, length = seg.shape
     heads = lanes // HD
     full = pl.BlockSpec((length, lanes), lambda s: (s, 0))
-    sh = jax.ShapeDtypeStruct((tok, lanes), BF16)
     return pl.pallas_call(
         functools.partial(bwd_kernel, heads, length, block),
         grid=(seqs,),
-        out_shape=(sh, sh, sh, jax.ShapeDtypeStruct((heads, NB, 128), F32)),
+        out_shape=(jax.ShapeDtypeStruct((tok, 3 * lanes), BF16), jax.ShapeDtypeStruct((heads, NB, 128), F32)),
         in_specs=[pl.BlockSpec(memory_space=pltpu.SMEM), full, full, full,
                   pl.BlockSpec((lanes, length), lambda s: (0, s)), full,
                   pl.BlockSpec((1, 1, length), lambda s: (s, 0, 0)),
                   pl.BlockSpec((length, 1), lambda s: (s, 0))],
-        out_specs=(full, full, full, pl.BlockSpec((heads, NB, 128), lambda s: (0, 0, 0))),
+        out_specs=(pl.BlockSpec((length, 3 * lanes), lambda s: (s, 0)), pl.BlockSpec((heads, NB, 128), lambda s: (0, 0, 0))),
         scratch_shapes=[pltpu.VMEM((heads, 2 * length - block, block), F32)] * 2
         + [pltpu.VMEM((length, lanes), F32)] * 2,
         compiler_params=pltpu.CompilerParams(vmem_limit_bytes=56 << 20),
@@ -526,7 +525,7 @@
         in_specs=[pl.BlockSpec(memory_space=pltpu.VMEM)],
         out_specs=pl.BlockSpec(memory_space=pl.ANY),
         scratch_shapes=ring.gather_semaphores() + [pltpu.SemaphoreType.DMA],
-        compiler_params=params(cid, 16 << 20),
+        compiler_params=params(cid, 60 << 20),
         cost_estimate=wire(90),
         name="gather_columns",
     )(x)
@@ -1083,8 +1082,7 @@
         attended_grad = lax.all_to_all(pieces, "tensor", 0, 0, tiled=False).reshape(tok, lanes)
         w_out_part = lax.dot_general(own(attended_all).astype(BF16), proj_grad, (((0,), (0,)), ((), ())), preferred_element_type=F32)
 
-        dq, dk, dv, bias_part = attention_bwd(q, k, v, k.T, attended_grad, segment_ids, rb)
-        qkv_grad = jnp.concatenate([dq, dk, dv], axis=1)
+        qkv_grad, bias_part = attention_bwd(q, k, v, k.T, attended_grad, segment_ids, rb)
         attn_in_part = lax.dot_general(qkv_grad, w_qkv.reshape(width, 3 * lanes), (((1,), (1,)), ((), ())), preferred_element_type=F32)
         w_qkv_part = lax.dot_general(attn_input, qkv_grad, (((0,), (0,)), ((), ())), preferred_element_type=F32)
 

time: 778 us -> 772 us (level)
  local copies, waits for them, and re-layouts: 45.3 us -> 34.1 us
    unnamed x45 -> x41, local copies, waits for them, and re-layouts: 28.4 us -> 18.5 us
  transfers between devices with their start and end apart: 5 -> 5, of which waited for: 2 -> 2; matrix products, arithmetic and copies ran while one was open for 8% -> 8% of each run, Pallas kernels for 45% -> 46%
where the time goes in v4:
time: 772 us; the launch traced here: 763 us
  Pallas kernels  595 us (77%)
  waiting for transfers between devices  48.5 us (6%)
  matrix products  37.8 us (5%)
  local copies, waits for them, and re-layouts  34.1 us (4%)
  other arithmetic  26.2 us (3%)
  between operations  15 us (2%)
    pallas_call x1, Pallas kernels, reduce_norm_gather(): pl.pallas_call(kernel, out_shape=[jax.ShapeDtypeStruct(s, F32) for s in (...  216 us
    pallas_call x1, Pallas kernels, experts_backward(): pl.pallas_call(functools.partial(backward_kernel, tok, chunk, ring, share...  98.6 us
    pallas_call x1, Pallas kernels, experts_weights(): pl.pallas_call(functools.partial(weights_kernel, parts, ring, n, share),...  97 us
    pallas_call x1, Pallas kernels, gather_columns(): pl.pallas_call(kernel, out_shape=jax.ShapeDtypeStruct(shape, F32), in_spe...  85.2 us
    pallas_call x1, Pallas kernels, experts_forward(): pl.pallas_call(functools.partial(forward_kernel, tok, sub, count), grid_s...  47.5 us
    all_to_all x1, waiting for transfers between devices, layer(): lax.all_to_all(pieces, 'tensor', 0, 0, tiled=False).reshape(tok, lanes)  43.2 us
    pallas_call x1, Pallas kernels, attention_bwd(): pl.pallas_call(functools.partial(bwd_kernel, heads, length, block), grid=...  30.8 us
    pallas_call x1, Pallas kernels, attention_fwd(): pl.pallas_call(functools.partial(fwd_kernel, heads, length, block), grid=...  19.6 us
  transfers between devices with their start and end apart: 5, of which 2 were waited for; matrix products, arithmetic and copies ran while one was open for 8% of the time, Pallas kernels for 46%

profile of v4, /device:TPU:0, one launch (start us, length us, event | category | flops | bytes accessed | tf_op | source)
XLA Modules:
  0.0 762.9 jit_solution(1338120094670354181)
XLA Ops:
  7.3 1.5 dynamic-slice_convert_fusion.3
  8.8 1.4 copy.54
  10.3 3.1 fusion.3
  13.4 4.1 convolution_convert_fusion
  21.4 1.4 copy.77
  23.8 1.7 select_reduce_fusion
  25.5 2.7 fusion.29
  28.3 19.6 %attn_fwd.1.x_ref = f32[2048,128]{1,0:T(8,128)} custom-call(f32[64]{0:T(128)} %reshape.139.rb_ref, bf16[2048,128]{1,0:T(8,128)(2,1)} %copy.56.q_ref, bf16[2048,128]{1,0:T(8,128)(2,1)} %copy.57.k_ref, bf16[128,2048]{1,0:T(8,128)(2,1)} %get-tuple-element.107.vt_ref, s32[2,1,1024]{2,1,0:T(1,128)} %reshape.130.segr_ref, s32[2048,1]{1,0:T(8,128)} %bitcast.101), custom_call_target="tpu_custom_call" | custom-call | flops 1073741824 | bytes 2621440 | tf_op jit(solution)/shard_map/attn_fwd/pallas_call | solution.py:198
  48.5 5.3 all-gather.4.cloned.1.call-done
  55.2 85.2 %gather_columns.1 = f32[2048,1024]{1,0:T(8,128)} custom-call(f32[2048,128]{1,0:T(8,128)} %attn_fwd.1.x_ref), custom_call_target="tpu_custom_call" | custom-call | bytes 270000000 | tf_op jit(solution)/shard_map/gather_columns/pallas_call | solution.py:522
  141.8 11.1 %multiply_reduce_fusion = (f32[2048]{0:T(1024)S(1)}, f32[2048,1024]{1,0:T(8,128)S(1)}) fusion(f32[2048,1024]{1,0:T(8,128)} %gather_columns.1, f32[1024,1024]{1,0:T(8,128)} %all-gather.6.cloned.1.call-done, f32[]{:T(128)} %bitcast.10, bf16[2048,1024]{1,0:T(8,128)(2,1)} %param.13), kind=kOutput, calls=%fused_computation.12 | convolution fusion | flops 4304402432 | bytes 25174020 | tf_op jit(solution)/shard_map/dot_general | solution.py:1043
  153.8 2.0 copy-done.2
  158.3 1.9 broadcast_in_dim.30.share
  160.2 47.5 %experts_forward.1 = (bf16[4608,1024]{1,0:T(8,128)(2,1)}, f32[4608,128]{1,0:T(8,128)}, f32[8,576,352]{2,1,0:T(8,128)}, f32[8,576,352]{2,1,0:T(8,128)}, bf16[8,57...) custom-call(s32[4096]{0:T(1024)} %bitcast.108, s32[8]{0:T(128)} %minimum_convert_fusion.held, bf16[2048,1024]{1,0:T(8,128)(2,1)} %copy-done.2, ...), custom_call_target="tpu_custom_call" | custom-call | flops 9965666304 | bytes 125829120 | tf_op jit(solution)/shard_map/experts_forward/pallas_call | solution.py:751
  207.7 98.6 %experts_backward.1 = (bf16[4608,1024]{1,0:T(8,128)(2,1)}, bf16[8,2,576,352]{3,2,1,0:T(8,128)(2,1)}, f32[2048,1024]{1,0:T(8,128)}, f32[2048,128]{1,0:T(8,128)}, f32[256,1024]{1,0:T(8,128)}) custom-call(bf16[2048,1024]{1,0:T(8,128)(2,1)} %cot.1, s32[2,2048]{1,0:T(2,128)} %copy-done.8, s32[2048,2]{1,0:T(8,128)} %bitcast.97, f32[4608,128]{1,0:T(8,128)} %get-tuple-element.43.sh, ...), custom_call_target="tpu_custom_call" | custom-call | bytes 270000000 | tf_op jit(solution)/shard_map/experts_backward/pallas_call | solution.py:856
  306.4 1.6 copy.62
  308.6 97.0 %experts_weights.1 = (f32[1,8,3,352,256]{4,3,2,1,0:T(8,128)}, f32[1,8,3,352,256]{4,3,2,1,0:T(8,128)}, f32[256,1024]{1,0:T(8,128)}, f32[8,256]{1,0:T(8,128)}) custom-call(bf16[4608,1024]{1,0:T(8,128)(2,1)} %get-tuple-element.49.x, bf16[4608,1024]{1,0:T(8,128)(2,1)} %get-tuple-element.50.y, f32[4608,128]{1,0:T(8,128)} %get-tuple-element.43.sh, ...), custom_call_target="tpu_custom_call" | custom-call | bytes 270000000 | tf_op jit(solution)/shard_map/experts_weights/pallas_call | solution.py:960
  405.6 2.0 collective-permute-start
  409.1 2.6 multiply_reduce_fusion.1
  411.7 1.8 subtract_add_fusion.up_ref
  415.3 4.3 all-to-all-start
  421.9 1.4 fusion.33
  423.3 4.0 fusion.32.ou_ref
  427.3 43.2 %all-to-all-done = f32[8,256,128]{2,1,0:T(8,128)} async-done(((f32[8,256,128]{2,1,0:T(8,128)}), f32[8,256,128]{2,1,0:T(8,128)}, u32[]{:S(2)}, u32[]{:S(2)}) %all-to-all-start) | async-done | bytes 1048608 | tf_op jit(solution)/shard_map/all_to_all | solution.py:1082
  470.5 30.8 %attn_bwd.1 = (bf16[2048,384]{1,0:T(8,128)(2,1)}, f32[2,32,128]{2,1,0:T(8,128)}) custom-call(f32[64]{0:T(128)} %reshape.139.rb_ref, bf16[2048,128]{1,0:T(8,128)(2,1)} %copy.56.q_ref, bf16[2048,128]{1,0:T(8,128)(2,1)} %copy.57.k_ref, bf16[2048,128]{1,0:T(8,128)(2,1)} %copy.66.v_ref, bf16[128,2048]{1,0:T(8,128)(2,1)} %get-tuple-element.106.kt_ref, ...), custom_call_target="tpu_custom_call" | custom-call | flops 2684354560 | bytes 5242880 | tf_op jit(solution)/shard_map/attn_bwd/pallas_call | solution.py:219
  502.4 7.3 fusion.52.part_ref
  509.7 2.6 fusion.26.in_ref
  512.3 216.0 %reduce_norm_gather.1 = (f32[2048,1024]{1,0:T(8,128)}, f32[16,256]{1,0:T(8,128)S(1)}, f32[256,384]{1,0:T(8,128)S(1)}, f32[128,256]{1,0:T(8,128)S(1)}) custom-call(f32[2048,1024]{1,0:T(8,128)} %fusion.52.part_ref, f32[256,1024]{1,0:T(8,128)S(1)} %dynamic-slice_convert_fusion.2.val_ref, f32[256,1024]{1,0:T(8,128)S(1)} %subtract_add_fusion.up_ref, ...), custom_call_target="tpu_custom_call" | custom-call | bytes 540000000 | tf_op jit(solution)/shard_map/reduce_norm_gather/pallas_call | solution.py:639
  731.1 4.6 fusion.13
  735.8 7.7 %fusion.8 = f32[8,2,256,352]{2,3,1,0:T(8,128)} fusion(f32[8,3,352,256]{3,2,1,0:T(8,128)} %bitcast.31, f32[8,3,352,256]{3,2,1,0:T(8,128)} %bitcast.94), kind=kLoop, calls=%fused_computation.16 | loop fusion | flops 1441792 | bytes 17301504 | tf_op jit(solution)/shard_map/transpose | solution.py:1100
  743.5 8.6 %copy.87 = f32[2048,1024]{1,0:T(8,128)} copy(f32[2048,1024]{1,0:T(8,128)} %all-gather.8.cloned.1.call-done) | data formatting | bytes 16777216
  752.1 3.4 copy.88
  (96 shorter events, 22.0 us)
Async XLA Ops:
  7.2 148.6 %copy-start = (bf16[1024,8]{0,1:T(8,128)(2,1)S(1)}, bf16[1024,8]{0,1:T(8,128)(2,1)}, u32[]{:S(2)}) copy-start(bf16[1024,8]{0,1:T(8,128)(2,1)} %param.20) | copy-start | bytes 49156
  7.2 6.2 copy-start.1
  7.2 46.6 %all-gather.4.cloned.1.call-start = ((), (), s32[]{:S(2)}) async-start(), calls=%async_computation.1 | async-start | bytes 1179648 | tf_op jit(solution)/shard_map/all_gather | solution.py:1031
  8.8 133.0 %all-gather.6.cloned.1.call-start = ((), (), s32[]{:S(2)}) async-start(), calls=%async_computation.2 | async-start | bytes 5242880 | tf_op jit(solution)/shard_map/all_gather | solution.py:1041
  17.5 3.3 copy-start.11
  17.5 5.3 copy-start.12
  17.5 6.1 copy-start.7
  17.5 6.3 copy-start.13
  28.3 112.2 %copy-start.9 = (s32[1,16,2,128]{3,1,2,0:T(8,128)}, s32[1,16,2,128]{3,1,2,0:T(8,128)S(1)}, u32[]{:S(2)}) copy-start(s32[1,16,2,128]{3,1,2,0:T(8,128)S(1)} %copy.78) | copy-start | bytes 49156
  53.8 689.7 %all-gather.8.cloned.1.call-start = ((), (), s32[]{:S(2)}) async-start(), calls=%async_computation.3 | async-start | bytes 9437184 | tf_op jit(solution)/shard_map/all_gather | solution.py:1067
  140.4 12.4 %copy-start.8 = (s32[2,2048]{1,0:T(2,128)}, s32[2,2048]{1,0:T(2,128)S(1)}, u32[]{:S(2)}) copy-start(s32[2,2048]{1,0:T(2,128)S(1)} %reshape.133.tgt_row) | copy-start | bytes 49156
  141.8 11.1 %copy-start.10 = (f32[1024]{0:T(1024)S(1)}, f32[1024]{0:T(1024)}, u32[]{:S(2)}) copy-start(f32[1024]{0:T(1024)} %param.16) | copy-start | bytes 12292
  153.8 2.0 copy-start.2
  405.5 7.9 %copy-start.4 = (f32[1024,1024]{1,0:T(8,128)S(1)}, f32[1024,1024]{1,0:T(8,128)}, u32[]{:S(2)}) copy-start(f32[1024,1024]{1,0:T(8,128)} %all-gather.6.cloned.1.call-done) | copy-start | bytes 12582916
  405.6 325.6 %collective-permute-start = (f32[1,8,3,352,256]{4,3,2,1,0:T(8,128)}, f32[1,8,3,352,256]{4,3,2,1,0:T(8,128)}, u32[]{:S(2)}, u32[]{:S(2)}) collective-permute-start(f32[1,8,3,352,256]{4,3,2,1,0:T(8,128)} %get-tuple-element.67), channel_id=1, source_target_pairs={{0,16},{8,24},{16,0},{24,8},{1,17},{9,25},{17,1},{25,9},{2,18},{10... | collective-permute-start | bytes 25952264 | tf_op jit(solution)/shard_map/ppermute | solution.py:1020
  413.5 6.2 copy-start.6
  415.3 55.2 %all-to-all-start = ((f32[8,256,128]{2,1,0:T(8,128)}), f32[8,256,128]{2,1,0:T(8,128)}, u32[]{:S(2)}, u32[]{:S(2)}) async-start(f32[8,256,128]{2,1,0:T(8,128)} %bitcast.87), calls=%async_computation | async-start | bytes 2097152 | tf_op jit(solution)/shard_map/all_to_all | solution.py:1082
  502.4 7.4 copy-start.3
  502.4 7.4 copy-start.5
  743.5 8.6 %slice-start = ((s8[8388608]{0:T(1024)(128)(4,1)}), s8[4194304]{0:T(1024)(128)(4,1)S(1)}, s32[]{:S(2)}) async-start(s8[8388608]{0:T(1024)(128)(4,1)} %bitcast.95), calls=%async_computation.4 | async-start | bytes 8388608
  743.5 8.6 %slice-start.1 = ((s8[8388608]{0:T(1024)(128)(4,1)}), s8[4194304]{0:T(1024)(128)(4,1)S(1)}, s32[]{:S(2)}) async-start(s8[8388608]{0:T(1024)(128)(4,1)} %bitcast.95), calls=%async_computation.5 | async-start | bytes 8388608
Sparse Core Ops, SparseCore 0:
  10.7 43.0 all-gather.3
  55.3 33.1 all-gather.5
  405.7 171.0 all-gather.7

commit v5 on v4

--- a/solution.py
+++ b/solution.py
@@ -843,7 +843,7 @@
         reduce.finish()
 
 
-def experts_backward(tgt, cot, sh, gate, up, act, win, wdn, part, hid, n, cid, chunk=256, share=(1.4, 0.65)):
+def experts_backward(tgt, cot, sh, gate, up, act, win, wdn, part, hid, n, cid, chunk=256, share=(1.2, 0.8)):
     tok, width = part.shape
     ff = wdn.shape[1]
     ring = Ring(n, tok // n)
@@ -947,7 +947,7 @@
         reduce.finish()
 
 
-def experts_weights(x, y, sh, act, dgu, part, small, n, parts, cid, share=(1.3, 0)):
+def experts_weights(x, y, sh, act, dgu, part, small, n, parts, cid, share=(1.7, 0)):
     tok, width = part.shape
     ff = act.shape[2]
     wide = width // parts
@@ -1034,7 +1034,7 @@
         qkv = jnp.dot(attn_input, w_qkv.reshape(width, 3 * lanes), preferred_element_type=F32).astype(BF16)
         q, k, v = (qkv[:, i * lanes:(i + 1) * lanes] for i in range(3))
         rb = rel_bias.astype(F32).reshape(-1)
-        attended = attention_fwd(q, k, v.T, segment_ids, rb)
+        attended = attention_fwd(q, k, v.T, segment_ids, rb, block=512)
         tgt, held = slot_targets(routes, order[0])
 
         attended, w_out_rows, tgt, held = lax.optimization_barrier((attended, w_out_rows, tgt, held))

time: 772 us -> 768 us (level)
  no operation moved by 1% of the time
where the time goes in v5:
time: 768 us; the launch traced here: 759 us
  Pallas kernels  589 us (77%)
  waiting for transfers between devices  51.1 us (7%)
  matrix products  37.7 us (5%)
  local copies, waits for them, and re-layouts  34.1 us (4%)
  other arithmetic  26.3 us (3%)
  between operations  15 us (2%)
    pallas_call x1, Pallas kernels, reduce_norm_gather(): pl.pallas_call(kernel, out_shape=[jax.ShapeDtypeStruct(s, F32) for s in (...  216 us
    pallas_call x1, Pallas kernels, experts_backward(): pl.pallas_call(functools.partial(backward_kernel, tok, chunk, ring, share...  97.3 us
    pallas_call x1, Pallas kernels, experts_weights(): pl.pallas_call(functools.partial(weights_kernel, parts, ring, n, share),...  95 us
    pallas_call x1, Pallas kernels, gather_columns(): pl.pallas_call(kernel, out_shape=jax.ShapeDtypeStruct(shape, F32), in_spe...  84.6 us
    pallas_call x1, Pallas kernels, experts_forward(): pl.pallas_call(functools.partial(forward_kernel, tok, sub, count), grid_s...  47.5 us
    all_to_all x1, waiting for transfers between devices, layer(): lax.all_to_all(pieces, 'tensor', 0, 0, tiled=False).reshape(tok, lanes)  43.5 us
    pallas_call x1, Pallas kernels, attention_bwd(): pl.pallas_call(functools.partial(bwd_kernel, heads, length, block), grid=...  30.8 us
    unnamed x41, local copies, waits for them, and re-layouts  18.5 us
  transfers between devices with their start and end apart: 5, of which 2 were waited for; matrix products, arithmetic and copies ran while one was open for 8% of the time, Pallas kernels for 46%

profile of v5, /device:TPU:0, one launch (start us, length us, event | category | flops | bytes accessed | tf_op | source)
XLA Modules:
  0.0 759.0 jit_solution(13755345820421387617)
XLA Ops:
  7.3 1.5 dynamic-slice_convert_fusion.3
  8.8 1.4 copy.54
  10.3 3.1 fusion.3
  13.4 4.1 convolution_convert_fusion
  21.4 1.4 copy.77
  23.8 1.7 select_reduce_fusion
  25.5 2.7 fusion.29
  28.3 17.2 %attn_fwd.1.x_ref = f32[2048,128]{1,0:T(8,128)} custom-call(f32[64]{0:T(128)} %reshape.139.rb_ref, bf16[2048,128]{1,0:T(8,128)(2,1)} %copy.56.q_ref, bf16[2048,128]{1,0:T(8,128)(2,1)} %copy.57.k_ref, bf16[128,2048]{1,0:T(8,128)(2,1)} %get-tuple-element.107.vt_ref, s32[2,1,1024]{2,1,0:T(1,128)} %reshape.130.segr_ref, s32[2048,1]{1,0:T(8,128)} %bitcast.101), custom_call_target="tpu_custom_call" | custom-call | flops 1073741824 | bytes 2621440 | tf_op jit(solution)/shard_map/attn_fwd/pallas_call | solution.py:198
  46.2 7.6 %all-gather.4.cloned.1.call-done = f32[1024,256]{1,0:T(8,128)} async-done(((f32[128,256]{1,0:T(8,128)}), f32[1024,256]{1,0:T(8,128)}) %all-gather.4.cloned.1.call-update) | async-done | bytes 1048592 | tf_op jit(solution)/shard_map/all_gather | solution.py:1031
  55.2 84.6 %gather_columns.1 = f32[2048,1024]{1,0:T(8,128)} custom-call(f32[2048,128]{1,0:T(8,128)} %attn_fwd.1.x_ref), custom_call_target="tpu_custom_call" | custom-call | bytes 270000000 | tf_op jit(solution)/shard_map/gather_columns/pallas_call | solution.py:522
  141.2 11.1 %multiply_reduce_fusion = (f32[2048]{0:T(1024)S(1)}, f32[2048,1024]{1,0:T(8,128)S(1)}) fusion(f32[2048,1024]{1,0:T(8,128)} %gather_columns.1, f32[1024,1024]{1,0:T(8,128)} %all-gather.6.cloned.1.call-done, f32[]{:T(128)} %bitcast.10, bf16[2048,1024]{1,0:T(8,128)(2,1)} %param.13), kind=kOutput, calls=%fused_computation.12 | convolution fusion | flops 4304402432 | bytes 25174020 | tf_op jit(solution)/shard_map/dot_general | solution.py:1043
  153.2 2.0 copy-done.2
  157.7 1.9 broadcast_in_dim.30.share
  159.6 47.5 %experts_forward.1 = (bf16[4608,1024]{1,0:T(8,128)(2,1)}, f32[4608,128]{1,0:T(8,128)}, f32[8,576,352]{2,1,0:T(8,128)}, f32[8,576,352]{2,1,0:T(8,128)}, bf16[8,57...) custom-call(s32[4096]{0:T(1024)} %bitcast.108, s32[8]{0:T(128)} %minimum_convert_fusion.held, bf16[2048,1024]{1,0:T(8,128)(2,1)} %copy-done.2, ...), custom_call_target="tpu_custom_call" | custom-call | flops 9965666304 | bytes 125829120 | tf_op jit(solution)/shard_map/experts_forward/pallas_call | solution.py:751
  207.2 97.3 %experts_backward.1 = (bf16[4608,1024]{1,0:T(8,128)(2,1)}, bf16[8,2,576,352]{3,2,1,0:T(8,128)(2,1)}, f32[2048,1024]{1,0:T(8,128)}, f32[2048,128]{1,0:T(8,128)}, f32[256,1024]{1,0:T(8,128)}) custom-call(bf16[2048,1024]{1,0:T(8,128)(2,1)} %cot.1, s32[2,2048]{1,0:T(2,128)} %copy-done.8, s32[2048,2]{1,0:T(8,128)} %bitcast.97, f32[4608,128]{1,0:T(8,128)} %get-tuple-element.43.sh, ...), custom_call_target="tpu_custom_call" | custom-call | bytes 270000000 | tf_op jit(solution)/shard_map/experts_backward/pallas_call | solution.py:856
  304.4 1.6 copy.62
  306.6 95.0 %experts_weights.1 = (f32[1,8,3,352,256]{4,3,2,1,0:T(8,128)}, f32[1,8,3,352,256]{4,3,2,1,0:T(8,128)}, f32[256,1024]{1,0:T(8,128)}, f32[8,256]{1,0:T(8,128)}) custom-call(bf16[4608,1024]{1,0:T(8,128)(2,1)} %get-tuple-element.49.x, bf16[4608,1024]{1,0:T(8,128)(2,1)} %get-tuple-element.50.y, f32[4608,128]{1,0:T(8,128)} %get-tuple-element.43.sh, ...), custom_call_target="tpu_custom_call" | custom-call | bytes 270000000 | tf_op jit(solution)/shard_map/experts_weights/pallas_call | solution.py:960
  401.7 1.6 collective-permute-start
  404.8 2.5 multiply_reduce_fusion.1
  407.3 1.8 subtract_add_fusion.up_ref
  411.1 4.3 all-to-all-start
  417.6 1.4 fusion.33
  419.0 4.0 fusion.32.ou_ref
  423.1 43.5 %all-to-all-done = f32[8,256,128]{2,1,0:T(8,128)} async-done(((f32[8,256,128]{2,1,0:T(8,128)}), f32[8,256,128]{2,1,0:T(8,128)}, u32[]{:S(2)}, u32[]{:S(2)}) %all-to-all-start) | async-done | bytes 1048608 | tf_op jit(solution)/shard_map/all_to_all | solution.py:1082
  466.5 30.8 %attn_bwd.1 = (bf16[2048,384]{1,0:T(8,128)(2,1)}, f32[2,32,128]{2,1,0:T(8,128)}) custom-call(f32[64]{0:T(128)} %reshape.139.rb_ref, bf16[2048,128]{1,0:T(8,128)(2,1)} %copy.56.q_ref, bf16[2048,128]{1,0:T(8,128)(2,1)} %copy.57.k_ref, bf16[2048,128]{1,0:T(8,128)(2,1)} %copy.66.v_ref, bf16[128,2048]{1,0:T(8,128)(2,1)} %get-tuple-element.106.kt_ref, ...), custom_call_target="tpu_custom_call" | custom-call | flops 2684354560 | bytes 5242880 | tf_op jit(solution)/shard_map/attn_bwd/pallas_call | solution.py:219
  498.4 7.3 fusion.52.part_ref
  505.7 2.6 fusion.26.in_ref
  508.3 216.1 %reduce_norm_gather.1 = (f32[2048,1024]{1,0:T(8,128)}, f32[16,256]{1,0:T(8,128)S(1)}, f32[256,384]{1,0:T(8,128)S(1)}, f32[128,256]{1,0:T(8,128)S(1)}) custom-call(f32[2048,1024]{1,0:T(8,128)} %fusion.52.part_ref, f32[256,1024]{1,0:T(8,128)S(1)} %dynamic-slice_convert_fusion.2.val_ref, f32[256,1024]{1,0:T(8,128)S(1)} %subtract_add_fusion.up_ref, ...), custom_call_target="tpu_custom_call" | custom-call | bytes 540000000 | tf_op jit(solution)/shard_map/reduce_norm_gather/pallas_call | solution.py:639
  727.2 4.6 fusion.13
  731.9 7.7 %fusion.8 = f32[8,2,256,352]{2,3,1,0:T(8,128)} fusion(f32[8,3,352,256]{3,2,1,0:T(8,128)} %bitcast.31, f32[8,3,352,256]{3,2,1,0:T(8,128)} %bitcast.94), kind=kLoop, calls=%fused_computation.16 | loop fusion | flops 1441792 | bytes 17301504 | tf_op jit(solution)/shard_map/transpose | solution.py:1100
  739.6 8.6 %copy.87 = f32[2048,1024]{1,0:T(8,128)} copy(f32[2048,1024]{1,0:T(8,128)} %all-gather.8.cloned.1.call-done) | data formatting | bytes 16777216
  748.2 3.4 copy.88
  (96 shorter events, 22.0 us)
Async XLA Ops:
  7.2 148.1 %copy-start = (bf16[1024,8]{0,1:T(8,128)(2,1)S(1)}, bf16[1024,8]{0,1:T(8,128)(2,1)}, u32[]{:S(2)}) copy-start(bf16[1024,8]{0,1:T(8,128)(2,1)} %param.20) | copy-start | bytes 49156
  7.2 6.2 copy-start.1
  7.2 46.6 %all-gather.4.cloned.1.call-start = ((), (), s32[]{:S(2)}) async-start(), calls=%async_computation.1 | async-start | bytes 1179648 | tf_op jit(solution)/shard_map/all_gather | solution.py:1031
  8.8 132.5 %all-gather.6.cloned.1.call-start = ((), (), s32[]{:S(2)}) async-start(), calls=%async_computation.2 | async-start | bytes 5242880 | tf_op jit(solution)/shard_map/all_gather | solution.py:1041
  17.5 3.3 copy-start.11
  17.5 5.3 copy-start.12
  17.5 6.1 copy-start.7
  17.5 6.3 copy-start.13
  28.3 111.6 %copy-start.9 = (s32[1,16,2,128]{3,1,2,0:T(8,128)}, s32[1,16,2,128]{3,1,2,0:T(8,128)S(1)}, u32[]{:S(2)}) copy-start(s32[1,16,2,128]{3,1,2,0:T(8,128)S(1)} %copy.78) | copy-start | bytes 49156
  53.8 685.8 %all-gather.8.cloned.1.call-start = ((), (), s32[]{:S(2)}) async-start(), calls=%async_computation.3 | async-start | bytes 9437184 | tf_op jit(solution)/shard_map/all_gather | solution.py:1067
  139.9 12.4 %copy-start.8 = (s32[2,2048]{1,0:T(2,128)}, s32[2,2048]{1,0:T(2,128)S(1)}, u32[]{:S(2)}) copy-start(s32[2,2048]{1,0:T(2,128)S(1)} %reshape.133.tgt_row) | copy-start | bytes 49156
  141.2 11.1 %copy-start.10 = (f32[1024]{0:T(1024)S(1)}, f32[1024]{0:T(1024)}, u32[]{:S(2)}) copy-start(f32[1024]{0:T(1024)} %param.16) | copy-start | bytes 12292
  153.2 2.0 copy-start.2
  401.6 7.5 copy-start.4
  401.7 325.6 %collective-permute-start = (f32[1,8,3,352,256]{4,3,2,1,0:T(8,128)}, f32[1,8,3,352,256]{4,3,2,1,0:T(8,128)}, u32[]{:S(2)}, u32[]{:S(2)}) collective-permute-start(f32[1,8,3,352,256]{4,3,2,1,0:T(8,128)} %get-tuple-element.67), channel_id=1, source_target_pairs={{0,16},{8,24},{16,0},{24,8},{1,17},{9,25},{17,1},{25,9},{2,18},{10... | collective-permute-start | bytes 25952264 | tf_op jit(solution)/shard_map/ppermute | solution.py:1020
  409.2 6.2 copy-start.6
  411.1 55.5 %all-to-all-start = ((f32[8,256,128]{2,1,0:T(8,128)}), f32[8,256,128]{2,1,0:T(8,128)}, u32[]{:S(2)}, u32[]{:S(2)}) async-start(f32[8,256,128]{2,1,0:T(8,128)} %bitcast.87), calls=%async_computation | async-start | bytes 2097152 | tf_op jit(solution)/shard_map/all_to_all | solution.py:1082
  498.4 7.4 copy-start.3
  498.4 7.4 copy-start.5
  739.6 8.6 %slice-start = ((s8[8388608]{0:T(1024)(128)(4,1)}), s8[4194304]{0:T(1024)(128)(4,1)S(1)}, s32[]{:S(2)}) async-start(s8[8388608]{0:T(1024)(128)(4,1)} %bitcast.95), calls=%async_computation.4 | async-start | bytes 8388608
  739.6 8.6 %slice-start.1 = ((s8[8388608]{0:T(1024)(128)(4,1)}), s8[4194304]{0:T(1024)(128)(4,1)S(1)}, s32[]{:S(2)}) async-start(s8[8388608]{0:T(1024)(128)(4,1)} %bitcast.95), calls=%async_computation.5 | async-start | bytes 8388608
Sparse Core Ops, SparseCore 0:
  10.7 43.0 all-gather.3
  55.4 33.1 all-gather.5
  401.8 172.9 all-gather.7
